TPU v7x, 16 devices: a whole 2x2x2 slice. The times are simulated.
16 devices in a mesh: pc: 4 (over z, y), pr: 4 (over x, core).
Axes of the slice: x: 2, y: 2, z: 2, core: 2. Of those that a mesh axis runs over, the one named last changes fastest.
Arguments:
- panel_in: float32 [12288, 16, 256], P('pr', 'pc')
- trail_in: float32 [12288, 8192], P('pr', 'pc')
Outputs:
- output 1: float32 [12288, 16, 256], P('pr', 'pc')
- output 2: float32 [12288, 8192], P('pr', 'pc')
All inputs are finite; a program needn't handle non-finite values.
Results may differ from a plain program's by a relative error of at most 0.001.
Values sent between devices are 32-bit elements.
A program may use at most 1 GiB of HBM per device.

v0:
```python
import jax
import jax.numpy as jnp
from jax import lax
from jax.sharding import PartitionSpec as P

PREC_HIGH = lax.Precision.HIGHEST


def solve_right(l_diag, right_side):
    return lax.linalg.triangular_solve(l_diag, right_side, left_side=False, lower=True, transpose_a=True)


def apply_update(panel_tile, trail_tile, row_panel, col_view, panel_step, row_procs, col_procs):
    local_rows, panel_dev, blk_size = panel_tile.shape
    row_start = ((panel_step + 1) // row_procs) * blk_size
    col_start = (panel_step + 1) // col_procs
    rows_part = row_panel[row_start:]
    if col_start < panel_dev:
        panel_update = jnp.einsum("rc,mbc->rmb", rows_part, col_view[col_start:panel_dev], precision=PREC_HIGH, preferred_element_type=jnp.float32)
        panel_tile = lax.dynamic_update_slice(panel_tile, panel_tile[row_start:, col_start:] - panel_update, (row_start, col_start, 0))
    trail_view = col_view[panel_dev:].reshape(trail_tile.shape[1], blk_size)
    trail_update = lax.dot_general(rows_part, trail_view, (((1,), (1,)), ((), ())), precision=PREC_HIGH, preferred_element_type=jnp.float32)
    trail_tile = lax.dynamic_update_slice(trail_tile, trail_tile[row_start:] - trail_update, (row_start, 0))
    return panel_tile, trail_tile


def solution(mesh):
    row_procs = mesh.shape["pr"]
    col_procs = mesh.shape["pc"]

    def local_part(panel_tile, trail_tile):
        local_rows, panel_dev, blk_size = panel_tile.shape
        row_blocks = local_rows // blk_size
        col_blocks = row_blocks * row_procs // col_procs
        my_row = lax.axis_index("pr")
        my_col = lax.axis_index("pc")
        block_ids = (jnp.arange(row_blocks) * row_procs + my_row)[:, None, None]
        eye_block = jnp.eye(blk_size, dtype=panel_tile.dtype)
        for panel_step in range(panel_dev * col_procs):
            owner_col = panel_step % col_procs
            local_slot = panel_step // col_procs
            owner_row = panel_step % row_procs
            diag_start = (panel_step // row_procs) * blk_size
            column = panel_tile[:, local_slot, :]
            diag_local = column[diag_start:diag_start + blk_size]
            diag_blk = lax.psum(jnp.where(my_row == owner_row, diag_local, 0.0), "pr")
            diag_blk = jnp.where(my_col == owner_col, diag_blk, eye_block)
            l_diag = jnp.linalg.cholesky(diag_blk)
            solved = solve_right(l_diag, column).reshape(row_blocks, blk_size, blk_size)
            below_diag = jnp.where(block_ids > panel_step, solved, 0.0)
            l_col = jnp.where(block_ids == panel_step, l_diag, below_diag).reshape(local_rows, blk_size)
            new_col = jnp.where(my_col == owner_col, l_col, column)
            panel_tile = lax.dynamic_update_slice(panel_tile, new_col[:, None, :], (0, local_slot, 0))
            row_panel = lax.psum(jnp.where(my_col == owner_col, below_diag.reshape(local_rows, blk_size), 0.0), "pc")
            gathered = lax.all_gather(row_panel, "pr", axis=0, tiled=False)
            by_block = gathered.reshape(row_procs, row_blocks, blk_size, blk_size).transpose(1, 0, 2, 3)
            col_view = lax.dynamic_index_in_dim(by_block.reshape(col_blocks, col_procs, blk_size, blk_size), my_col, axis=1, keepdims=False)
            panel_tile, trail_tile = apply_update(panel_tile, trail_tile, row_panel, col_view, panel_step, row_procs, col_procs)
        return panel_tile, trail_tile

    spec_panel = P("pr", "pc", None)
    spec_trail = P("pr", "pc")
    return jax.shard_map(local_part, mesh=mesh, in_specs=(spec_panel, spec_trail), out_specs=(spec_panel, spec_trail), check_vma=False)
```

profile of v0, /device:TPU:0, one launch (start us, length us, event | category | flops | bytes accessed | tf_op | source)
XLA Modules:
  0.0 5161.5 jit_solution(6950724847984829634)
XLA Ops:
  25.7 29.1 all-reduce.34.cloned.1.call-done
  131.1 78.0 %all-reduce.36.cloned.1.call-done = f32[3072,256]{0,1:T(8,128)} async-done(((f32[3072,256]{0,1:T(8,128)}), f32[3072,256]{0,1:T(8,128)}) %all-reduce.36.cloned.1.call-update) | async-done | bytes 3145744 | tf_op jit(solution)/shard_map/psum | solution.py:54
  220.2 71.4 %all-gather.33.cloned.1.call-done = f32[12288,256]{0,1:T(8,128)} async-done(((f32[3072,256]{0,1:T(8,128)}), f32[12288,256]{0,1:T(8,128)}) %all-gather.33.cloned.1.call-update) | async-done | bytes 12582928 | tf_op jit(solution)/shard_map/all_gather | solution.py:55
  428.2 79.2 %all-reduce.40.cloned.1.call-done = f32[3072,256]{0,1:T(8,128)} async-done(((f32[3072,256]{0,1:T(8,128)}), f32[3072,256]{0,1:T(8,128)}) %all-reduce.40.cloned.1.call-update) | async-done | bytes 3145744 | tf_op jit(solution)/shard_map/psum | solution.py:54
  518.8 71.0 %all-gather.35.cloned.1.call-done = f32[12288,256]{0,1:T(8,128)} async-done(((f32[3072,256]{0,1:T(8,128)}), f32[12288,256]{0,1:T(8,128)}) %all-gather.35.cloned.1.call-update) | async-done | bytes 12582928 | tf_op jit(solution)/shard_map/all_gather | solution.py:55
  727.2 79.2 %all-reduce.44.cloned.1.call-done = f32[3072,256]{0,1:T(8,128)} async-done(((f32[3072,256]{0,1:T(8,128)}), f32[3072,256]{0,1:T(8,128)}) %all-reduce.44.cloned.1.call-update) | async-done | bytes 3145744 | tf_op jit(solution)/shard_map/psum | solution.py:54
  818.0 70.9 %all-gather.37.cloned.1.call-done = f32[12288,256]{0,1:T(8,128)} async-done(((f32[3072,256]{0,1:T(8,128)}), f32[12288,256]{0,1:T(8,128)}) %all-gather.37.cloned.1.call-update) | async-done | bytes 12582928 | tf_op jit(solution)/shard_map/all_gather | solution.py:55
  1023.0 80.1 %all-reduce.48.cloned.1.call-done = f32[3072,256]{0,1:T(8,128)} async-done(((f32[3072,256]{0,1:T(8,128)}), f32[3072,256]{0,1:T(8,128)}) %all-reduce.48.cloned.1.call-update) | async-done | bytes 3145744 | tf_op jit(solution)/shard_map/psum | solution.py:54
  1114.3 71.1 %all-gather.39.cloned.1.call-done = f32[12288,256]{0,1:T(8,128)} async-done(((f32[3072,256]{0,1:T(8,128)}), f32[12288,256]{0,1:T(8,128)}) %all-gather.39.cloned.1.call-update) | async-done | bytes 12582928 | tf_op jit(solution)/shard_map/all_gather | solution.py:55
  1316.5 78.0 %all-reduce.52.cloned.1.call-done = f32[3072,256]{0,1:T(8,128)} async-done(((f32[3072,256]{0,1:T(8,128)}), f32[3072,256]{0,1:T(8,128)}) %all-reduce.52.cloned.1.call-update) | async-done | bytes 3145744 | tf_op jit(solution)/shard_map/psum | solution.py:54
  1406.1 70.7 %all-gather.41.cloned.1.call-done = f32[12288,256]{0,1:T(8,128)} async-done(((f32[3072,256]{0,1:T(8,128)}), f32[12288,256]{0,1:T(8,128)}) %all-gather.41.cloned.1.call-update) | async-done | bytes 12582928 | tf_op jit(solution)/shard_map/all_gather | solution.py:55
  1607.4 79.2 %all-reduce.56.cloned.1.call-done = f32[3072,256]{0,1:T(8,128)} async-done(((f32[3072,256]{0,1:T(8,128)}), f32[3072,256]{0,1:T(8,128)}) %all-reduce.56.cloned.1.call-update) | async-done | bytes 3145744 | tf_op jit(solution)/shard_map/psum | solution.py:54
  1698.2 70.7 %all-gather.43.cloned.1.call-done = f32[12288,256]{0,1:T(8,128)} async-done(((f32[3072,256]{0,1:T(8,128)}), f32[12288,256]{0,1:T(8,128)}) %all-gather.43.cloned.1.call-update) | async-done | bytes 12582928 | tf_op jit(solution)/shard_map/all_gather | solution.py:55
  1899.2 79.2 %all-reduce.60.cloned.1.call-done = f32[3072,256]{0,1:T(8,128)} async-done(((f32[3072,256]{0,1:T(8,128)}), f32[3072,256]{0,1:T(8,128)}) %all-reduce.60.cloned.1.call-update) | async-done | bytes 3145744 | tf_op jit(solution)/shard_map/psum | solution.py:54
  1989.4 71.4 %all-gather.45.cloned.1.call-done = f32[12288,256]{0,1:T(8,128)} async-done(((f32[3072,256]{0,1:T(8,128)}), f32[12288,256]{0,1:T(8,128)}) %all-gather.45.cloned.1.call-update) | async-done | bytes 12582928 | tf_op jit(solution)/shard_map/all_gather | solution.py:55
  2192.8 80.1 %all-reduce.64.cloned.1.call-done = f32[3072,256]{0,1:T(8,128)} async-done(((f32[3072,256]{0,1:T(8,128)}), f32[3072,256]{0,1:T(8,128)}) %all-reduce.64.cloned.1.call-update) | async-done | bytes 3145744 | tf_op jit(solution)/shard_map/psum | solution.py:54
  2283.9 71.3 %all-gather.47.cloned.1.call-done = f32[12288,256]{0,1:T(8,128)} async-done(((f32[3072,256]{0,1:T(8,128)}), f32[12288,256]{0,1:T(8,128)}) %all-gather.47.cloned.1.call-update) | async-done | bytes 12582928 | tf_op jit(solution)/shard_map/all_gather | solution.py:55
  2482.3 78.0 %all-reduce.68.cloned.1.call-done = f32[3072,256]{0,1:T(8,128)} async-done(((f32[3072,256]{0,1:T(8,128)}), f32[3072,256]{0,1:T(8,128)}) %all-reduce.68.cloned.1.call-update) | async-done | bytes 3145744 | tf_op jit(solution)/shard_map/psum | solution.py:54
  2571.3 71.2 %all-gather.49.cloned.1.call-done = f32[12288,256]{0,1:T(8,128)} async-done(((f32[3072,256]{0,1:T(8,128)}), f32[12288,256]{0,1:T(8,128)}) %all-gather.49.cloned.1.call-update) | async-done | bytes 12582928 | tf_op jit(solution)/shard_map/all_gather | solution.py:55
  2770.1 79.2 %all-reduce.72.cloned.1.call-done = f32[3072,256]{0,1:T(8,128)} async-done(((f32[3072,256]{0,1:T(8,128)}), f32[3072,256]{0,1:T(8,128)}) %all-reduce.72.cloned.1.call-update) | async-done | bytes 3145744 | tf_op jit(solution)/shard_map/psum | solution.py:54
  2860.3 71.2 %all-gather.51.cloned.1.call-done = f32[12288,256]{0,1:T(8,128)} async-done(((f32[3072,256]{0,1:T(8,128)}), f32[12288,256]{0,1:T(8,128)}) %all-gather.51.cloned.1.call-update) | async-done | bytes 12582928 | tf_op jit(solution)/shard_map/all_gather | solution.py:55
  3057.9 79.2 %all-reduce.76.cloned.1.call-done = f32[3072,256]{0,1:T(8,128)} async-done(((f32[3072,256]{0,1:T(8,128)}), f32[3072,256]{0,1:T(8,128)}) %all-reduce.76.cloned.1.call-update) | async-done | bytes 3145744 | tf_op jit(solution)/shard_map/psum | solution.py:54
  3148.1 71.2 %all-gather.53.cloned.1.call-done = f32[12288,256]{0,1:T(8,128)} async-done(((f32[3072,256]{0,1:T(8,128)}), f32[12288,256]{0,1:T(8,128)}) %all-gather.53.cloned.1.call-update) | async-done | bytes 12582928 | tf_op jit(solution)/shard_map/all_gather | solution.py:55
  3243.1 26.3 all-reduce.78.cloned.1.call-done
  3346.8 80.1 %all-reduce.80.cloned.1.call-done = f32[3072,256]{0,1:T(8,128)} async-done(((f32[3072,256]{0,1:T(8,128)}), f32[3072,256]{0,1:T(8,128)}) %all-reduce.80.cloned.1.call-update) | async-done | bytes 3145744 | tf_op jit(solution)/shard_map/psum | solution.py:54
  3438.0 71.1 %all-gather.55.cloned.1.call-done = f32[12288,256]{0,1:T(8,128)} async-done(((f32[3072,256]{0,1:T(8,128)}), f32[12288,256]{0,1:T(8,128)}) %all-gather.55.cloned.1.call-update) | async-done | bytes 12582928 | tf_op jit(solution)/shard_map/all_gather | solution.py:55
  3641.2 78.0 %all-reduce.84.cloned.1.call-done = f32[3072,256]{0,1:T(8,128)} async-done(((f32[3072,256]{0,1:T(8,128)}), f32[3072,256]{0,1:T(8,128)}) %all-reduce.84.cloned.1.call-update) | async-done | bytes 3145744 | tf_op jit(solution)/shard_map/psum | solution.py:54
  3721.4 80.2 %all-gather.57.cloned.1.call-done = f32[12288,256]{0,1:T(8,128)} async-done(((f32[3072,256]{0,1:T(8,128)}), f32[12288,256]{0,1:T(8,128)}) %all-gather.57.cloned.1.call-update) | async-done | bytes 12582928 | tf_op jit(solution)/shard_map/all_gather | solution.py:55
  3933.2 79.2 %all-reduce.88.cloned.1.call-done = f32[3072,256]{0,1:T(8,128)} async-done(((f32[3072,256]{0,1:T(8,128)}), f32[3072,256]{0,1:T(8,128)}) %all-reduce.88.cloned.1.call-update) | async-done | bytes 3145744 | tf_op jit(solution)/shard_map/psum | solution.py:54
  4018.9 75.9 %all-gather.59.cloned.1.call-done = f32[12288,256]{0,1:T(8,128)} async-done(((f32[3072,256]{0,1:T(8,128)}), f32[12288,256]{0,1:T(8,128)}) %all-gather.59.cloned.1.call-update) | async-done | bytes 12582928 | tf_op jit(solution)/shard_map/all_gather | solution.py:55
  4228.1 44.0 fusion.242
  4274.6 44.9 fusion.243
  4322.8 55.3 %subtract_subtract_fusion = f32[3072,2048]{1,0:T(8,128)} fusion(f32[3072,2048]{1,0:T(8,128)} %fusion.243, f32[3072,2048]{1,0:T(8,128)} %param.6, f32[3072,2048]{1,0:T(8,128)} %fusion.242, f32[3072,256]{0,1:T(8,128)S(1)} %copy-done.3, f32[2048,256]{1,0:T(8,128)} %bitcast.877), kind=kOutput, calls=%fused_computation.32 | convolution fusion | flops 19346227200 | bytes 105906176 | tf_op jit(solution)/shard_map/dot_general | solution.py:22
  4380.6 47.2 constant_dynamic-update-slice_fusion.27
  4430.3 47.0 constant_dynamic-update-slice_fusion.26
  4479.8 47.0 constant_dynamic-update-slice_fusion.25
  4529.4 47.2 constant_dynamic-update-slice_fusion.24
  4603.0 26.4 all-reduce.94.cloned.1.call-done
  4706.6 42.9 constant_dynamic-update-slice_fusion.23
  4752.7 32.1 all-reduce.96.cloned.1.call-done
  4784.9 43.1 constant_dynamic-update-slice_fusion.22
  4830.5 41.7 constant_dynamic-update-slice_fusion.21
  4874.7 41.7 constant_dynamic-update-slice_fusion.20
  4919.0 38.4 constant_dynamic-update-slice_fusion.19
  4960.0 38.7 constant_dynamic-update-slice_fusion.18
  5001.1 38.4 constant_dynamic-update-slice_fusion.17
  5042.0 38.4 constant_dynamic-update-slice_fusion.16
  5121.0 33.6 fusion
  (1063 shorter events, 2272.4 us)
Async XLA Ops:
  7.2 47.7 all-reduce.34.cloned.1.call-start
  23.4 185.7 %all-reduce.36.cloned.1.call-start = ((), (), s32[]{:S(2)}) async-start(), calls=%async_computation.1 | async-start | bytes 6291456 | tf_op jit(solution)/shard_map/psum | solution.py:54
  131.0 160.5 %all-gather.33.cloned.1.call-start = ((), (), s32[]{:S(2)}) async-start(), calls=%async_computation.32 | async-start | bytes 15728640 | tf_op jit(solution)/shard_map/all_gather | solution.py:55
  209.1 143.7 %all-reduce.38.cloned.1.call-start = ((), (), s32[]{:S(2)}) async-start(), calls=%async_computation.2 | async-start | bytes 524288 | tf_op jit(solution)/shard_map/psum | solution.py:46
  324.3 183.1 %all-reduce.40.cloned.1.call-start = ((), (), s32[]{:S(2)}) async-start(), calls=%async_computation.3 | async-start | bytes 6291456 | tf_op jit(solution)/shard_map/psum | solution.py:54
  428.2 161.5 %all-gather.35.cloned.1.call-start = ((), (), s32[]{:S(2)}) async-start(), calls=%async_computation.33 | async-start | bytes 15728640 | tf_op jit(solution)/shard_map/all_gather | solution.py:55
  507.4 143.6 %all-reduce.42.cloned.1.call-start = ((), (), s32[]{:S(2)}) async-start(), calls=%async_computation.4 | async-start | bytes 524288 | tf_op jit(solution)/shard_map/psum | solution.py:46
  622.4 184.0 %all-reduce.44.cloned.1.call-start = ((), (), s32[]{:S(2)}) async-start(), calls=%async_computation.5 | async-start | bytes 6291456 | tf_op jit(solution)/shard_map/psum | solution.py:54
  727.2 161.7 %all-gather.37.cloned.1.call-start = ((), (), s32[]{:S(2)}) async-start(), calls=%async_computation.34 | async-start | bytes 15728640 | tf_op jit(solution)/shard_map/all_gather | solution.py:55
  806.4 140.7 %all-reduce.46.cloned.1.call-start = ((), (), s32[]{:S(2)}) async-start(), calls=%async_computation.6 | async-start | bytes 524288 | tf_op jit(solution)/shard_map/psum | solution.py:46
  918.5 184.6 %all-reduce.48.cloned.1.call-start = ((), (), s32[]{:S(2)}) async-start(), calls=%async_computation.7 | async-start | bytes 6291456 | tf_op jit(solution)/shard_map/psum | solution.py:54
  1023.0 162.4 %all-gather.39.cloned.1.call-start = ((), (), s32[]{:S(2)}) async-start(), calls=%async_computation.35 | async-start | bytes 15728640 | tf_op jit(solution)/shard_map/all_gather | solution.py:55
  1103.1 136.8 %all-reduce.50.cloned.1.call-start = ((), (), s32[]{:S(2)}) async-start(), calls=%async_computation.8 | async-start | bytes 524288 | tf_op jit(solution)/shard_map/psum | solution.py:46
  1211.3 183.2 %all-reduce.52.cloned.1.call-start = ((), (), s32[]{:S(2)}) async-start(), calls=%async_computation.9 | async-start | bytes 6291456 | tf_op jit(solution)/shard_map/psum | solution.py:54
  1316.5 160.4 %all-gather.41.cloned.1.call-start = ((), (), s32[]{:S(2)}) async-start(), calls=%async_computation.36 | async-start | bytes 15728640 | tf_op jit(solution)/shard_map/all_gather | solution.py:55
  1394.5 136.8 %all-reduce.54.cloned.1.call-start = ((), (), s32[]{:S(2)}) async-start(), calls=%async_computation.10 | async-start | bytes 524288 | tf_op jit(solution)/shard_map/psum | solution.py:46
  1502.8 183.8 %all-reduce.56.cloned.1.call-start = ((), (), s32[]{:S(2)}) async-start(), calls=%async_computation.11 | async-start | bytes 6291456 | tf_op jit(solution)/shard_map/psum | solution.py:54
  1607.4 161.5 %all-gather.43.cloned.1.call-start = ((), (), s32[]{:S(2)}) async-start(), calls=%async_computation.37 | async-start | bytes 15728640 | tf_op jit(solution)/shard_map/all_gather | solution.py:55
  1686.6 136.8 %all-reduce.58.cloned.1.call-start = ((), (), s32[]{:S(2)}) async-start(), calls=%async_computation.12 | async-start | bytes 524288 | tf_op jit(solution)/shard_map/psum | solution.py:46
  1794.8 183.5 %all-reduce.60.cloned.1.call-start = ((), (), s32[]{:S(2)}) async-start(), calls=%async_computation.13 | async-start | bytes 6291456 | tf_op jit(solution)/shard_map/psum | solution.py:54
  1899.1 161.7 %all-gather.45.cloned.1.call-start = ((), (), s32[]{:S(2)}) async-start(), calls=%async_computation.38 | async-start | bytes 15728640 | tf_op jit(solution)/shard_map/all_gather | solution.py:55
  1978.3 136.9 %all-reduce.62.cloned.1.call-start = ((), (), s32[]{:S(2)}) async-start(), calls=%async_computation.14 | async-start | bytes 524288 | tf_op jit(solution)/shard_map/psum | solution.py:46
  2086.7 186.2 %all-reduce.64.cloned.1.call-start = ((), (), s32[]{:S(2)}) async-start(), calls=%async_computation.15 | async-start | bytes 6291456 | tf_op jit(solution)/shard_map/psum | solution.py:54
  2192.8 162.4 %all-gather.47.cloned.1.call-start = ((), (), s32[]{:S(2)}) async-start(), calls=%async_computation.39 | async-start | bytes 15728640 | tf_op jit(solution)/shard_map/all_gather | solution.py:55
  2272.9 132.3 %all-reduce.66.cloned.1.call-start = ((), (), s32[]{:S(2)}) async-start(), calls=%async_computation.16 | async-start | bytes 524288 | tf_op jit(solution)/shard_map/psum | solution.py:46
  2376.6 183.7 %all-reduce.68.cloned.1.call-start = ((), (), s32[]{:S(2)}) async-start(), calls=%async_computation.17 | async-start | bytes 6291456 | tf_op jit(solution)/shard_map/psum | solution.py:54
  2482.2 160.4 %all-gather.49.cloned.1.call-start = ((), (), s32[]{:S(2)}) async-start(), calls=%async_computation.40 | async-start | bytes 15728640 | tf_op jit(solution)/shard_map/all_gather | solution.py:55
  2560.3 132.4 %all-reduce.70.cloned.1.call-start = ((), (), s32[]{:S(2)}) async-start(), calls=%async_computation.18 | async-start | bytes 524288 | tf_op jit(solution)/shard_map/psum | solution.py:46
  2664.1 185.1 %all-reduce.72.cloned.1.call-start = ((), (), s32[]{:S(2)}) async-start(), calls=%async_computation.19 | async-start | bytes 6291456 | tf_op jit(solution)/shard_map/psum | solution.py:54
  2770.0 161.5 %all-gather.51.cloned.1.call-start = ((), (), s32[]{:S(2)}) async-start(), calls=%async_computation.41 | async-start | bytes 15728640 | tf_op jit(solution)/shard_map/all_gather | solution.py:55
  2849.2 132.4 %all-reduce.74.cloned.1.call-start = ((), (), s32[]{:S(2)}) async-start(), calls=%async_computation.20 | async-start | bytes 524288 | tf_op jit(solution)/shard_map/psum | solution.py:46
  2953.0 184.0 %all-reduce.76.cloned.1.call-start = ((), (), s32[]{:S(2)}) async-start(), calls=%async_computation.21 | async-start | bytes 6291456 | tf_op jit(solution)/shard_map/psum | solution.py:54
  3057.8 161.5 %all-gather.53.cloned.1.call-start = ((), (), s32[]{:S(2)}) async-start(), calls=%async_computation.42 | async-start | bytes 15728640 | tf_op jit(solution)/shard_map/all_gather | solution.py:55
  3137.0 132.4 %all-reduce.78.cloned.1.call-start = ((), (), s32[]{:S(2)}) async-start(), calls=%async_computation.22 | async-start | bytes 524288 | tf_op jit(solution)/shard_map/psum | solution.py:46
  3240.7 186.1 %all-reduce.80.cloned.1.call-start = ((), (), s32[]{:S(2)}) async-start(), calls=%async_computation.23 | async-start | bytes 6291456 | tf_op jit(solution)/shard_map/psum | solution.py:54
  3346.7 162.4 %all-gather.55.cloned.1.call-start = ((), (), s32[]{:S(2)}) async-start(), calls=%async_computation.43 | async-start | bytes 15728640 | tf_op jit(solution)/shard_map/all_gather | solution.py:55
  3426.9 129.9 %all-reduce.82.cloned.1.call-start = ((), (), s32[]{:S(2)}) async-start(), calls=%async_computation.24 | async-start | bytes 524288 | tf_op jit(solution)/shard_map/psum | solution.py:46
  3528.2 191.1 %all-reduce.84.cloned.1.call-start = ((), (), s32[]{:S(2)}) async-start(), calls=%async_computation.25 | async-start | bytes 6291456 | tf_op jit(solution)/shard_map/psum | solution.py:54
  3641.2 160.4 %all-gather.57.cloned.1.call-start = ((), (), s32[]{:S(2)}) async-start(), calls=%async_computation.44 | async-start | bytes 15728640 | tf_op jit(solution)/shard_map/all_gather | solution.py:55
  3719.3 129.7 %all-reduce.86.cloned.1.call-start = ((), (), s32[]{:S(2)}) async-start(), calls=%async_computation.26 | async-start | bytes 524288 | tf_op jit(solution)/shard_map/psum | solution.py:46
  3820.4 191.9 %all-reduce.88.cloned.1.call-start = ((), (), s32[]{:S(2)}) async-start(), calls=%async_computation.27 | async-start | bytes 6291456 | tf_op jit(solution)/shard_map/psum | solution.py:54
  3933.1 161.7 %all-gather.59.cloned.1.call-start = ((), (), s32[]{:S(2)}) async-start(), calls=%async_computation.45 | async-start | bytes 15728640 | tf_op jit(solution)/shard_map/all_gather | solution.py:55
  4012.4 129.8 %all-reduce.90.cloned.1.call-start = ((), (), s32[]{:S(2)}) async-start(), calls=%async_computation.28 | async-start | bytes 524288 | tf_op jit(solution)/shard_map/psum | solution.py:46
  4113.6 209.1 %all-reduce.92.cloned.1.call-start = ((), (), s32[]{:S(2)}) async-start(), calls=%async_computation.29 | async-start | bytes 6291456 | tf_op jit(solution)/shard_map/psum | solution.py:54
  4226.2 355.5 %all-gather.61.cloned.1.call-start = ((), (), s32[]{:S(2)}) async-start(), calls=%async_computation.46 | async-start | bytes 15728640 | tf_op jit(solution)/shard_map/all_gather | solution.py:55
  4322.7 306.6 %all-reduce.94.cloned.1.call-start = ((), (), s32[]{:S(2)}) async-start(), calls=%async_computation.30 | async-start | bytes 524288 | tf_op jit(solution)/shard_map/psum | solution.py:46
  4600.6 184.2 %all-reduce.96.cloned.1.call-start = ((), (), s32[]{:S(2)}) async-start(), calls=%async_computation.31 | async-start | bytes 6291456 | tf_op jit(solution)/shard_map/psum | solution.py:54
  4704.7 401.2 %all-gather.63.cloned.1.call-start = ((), (), s32[]{:S(2)}) async-start(), calls=%async_computation.47 | async-start | bytes 15728640 | tf_op jit(solution)/shard_map/all_gather | solution.py:55
  (146 other events, 3560.2 us)
Sparse Core Ops, SparseCore 0:
  23.6 31.2 all-reduce.33
  131.2 77.9 all-reduce.35
  210.7 80.8 all-gather.32
  324.4 28.4 all-reduce.37
  428.3 79.0 all-reduce.39
  508.8 80.8 all-gather.34
  622.5 28.4 all-reduce.41
  727.3 79.0 all-reduce.43
  807.9 80.8 all-gather.36
  918.7 28.4 all-reduce.45
  1023.1 79.9 all-reduce.47
  1104.5 80.8 all-gather.38
  1211.4 28.4 all-reduce.49
  1316.6 77.9 all-reduce.51
  1395.9 80.8 all-gather.40
  1502.9 28.4 all-reduce.53
  1607.5 79.0 all-reduce.55
  1688.0 80.8 all-gather.42
  1795.0 28.3 all-reduce.57
  1899.2 79.0 all-reduce.59
  1979.9 80.8 all-gather.44
  2086.8 28.3 all-reduce.61
  2192.9 79.9 all-reduce.63
  2274.3 80.8 all-gather.46
  2376.7 28.4 all-reduce.65
  2482.3 77.9 all-reduce.67
  2561.7 80.8 all-gather.48
  2664.3 28.4 all-reduce.69
  2770.1 79.0 all-reduce.71
  2850.6 80.8 all-gather.50
  2953.2 28.4 all-reduce.73
  3057.9 79.0 all-reduce.75
  3138.4 80.8 all-gather.52
  3240.9 28.5 all-reduce.77
  3346.9 79.9 all-reduce.79
  3428.2 80.8 all-gather.54
  3528.3 28.4 all-reduce.81
  3641.3 77.9 all-reduce.83
  3720.7 80.8 all-gather.56
  3820.5 28.4 all-reduce.85
  3933.3 79.0 all-reduce.87
  4013.9 80.8 all-gather.58
  4113.7 28.4 all-reduce.89
  4226.3 79.0 all-reduce.91
  4322.8 80.9 all-gather.60
  4600.7 28.5 all-reduce.93
  4704.8 79.9 all-reduce.95
  4786.2 80.8 all-gather.62
where the time goes:
time: 5180 us; the launch traced here: 5160 us
  waiting for transfers between devices  2570 us (50%)
  other arithmetic  1050 us (20%)
  matrix products  945 us (18%)
  local copies, waits for them, and re-layouts  542 us (10%)
    psum x16, waiting for transfers between devices, local_part(): lax.psum(jnp.where(my_col == owner_col, below_diag.reshape(local_rows, bl...  1140 us
    all_gather x16, waiting for transfers between devices, local_part(): gathered = lax.all_gather(row_panel, 'pr', axis=0, tiled=False)  1010 us
    dot_general x16, matrix products, apply_update(): lax.dot_general(rows_part, trail_view, (((1,), (1,)), ((), ())), precisio...  689 us
    another operation x111, other arithmetic, local_part(): l_diag = jnp.linalg.cholesky(diag_blk)  554 us
    psum x16, waiting for transfers between devices, local_part(): diag_blk = lax.psum(jnp.where(my_row == owner_row, diag_local, 0.0), 'pr')  421 us
    another operation x33, other arithmetic, solve_right(): lax.linalg.triangular_solve(l_diag, right_side, left_side=False, lower=Tr...  355 us
    all_gather x16, local copies, waits for them, and re-layouts, local_part(): gathered = lax.all_gather(row_panel, 'pr', axis=0, tiled=False)  202 us
    dot_general x15, matrix products, apply_update(): jnp.einsum('rc,mbc->rmb', rows_part, col_view[col_start:panel_dev], preci...  148 us
  transfers between devices with their start and end apart: 48, of which 45 were waited for; matrix products, arithmetic and copies ran while one was open for 17% of the time, Pallas kernels for 0%

commit v1 on v0

v1 whole, which is shorter than its diff:
```python
import functools

import jax
import jax.numpy as jnp
from jax import lax
from jax.experimental import pallas as pl
from jax.experimental.pallas import tpu as pltpu
from jax.sharding import PartitionSpec as P


F32 = jnp.float32
BF16 = jnp.bfloat16
HIGH = lax.Precision.HIGHEST
NB = 256
SUP = 1024
VMEM_LIMIT = 60 * 1024 * 1024


def dot(a, b):
    return lax.dot_general(a, b, (((1,), (0,)), ((), ())), precision=HIGH, preferred_element_type=F32)


def dot_nt(a, b):
    return lax.dot_general(a, b, (((1,), (1,)), ((), ())), precision=HIGH, preferred_element_type=F32)


def dot_tn(a, b):
    return lax.dot_general(a, b, (((0,), (0,)), ((), ())), precision=HIGH, preferred_element_type=F32)


def split3(x):
    high = x.astype(BF16)
    rest = x - high.astype(F32)
    mid = rest.astype(BF16)
    return high, mid, (rest - mid.astype(F32)).astype(BF16)


def panel32(work, p):
    r0 = 32 * p
    diag_tile = p // 4
    lane0 = r0 % 128
    tiles = [0, 1, 2] if p < 4 else [1, 2, 3]
    rows = {ti: [work[r0 + 8 * sg:r0 + 8 * sg + 8, 128 * ti:128 * ti + 128] for sg in range(4)] for ti in tiles}
    sub_id = lax.broadcasted_iota(jnp.int32, (8, 128), 0)

    def over_lanes(u, sg):
        return jnp.broadcast_to(rows[diag_tile][sg][:, lane0 + u:lane0 + u + 1], (8, 128))

    def over_sublanes(v, i):
        return jnp.broadcast_to(v[i:i + 1, :], (8, 128))

    col, fac = {}, {}
    for u in range(16):
        for sg in range(u // 8, 4):
            col[u, sg] = over_lanes(u, sg)
    for g in range(4):
        for t in range(8 * g, 8 * g + 8):
            tt = t - 8 * g
            rs = lax.rsqrt(over_sublanes(col[t, g], tt))
            for sg in range(g, 4):
                fac[t, sg] = col[t, sg] * rs
            for u in range(t + 1, min(8 * g + 16, 32)):
                ug = u // 8
                s = over_sublanes(fac[t, ug], u - 8 * ug)
                for sg in range(ug, 4):
                    col[u, sg] = col[u, sg] - fac[t, sg] * s
            for ti in tiles:
                row = over_sublanes(rows[ti][g], tt) * rs
                own = rows[ti][g] - fac[t, g] * row
                rows[ti][g] = jnp.where(sub_id > tt, own, jnp.where(sub_id == tt, row, rows[ti][g]))
                for sg in range(g + 1, 4):
                    rows[ti][sg] = rows[ti][sg] - fac[t, sg] * row
        if g < 2:
            for u in range(8 * g + 16, 8 * g + 24):
                for sg in range(u // 8, 4):
                    col[u, sg] = over_lanes(u, sg)
    for ti in tiles:
        for sg in range(4):
            work[r0 + 8 * sg:r0 + 8 * sg + 8, 128 * ti:128 * ti + 128] = rows[ti][sg]
    if p == 7:
        return
    high, mid, low = split3(jnp.concatenate([jnp.concatenate(rows[ti], axis=0) for ti in tiles], axis=1))
    first = (r0 + 32 - 128 * diag_tile) // 128 * 128
    rhs = jnp.concatenate([high, mid, high, mid, low, high], axis=0)
    lhs = jnp.concatenate([high, high, mid, mid, high, low], axis=0)[:, first:256 - 128 * diag_tile]
    upd = lax.dot_general(lhs, rhs, (((0,), (0,)), ((), ())), preferred_element_type=F32)
    skip = r0 + 32 - first - 128 * diag_tile
    for j, ti in enumerate(tiles):
        lanes = slice(128 * ti, 128 * ti + 128)
        work[r0 + 32:256, lanes] = work[r0 + 32:256, lanes] - upd[skip:, 128 * j:128 * j + 128]


def factor_kernel(*refs):
    blocks, (x_ref, own_l_ref, own_diag_ref, u_ref, work) = refs[:-5], refs[-5:]
    my_col, my_row = lax.axis_index("pc"), lax.axis_index("pr")
    row = lax.broadcasted_iota(jnp.int32, (NB, NB), 0)
    col = lax.broadcasted_iota(jnp.int32, (NB, NB), 1)
    for c in range(4):
        for r in range(4):
            if len(blocks) == 1:
                u_ref[NB * r:NB * r + NB, NB * c:NB * c + NB] = blocks[0][4 * c + r]
            else:
                at_row, at_col = (pl.ds(pl.multiple_of(v * NB, NB), NB) for v in (my_row ^ r, my_col ^ c))
                u_ref[at_row, at_col] = blocks[4 * c + r][...]
    x_ref[...] = jnp.zeros_like(x_ref)
    for b in range(4):
        a, e = NB * b, NB * b + NB
        work[:, :NB] = u_ref[a:e, a:e]
        work[:, NB:] = jnp.where(row == col, 1.0, 0.0)
        for p in range(8):
            panel32(work, p)
        ubb = jnp.where(col >= row, work[:, :NB], 0.0)
        xbb = jnp.where(col <= row, work[:, NB:], 0.0)
        u_ref[a:e, a:e] = ubb
        if b > 0:
            x_ref[a:e, :a] = dot(xbb, x_ref[a:e, :a])
            u_ref[a:e, :a] = jnp.zeros((NB, a), F32)
        x_ref[a:e, a:e] = xbb
        if b < 3:
            urow = dot(xbb, u_ref[a:e, e:])
            u_ref[a:e, e:] = urow
            for c in range(b + 1, 4):
                lo = NB * c
                uc = urow[:, lo - e:lo - e + NB]
                u_ref[lo:lo + NB, lo:] = u_ref[lo:lo + NB, lo:] - dot_tn(uc, urow[:, lo - e:])
                x_ref[lo:lo + NB, :e] = x_ref[lo:lo + NB, :e] - dot_tn(uc, x_ref[a:e, :e])
    at_row = pl.ds(pl.multiple_of(my_row * NB, NB), NB)
    at_col = pl.ds(pl.multiple_of(my_col * NB, NB), NB)
    own_l_ref[...] = u_ref[at_col, at_row].T
    own_diag_ref[...] = u_ref[at_row, at_row]


def call(kernel, flops, moved, **kw):
    cost = pl.CostEstimate(flops=flops, bytes_accessed=moved, transcendentals=0)
    return pl.pallas_call(kernel, cost_estimate=cost, compiler_params=pltpu.CompilerParams(vmem_limit_bytes=VMEM_LIMIT), **kw)


def shape(*dims):
    return jax.ShapeDtypeStruct(dims, F32)


def factor(blocks):
    vmem = pl.BlockSpec(memory_space=pltpu.VMEM)
    return call(
        factor_kernel, 30_000_000_000, 1 << 24,
        out_shape=(shape(SUP, SUP), shape(NB, NB), shape(NB, NB)), in_specs=[vmem] * len(blocks), out_specs=(vmem,) * 3,
        scratch_shapes=[pltpu.VMEM((SUP, SUP), F32), pltpu.VMEM((NB, 2 * NB), F32)],
    )(*blocks)


def flat_panel(panel):
    return panel.reshape(-1, 4, 2, 128).transpose(0, 2, 1, 3).reshape(-1, 128)


def unpack_kernel(in_ref, rest_ref):
    for n, s in enumerate((3, 2, 1)):
        for half in range(2):
            rest_ref[:, NB * n + 128 * half:NB * n + 128 * half + 128] = in_ref[pl.ds(4 * half + s, NB, stride=8), :]


def unpack(panel):
    rows = panel.shape[0] - NB
    return call(
        unpack_kernel, 1_000_000, 8 * rows * SUP, grid=(rows // NB,), out_shape=shape(rows, 3 * NB),
        in_specs=[pl.BlockSpec((8 * NB, 128), lambda i: (i + 1, 0))], out_specs=pl.BlockSpec((NB, 3 * NB), lambda i: (i, 0)),
    )(flat_panel(panel))


def pack_rows(i, cols, diags, out_ref):
    for s in range(4):
        def put(value, s=s):
            for half in range(2):
                out_ref[pl.ds(4 * half + s, NB, stride=8), :] = value[:, 128 * half:128 * half + 128]

        pl.when(i < s)(lambda: put(jnp.zeros((NB, NB), F32)))
        pl.when(i == s)(lambda s=s: put(diags[s][...]))
        pl.when(i > s)(lambda s=s: put(cols[s][...]))


def rows_kernel(split, own, y, z, top, bottom, x_ref, out_ref, own_ref, wide):
    my_col = lax.axis_index("pc")
    i = pl.program_id(0)

    def place(flip, ref):
        wide[:, pl.ds(pl.multiple_of((my_col ^ flip) * NB, NB), NB)] = ref[...]

    place(0, own)
    place(1, y)
    place(2, z)
    pl.when(i < split)(lambda: place(3, top))
    pl.when(i >= split)(lambda: place(3, bottom))
    for k in range(4):
        lanes = slice(NB * k, NB * k + NB)
        part = dot_nt(wide[:, lanes], x_ref[NB * k:, lanes])
        out_ref[:, NB * k:] = part if k == 0 else out_ref[:, NB * k:] + part
    own_ref[...] = out_ref[:, pl.ds(pl.multiple_of(my_col * NB, NB), NB)]


def solve_rows(pieces, x):
    own, _, _, _, _ = pieces
    rows = own.shape[0]
    tile = rows // 4
    split = 2
    block = pl.BlockSpec((tile, NB), lambda i: (i, 0))
    return call(
        functools.partial(rows_kernel, split), 30 * rows * SUP * SUP // 4, 12 * rows * SUP, grid=(4,),
        out_shape=(shape(rows, SUP), shape(rows, NB)),
        in_specs=[block, block, block, pl.BlockSpec((tile, NB), lambda i: (jnp.minimum(i, split - 1), 0)),
                  pl.BlockSpec((tile, NB), lambda i: (jnp.maximum(i - split, 0), 0)), pl.BlockSpec((SUP, SUP), lambda i: (0, 0))],
        out_specs=(pl.BlockSpec((tile, SUP), lambda i: (i, 0)), block),
        scratch_shapes=[pltpu.VMEM((tile, SUP), F32)],
    )(*pieces, x)


def cols_kernel(*refs):
    pieces, x_ref, outs, tall = refs[:4], refs[4], refs[5:-1], refs[-1]
    my_row = lax.axis_index("pr")
    i = pl.program_id(0)
    for j in range(4):
        tall[pl.ds(pl.multiple_of((my_row ^ j) * NB, NB), NB), :] = pieces[j][...]

    def put(ref):
        for k in range(4):
            e = NB * (k + 1)
            ref[NB * k:e, :] = dot(x_ref[NB * k:e, :e], tall[:e, :])

    if len(outs) == 1:
        put(outs[0])
    else:
        pl.when(i < 4)(lambda: put(outs[0]))
        pl.when(i >= 4)(lambda: put(outs[1]))


def solve_cols(pieces, x):
    cols = pieces[0].shape[1]
    outs = [shape(SUP, min(SUP, cols))] + ([shape(SUP, cols - SUP)] if cols > SUP else [])
    specs = [pl.BlockSpec((SUP, NB), lambda i: (0, jnp.minimum(i, min(SUP, cols) // NB - 1))), pl.BlockSpec((SUP, NB), lambda i: (0, jnp.maximum(i - 4, 0)))]
    return call(
        cols_kernel, 30 * cols * SUP * SUP // 4, 12 * cols * SUP, grid=(cols // NB,), out_shape=outs,
        in_specs=[pl.BlockSpec((NB, NB), lambda i: (0, i))] * 4 + [pl.BlockSpec((SUP, SUP), lambda i: (0, 0))],
        out_specs=specs[:len(outs)], scratch_shapes=[pltpu.VMEM((SUP, NB), F32)],
    )(*pieces, x)


def panel_kernel(*refs):
    rest_ref, l_ref, u_ref, diag_ref, col_ref = refs[:5]
    keep = rest_ref.shape[1] - NB
    new = rest_ref[...] - dot(l_ref[...], u_ref[...])
    i = pl.program_id(0)

    @pl.when(i == 0)
    def _():
        diag_ref[...] = new[:, keep:]
        if keep:
            refs[5][...] = new[:, :keep]

    @pl.when(i > 0)
    def _():
        col_ref[...] = new[:, keep:]
        if keep:
            refs[6][...] = new[:, :keep]


def update_panel(rest, l_rows, u_panel):
    rows, width = rest.shape
    keep = width - NB
    below = lambda i: (jnp.maximum(i - 1, 0), 0)
    zero = lambda i: (0, 0)
    outs = [shape(NB, NB), shape(rows - NB, NB)] + ([shape(NB, keep), shape(rows - NB, keep)] if keep else [])
    specs = [pl.BlockSpec((NB, NB), zero), pl.BlockSpec((NB, NB), below)]
    if keep:
        specs += [pl.BlockSpec((NB, keep), zero), pl.BlockSpec((NB, keep), below)]
    return call(
        panel_kernel, 12 * rows * width * SUP, 8 * rows * width + 4 * rows * SUP, grid=(rows // NB,), out_shape=outs,
        in_specs=[pl.BlockSpec((NB, width), lambda i: (i, 0)), pl.BlockSpec((NB, SUP), lambda i: (i, 0)), pl.BlockSpec((SUP, width), zero)],
        out_specs=specs,
    )(rest, l_rows, u_panel)


def row_kernel(*refs):
    trail_ref, l_ref, mine_ref, theirs_ref = refs[1:5]
    keep_ref, send_ref = refs[-2:]
    j = pl.program_id(0)

    @pl.when(j == 0)
    def _():
        keep_ref[:, :SUP] = trail_ref[...] - dot(l_ref[...], mine_ref[...])
        if len(refs) == 8:
            keep_ref[:, SUP:] = refs[5][...]
            send_ref[:, SUP:] = refs[5][...]

    @pl.when(j == 1)
    def _():
        send_ref[:, :SUP] = trail_ref[...] - dot(l_ref[...], theirs_ref[...])


def update_row(core, trail, l_rows, mine, theirs, panel_row, step):
    extra = [] if panel_row is None else [panel_row]
    width = SUP + (0 if panel_row is None else panel_row.shape[1])
    whole = lambda a: pl.BlockSpec(a.shape, lambda j, h: (0, 0))
    out = pl.BlockSpec((NB, width), lambda j, h: (0, 0))
    return call(
        row_kernel, 24 * NB * SUP * SUP, 12 * SUP * SUP,
        grid_spec=pltpu.PrefetchScalarGridSpec(
            num_scalar_prefetch=1, grid=(2,),
            in_specs=[pl.BlockSpec((NB, SUP), lambda j, h: (step + 1, h[0] ^ j)), pl.BlockSpec((NB, SUP), lambda j, h: (0, 0)),
                      whole(mine), whole(theirs)] + [whole(a) for a in extra],
            out_specs=(out, out)),
        out_shape=(shape(NB, width), shape(NB, width)),
    )(core, trail, l_rows, mine, theirs, *extra)


def trail_kernel(core_ref, trail_ref, l_ref, mine_ref, theirs_ref, diag_ref, *rest):
    my_row = lax.axis_index("pr")
    j, i = pl.program_id(0), pl.program_id(1)
    out_ref = rest[0]
    if len(rest) > 1:
        out_ref = rest[8]
        pack_rows(jnp.minimum(j * pl.num_programs(1) + i, pl.num_programs(1) + 2), rest[:4], rest[4:8], rest[9])

    def go(u_ref):
        @pl.when(i == 0)
        def _():
            own = u_ref[pl.ds(pl.multiple_of(my_row * NB, NB), NB), :]
            out_ref[...] = dot_tn(diag_ref[...], own)

        @pl.when(i > 0)
        def _():
            out_ref[...] = trail_ref[...] - dot(l_ref[...], u_ref[...])

    pl.when(j == 0)(lambda: go(mine_ref))
    pl.when(j == 1)(lambda: go(theirs_ref))


def update_trail(core, trail, l_rows, mine, theirs, own_diag, step, out_cols=(), out_diags=()):
    rows, cols = trail.shape
    off = 1 if step < 3 else 0
    count = rows // NB - step - off
    at = pl.BlockSpec((NB, SUP), lambda j, i, h: (jnp.where(i == 0, step, step + off + i), h[0] ^ j))
    whole = pl.BlockSpec((SUP, SUP), lambda j, i, h: (0, 0))
    ins = [at, pl.BlockSpec((NB, SUP), lambda j, i, h: (jnp.maximum(i, 1) - 1 + off, 0)), whole, whole,
           pl.BlockSpec((NB, NB), lambda j, i, h: (0, 0))]
    outs, shapes = [at], [shape(rows, cols)]
    if out_cols:
        block = lambda j, i: jnp.minimum(j * count + i, rows // NB - 1)
        ins += [pl.BlockSpec((NB, NB), lambda j, i, h, s=s: (jnp.maximum(block(j, i) - s - 1, 0), 0)) for s in range(4)]
        ins += [pl.BlockSpec((NB, NB), lambda j, i, h: (0, 0))] * 4
        outs.append(pl.BlockSpec((8 * NB, 128), lambda j, i, h: (block(j, i), 0)))
        shapes.append(shape(rows * 8, 128))
    return call(
        trail_kernel, 12 * count * NB * cols * SUP, 8 * count * NB * cols,
        grid_spec=pltpu.PrefetchScalarGridSpec(num_scalar_prefetch=1, grid=(2, count), in_specs=ins, out_specs=outs),
        out_shape=shapes, input_output_aliases={1: 0} if step else {},
    )(core, trail, l_rows, mine, theirs, own_diag, *out_cols, *out_diags)


FLIP1 = [(0, 1), (1, 0), (2, 3), (3, 2)]
FLIP2 = [(0, 2), (2, 0), (1, 3), (3, 1)]
FLIP3 = [(0, 3), (3, 0), (1, 2), (2, 1)]


def gather_diag(block):
    got = {(0, 0): block}
    for jc in range(4):
        for jr in (0, 2):
            if (jc, jr) != (0, 0):
                perm = [(4 * c + r, 4 * (c ^ jc) + (r ^ jr)) for c in range(4) for r in range(4)]
                got[jc, jr] = lax.ppermute(block, ("pc", "pr"), perm)
    for jc in range(4):
        for jr in (0, 2):
            got[jc, jr + 1] = lax.ppermute(got[jc, jr], "pr", FLIP1)
    return [got[jc, jr] for jc in range(4) for jr in range(4)]


def gather_cols(keep, send):
    return [keep, lax.ppermute(send, "pr", FLIP1), lax.ppermute(keep, "pr", FLIP2), lax.ppermute(send, "pr", FLIP3)]


def gather_all(panel):
    x = lax.ppermute(panel, "pr", FLIP2)
    return [panel, lax.ppermute(panel, "pr", FLIP1), x, lax.ppermute(x, "pr", FLIP1)]


def solution(mesh):
    def local_part(panel_tile, trail_tile):
        my_row = lax.axis_index("pr")
        half = my_row % 2
        core = jnp.full((1,), half, jnp.int32)
        trail = trail_tile
        out_cols, out_diags = [], []
        for step in range(4):
            if step == 0:
                blocks = gather_diag(panel_tile[:NB, 0, :])
                col_panel = panel_tile[NB:, 0, :]
                keep, send = (lax.dynamic_slice(trail_tile, (0, SUP * h), (NB, SUP)) for h in (half, 1 - half))
                panel_row = jnp.concatenate([panel_tile[:NB, s, :] for s in (3, 2, 1)], axis=1)
                rest = unpack(panel_tile)
            else:
                blocks = [lax.all_gather(diag_block, ("pc", "pr"))]
            y = lax.ppermute(col_panel, "pc", FLIP1)
            z = lax.ppermute(col_panel, "pc", FLIP2)
            col_pieces = gather_cols(keep, send)
            if step == 0:
                row_pieces = gather_all(panel_row)
            if step:
                trail, = update_trail(core, trail, l_rows, mine, theirs, own_diag, step - 1)
                blocks, y, z, trail = lax.optimization_barrier((blocks, y, z, trail))
            split = col_panel.shape[0] // 2
            top = lax.ppermute(z[:split], "pc", FLIP1)
            bottom = lax.ppermute(y[split:], "pc", FLIP2)
            x_sup, own_l, own_diag = factor(blocks)
            mine, *more = solve_cols(col_pieces, x_sup)
            if step == 0:
                more = solve_cols(row_pieces, x_sup)
            theirs = lax.ppermute(mine, "pr", FLIP1)
            l_rows, own_col = solve_rows([col_panel, y, z, top, bottom], x_sup)
            out_cols.append(own_col)
            out_diags.append(own_l)
            if step < 3:
                diag_block, col_panel, *left = update_panel(rest, l_rows, more[0])
                panel_row, rest = left if left else (None, None)
                keep, send = update_row(core, trail, l_rows, mine, theirs, panel_row, step)
        trail, flat = update_trail(core, trail, l_rows, mine, theirs, own_diag, 3, out_cols, out_diags)
        rows = trail.shape[0]
        return flat.reshape(rows, 2, 4, 128).transpose(0, 2, 1, 3).reshape(rows, 4, NB), trail

    spec_panel = P("pr", "pc", None)
    spec_trail = P("pr", "pc")
    return jax.shard_map(local_part, mesh=mesh, in_specs=(spec_panel, spec_trail), out_specs=(spec_panel, spec_trail), check_vma=False)
```

time: 5180 us -> 954 us (0.18)
  waiting for transfers between devices: 2570 us -> 128 us
  other arithmetic: 1050 us -> 0.93 us
  matrix products: 945 us -> 0 us
  Pallas kernels: 0 us -> 737 us
  local copies, waits for them, and re-layouts: 542 us -> 31.4 us
    psum x32 -> x0, waiting for transfers between devices: 1560 us -> none  [the longest x16 1140 us: local_part(): lax.psum(jnp.where(my_col == owner_col, below_diag.reshape(local_rows, bl...]
    all_gather x16 -> x3, waiting for transfers between devices: 1010 us -> 0.06 us  [local_part(): blocks = [lax.all_gather(diag_block, ('pc', 'pr'))]]
    another operation x144 -> x0, other arithmetic: 909 us -> none  [the longest x111 554 us: local_part(): l_diag = jnp.linalg.cholesky(diag_blk)]
    dot_general x31 -> x0, matrix products: 837 us -> none  [the longest x16 689 us: apply_update(): lax.dot_general(rows_part, trail_view, (((1,), (1,)), ((), ())), precisio...]
    pallas_call x0 -> x24, Pallas kernels: none -> 737 us  [the longest x4 294 us: update_trail(): call(trail_kernel, 12 * count * NB * cols * SUP, 8 * count * NB * cols, g...]
    all_gather x16 -> x0, local copies, waits for them, and re-layouts: 202 us -> none  [local_part(): gathered = lax.all_gather(row_panel, 'pr', axis=0, tiled=False)]
    ppermute x0 -> x50, waiting for transfers between devices: none -> 128 us  [the longest x7 80.4 us: gather_diag(): got[jc, jr] = lax.ppermute(block, ('pc', 'pr'), perm)]
    another operation x80 -> x0, matrix products: 108 us -> none  [the longest x48 73.6 us: solve_right(): lax.linalg.triangular_solve(l_diag, right_side, left_side=False, lower=Tr...]
  transfers between devices with their start and end apart: 48 -> 53, of which waited for: 45 -> 9; matrix products, arithmetic and copies ran while one was open for 17% -> 2% of each run, Pallas kernels for 0% -> 68%
where the time goes in v1:
time: 954 us; the launch traced here: 950 us
  Pallas kernels  737 us (77%)
  waiting for transfers between devices  128 us (13%)
  starting transfers between devices  37.9 us (4%)
  local copies, waits for them, and re-layouts  31.4 us (3%)
  between operations  14.5 us (2%)
    pallas_call x4, Pallas kernels, update_trail(): call(trail_kernel, 12 * count * NB * cols * SUP, 8 * count * NB * cols, g...  294 us
    pallas_call x4, Pallas kernels, factor(): call(factor_kernel, 30000000000, 1 << 24, out_shape=(shape(SUP, SUP), sha...  137 us
    pallas_call x4, Pallas kernels, solve_rows(): call(functools.partial(rows_kernel, split), 30 * rows * SUP * SUP // 4, 1...  107 us
    ppermute x7, waiting for transfers between devices, gather_diag(): got[jc, jr] = lax.ppermute(block, ('pc', 'pr'), perm)  80.4 us
    pallas_call x5, Pallas kernels, solve_cols(): call(cols_kernel, 30 * cols * SUP * SUP // 4, 12 * cols * SUP, grid=(cols...  74.9 us
    pallas_call x3, Pallas kernels, update_panel(): call(panel_kernel, 12 * rows * width * SUP, 8 * rows * width + 4 * rows *...  72.2 us
    pallas_call x3, Pallas kernels, update_row(): call(row_kernel, 24 * NB * SUP * SUP, 12 * SUP * SUP, grid_spec=pltpu.Pre...  38.8 us
    ppermute x4, waiting for transfers between devices, local_part(): top = lax.ppermute(z[:split], 'pc', FLIP1)  24.3 us
  transfers between devices with their start and end apart: 53, of which 9 were waited for; matrix products, arithmetic and copies ran while one was open for 2% of the time, Pallas kernels for 68%

profile of v1, /device:TPU:0, one launch (start us, length us, event | category | flops | bytes accessed | tf_op | source)
XLA Modules:
  0.0 949.6 jit_solution(7995157748875069801)
XLA Ops:
  7.2 6.5 slice.39
  13.9 3.3 collective-permute-start.1
  17.2 1.5 collective-permute-start
  18.7 4.5 fusion
  23.2 1.5 collective-permute-start.9
  25.2 1.5 collective-permute-start.13
  26.7 6.6 collective-permute-done.9.refs_6_
  33.4 63.3 %collective-permute-done.11.refs_8_ = f32[256,256]{1,0:T(8,128)} collective-permute-done((f32[256,256]{1,0:T(8,128)S(1)}, f32[256,256]{1,0:T(8,128)}, u32[]{:S(2)}, u32[]{:S(2)}) %collective-permute-start.11) | collective-permute-done | bytes 262176 | tf_op jit(solution)/shard_map/ppermute | solution.py:368
  96.7 3.6 collective-permute-start.17
  101.3 6.3 collective-permute-done.17.refs_14_
  107.7 4.1 collective-permute-done.5.refs_2_
  114.1 3.2 constant_dynamic-slice_fusion
  117.4 1.5 collective-permute-start.25
  120.5 1.5 collective-permute-start.20
  122.6 12.7 %shard_map.41.refs_0_ = f32[2816,768]{1,0:T(8,128)} custom-call(f32[24576,128]{1,0:T(8,128)} %bitcast.27), custom_call_target="tpu_custom_call" | custom-call | flops 1000000 | bytes 23068672 | tf_op jit(solution)/shard_map/pallas_call | solution.py:163
  135.3 1.5 slice.52
  136.8 1.5 slice.53
  139.2 21.4 %collective-permute-done.20.refs_2_ = f32[256,768]{1,0:T(8,128)} collective-permute-done((f32[256,768]{1,0:T(8,128)}, f32[256,768]{1,0:T(8,128)}, u32[]{:S(2)}, u32[]{:S(2)}) %collective-permute-start.20) | collective-permute-done | bytes 786464 | tf_op jit(solution)/shard_map/ppermute | solution.py:380
  161.7 34.2 %shard_map.42 = (f32[1024,1024]{1,0:T(8,128)}, f32[256,256]{1,0:T(8,128)}, f32[256,256]{1,0:T(8,128)}) custom-call(f32[256,256]{1,0:T(8,128)} %bitcast.40, f32[256,256]{1,0:T(8,128)} %copy-done.16, f32[256,256]{1,0:T(8,128)} %collective-permute-done.5.refs_2_, f32[256,256]{1,0:T(8,128)} %copy-done.19, f32[256,256]{1,0:T(8,128)} %collective-permute-done.7.refs_4_, ...), custom_call_target="tpu_custom_call" | custom-call | flops 30000001024 | bytes 16777216 | tf_op jit(solution)/shard_map/pallas_call | solution.py:144
  196.9 13.8 %shard_map.46.mine_ref.refs_3_ = f32[1024,1024]{1,0:T(8,128)} custom-call(f32[256,1024]{1,0:T(8,128)} %get-tuple-element.111.refs_0_, f32[256,1024]{1,0:T(8,128)} %collective-permute-done.24.refs_1_, f32[256,1024]{1,0:T(8,128)} %collective-permute-done.25.refs_2_, f32[256,1024]{1,0:T(8,128)} %copy-done.9, f32[1024,1024]{1,0:T(8,128)} %get-tuple-element.56.x_ref.refs_4_), custom_call_target="tpu_custom_call" | custom-call | flops 8053063680 | bytes 12582912 | tf_op jit(solution)/shard_map/pallas_call | solution.py:238
  210.7 11.3 %shard_map.44.refs_2_ = f32[1024,768]{1,0:T(8,128)} custom-call(f32[256,768]{1,0:T(8,128)} %pad_maximum_fusion.refs_0_, f32[256,768]{1,0:T(8,128)} %collective-permute-done.19.refs_1_, f32[256,768]{1,0:T(8,128)} %collective-permute-done.20.refs_2_, f32[256,768]{1,0:T(8,128)} %collective-permute-done.21.refs_3_, f32[1024,1024]{1,0:T(8,128)} %get-tuple-element.56.x_ref.refs_4_), custom_call_target="tpu_custom_call" | custom-call | flops 6039797760 | bytes 9437184 | tf_op jit(solution)/shard_map/pallas_call | solution.py:238
  222.1 30.5 %shard_map.43 = (f32[2816,1024]{1,0:T(8,128)}, f32[2816,256]{1,0:T(8,128)}) custom-call(f32[2816,256]{1,0:T(8,128)} %bitcast.30, f32[2816,256]{1,0:T(8,128)} %collective-permute-done.y, f32[2816,256]{1,0:T(8,128)} %collective-permute-done.1.z, f32[1408,256]{1,0:T(8,128)} %collective-permute-done.2.top, f32[1408,256]{1,0:T(8,128)} %collective-permute-done.3.bottom, ...), custom_call_target="tpu_custom_call" | custom-call | flops 22145925120 | bytes 34603008 | tf_op jit(solution)/shard_map/pallas_call | solution.py:205
  252.6 35.4 %shard_map.45 = (f32[256,256]{1,0:T(8,128)}, f32[2560,256]{1,0:T(8,128)}, f32[256,512]{1,0:T(8,128)}, f32[2560,512]{1,0:T(8,128)}) custom-call(f32[2816,768]{1,0:T(8,128)} %shard_map.41.refs_0_, f32[2816,1024]{1,0:T(8,128)} %get-tuple-element.57.refs_1_.l_ref.refs_2_, f32[1024,768]{1,0:T(8,128)} %shard_map.44.refs_2_), custom_call_target="tpu_custom_call" | custom-call | flops 26575110144 | bytes 28835840 | tf_op jit(solution)/shard_map/pallas_call | solution.py:273
  289.5 1.6 collective-permute-start.23
  291.1 13.5 %shard_map.50 = (f32[256,1536]{1,0:T(8,128)}, f32[256,1536]{1,0:T(8,128)}) custom-call(s32[1]{0:T(128)} %bitcast.core_ref.refs_0_, f32[3072,2048]{1,0:T(8,128)} %refs_1_.1, f32[2816,1024]{1,0:T(8,128)} %get-tuple-element.57.refs_1_.l_ref.refs_2_, f32[1024,1024]{1,0:T(8,128)} %shard_map.46.mine_ref.refs_3_, ...), custom_call_target="tpu_custom_call" | custom-call | flops 6442450944 | bytes 12582912 | tf_op jit(solution)/shard_map/pallas_call | solution.py:302
  304.6 1.5 collective-permute-start.32
  306.7 80.5 %shard_map.47.trail_ref.refs_1_ = f32[3072,2048]{1,0:T(8,128)} custom-call(s32[1]{0:T(128)} %bitcast.core_ref.refs_0_, f32[3072,2048]{1,0:T(8,128)} %refs_1_.1, f32[2816,1024]{1,0:T(8,128)} %get-tuple-element.57.refs_1_.l_ref.refs_2_, f32[1024,1024]{1,0:T(8,128)} %shard_map.46.mine_ref.refs_3_, f32[1024,1024]{1,0:T(8,128)} %collective-permute-done.27.theirs_ref.refs_4_, ...), custom_call_target="tpu_custom_call" | custom-call | flops 70866960384 | bytes 46137344 | tf_op jit(solution)/shard_map/pallas_call | solution.py:350
  387.3 1.5 copy-done.3
  391.3 34.1 %shard_map.48 = (f32[1024,1024]{1,0:T(8,128)}, f32[256,256]{1,0:T(8,128)}, f32[256,256]{1,0:T(8,128)}) custom-call(f32[16,256,256]{2,1,0:T(8,128)} %bitcast.42), custom_call_target="tpu_custom_call" | custom-call | flops 30000001024 | bytes 16777216 | tf_op jit(solution)/shard_map/pallas_call | solution.py:144
  425.4 19.3 %shard_map.51 = (f32[1024,1024]{1,0:T(8,128)}, f32[1024,512]{1,0:T(8,128)}) custom-call(f32[256,1536]{1,0:T(8,128)} %get-tuple-element.68.refs_0_, f32[256,1536]{1,0:T(8,128)} %collective-permute-done.30.refs_1_, f32[256,1536]{1,0:T(8,128)} %collective-permute-done.31.refs_2_, f32[256,1536]{1,0:T(8,128)} %collective-permute-done.32.refs_3_, ...), custom_call_target="tpu_custom_call" | custom-call | flops 12079595520 | bytes 18874368 | tf_op jit(solution)/shard_map/pallas_call | solution.py:238
  445.9 27.9 %shard_map.49 = (f32[2560,1024]{1,0:T(8,128)}, f32[2560,256]{1,0:T(8,128)}) custom-call(f32[2560,256]{1,0:T(8,128)} %get-tuple-element.59.own, f32[2560,256]{1,0:T(8,128)} %collective-permute-done.22.y, f32[2560,256]{1,0:T(8,128)} %copy-done.3, f32[1280,256]{1,0:T(8,128)} %collective-permute-done.28.top, f32[1280,256]{1,0:T(8,128)} %copy-done.7, ...), custom_call_target="tpu_custom_call" | custom-call | flops 20132659200 | bytes 31457280 | tf_op jit(solution)/shard_map/pallas_call | solution.py:205
  473.7 22.9 %shard_map.52 = (f32[256,256]{1,0:T(8,128)}, f32[2304,256]{1,0:T(8,128)}, f32[256,256]{1,0:T(8,128)}, f32[2304,256]{1,0:T(8,128)}) custom-call(f32[2560,512]{1,0:T(8,128)} %get-tuple-element.58.refs_0_, f32[2560,1024]{1,0:T(8,128)} %get-tuple-element.66.refs_1_.l_ref.refs_2_, f32[1024,512]{1,0:T(8,128)} %get-tuple-element.70.refs_2_), custom_call_target="tpu_custom_call" | custom-call | flops 16106127360 | bytes 20971520 | tf_op jit(solution)/shard_map/pallas_call | solution.py:273
  498.0 1.8 collective-permute-start.34
  499.8 12.7 %shard_map.56 = (f32[256,1280]{1,0:T(8,128)}, f32[256,1280]{1,0:T(8,128)}) custom-call(s32[1]{0:T(128)} %bitcast.core_ref.refs_0_, f32[3072,2048]{1,0:T(8,128)} %shard_map.47.trail_ref.refs_1_, f32[2560,1024]{1,0:T(8,128)} %get-tuple-element.66.refs_1_.l_ref.refs_2_, f32[1024,1024]{1,0:T(8,128)} %get-tuple-element.75.mine_ref.refs_3_, ...), custom_call_target="tpu_custom_call" | custom-call | flops 6442450944 | bytes 12582912 | tf_op jit(solution)/shard_map/pallas_call | solution.py:302
  512.5 1.5 collective-permute-start.40
  514.6 73.4 %shard_map.53.trail_ref.refs_1_ = f32[3072,2048]{1,0:T(8,128)} custom-call(s32[1]{0:T(128)} %bitcast.core_ref.refs_0_, f32[3072,2048]{1,0:T(8,128)} %shard_map.47.trail_ref.refs_1_, f32[2560,1024]{1,0:T(8,128)} %get-tuple-element.66.refs_1_.l_ref.refs_2_, f32[1024,1024]{1,0:T(8,128)} %get-tuple-element.75.mine_ref.refs_3_, ...), custom_call_target="tpu_custom_call", output_to_operand_aliasing={{}: (1, {})} | custom-call | flops 64424509440 | bytes 41943040 | tf_op jit(solution)/shard_map/pallas_call | solution.py:350
  592.0 34.3 %shard_map.54 = (f32[1024,1024]{1,0:T(8,128)}, f32[256,256]{1,0:T(8,128)}, f32[256,256]{1,0:T(8,128)}) custom-call(f32[16,256,256]{2,1,0:T(8,128)} %bitcast.41), custom_call_target="tpu_custom_call" | custom-call | flops 30000001024 | bytes 16777216 | tf_op jit(solution)/shard_map/pallas_call | solution.py:144
  626.3 16.7 %shard_map.57 = (f32[1024,1024]{1,0:T(8,128)}, f32[1024,256]{1,0:T(8,128)}) custom-call(f32[256,1280]{1,0:T(8,128)} %get-tuple-element.83.refs_0_, f32[256,1280]{1,0:T(8,128)} %collective-permute-done.38.refs_1_, f32[256,1280]{1,0:T(8,128)} %collective-permute-done.39.refs_2_, f32[256,1280]{1,0:T(8,128)} %collective-permute-done.40.refs_3_, ...), custom_call_target="tpu_custom_call" | custom-call | flops 10066329600 | bytes 15728640 | tf_op jit(solution)/shard_map/pallas_call | solution.py:238
  644.0 25.5 %shard_map.55 = (f32[2304,1024]{1,0:T(8,128)}, f32[2304,256]{1,0:T(8,128)}) custom-call(f32[2304,256]{1,0:T(8,128)} %get-tuple-element.72.own, f32[2304,256]{1,0:T(8,128)} %collective-permute-done.33.y, f32[2304,256]{1,0:T(8,128)} %copy-done.4, f32[1152,256]{1,0:T(8,128)} %collective-permute-done.36.top, f32[1152,256]{1,0:T(8,128)} %copy-done.8, ...), custom_call_target="tpu_custom_call" | custom-call | flops 18119393280 | bytes 28311552 | tf_op jit(solution)/shard_map/pallas_call | solution.py:205
  669.5 14.0 %shard_map.58 = (f32[256,256]{1,0:T(8,128)}, f32[2048,256]{1,0:T(8,128)}) custom-call(f32[2304,256]{1,0:T(8,128)} %get-tuple-element.71.refs_0_, f32[2304,1024]{1,0:T(8,128)} %get-tuple-element.81.refs_1_.l_ref.refs_2_, f32[1024,256]{1,0:T(8,128)} %get-tuple-element.85.refs_2_), custom_call_target="tpu_custom_call" | custom-call | flops 7247757312 | bytes 14155776 | tf_op jit(solution)/shard_map/pallas_call | solution.py:273
  684.7 1.7 collective-permute-start.42
  686.5 12.6 %shard_map.62 = (f32[256,1024]{1,0:T(8,128)}, f32[256,1024]{1,0:T(8,128)}) custom-call(s32[1]{0:T(128)} %bitcast.core_ref.refs_0_, f32[3072,2048]{1,0:T(8,128)} %shard_map.53.trail_ref.refs_1_, f32[2304,1024]{1,0:T(8,128)} %get-tuple-element.81.refs_1_.l_ref.refs_2_, f32[1024,1024]{1,0:T(8,128)} %get-tuple-element.89.mine_ref.refs_3_, ...), custom_call_target="tpu_custom_call" | custom-call | flops 6442450944 | bytes 12582912 | tf_op jit(solution)/shard_map/pallas_call | solution.py:302
  701.2 66.2 %shard_map.59.trail_ref = f32[3072,2048]{1,0:T(8,128)} custom-call(s32[1]{0:T(128)} %bitcast.core_ref.refs_0_, f32[3072,2048]{1,0:T(8,128)} %shard_map.53.trail_ref.refs_1_, f32[2304,1024]{1,0:T(8,128)} %get-tuple-element.81.refs_1_.l_ref.refs_2_, f32[1024,1024]{1,0:T(8,128)} %get-tuple-element.89.mine_ref.refs_3_, ...), custom_call_target="tpu_custom_call", output_to_operand_aliasing={{}: (1, {})} | custom-call | flops 57982058496 | bytes 37748736 | tf_op jit(solution)/shard_map/pallas_call | solution.py:350
  767.5 34.7 %shard_map.60 = (f32[1024,1024]{1,0:T(8,128)}, f32[256,256]{1,0:T(8,128)}, f32[256,256]{1,0:T(8,128)}) custom-call(f32[16,256,256]{2,1,0:T(8,128)} %bitcast.43), custom_call_target="tpu_custom_call" | custom-call | flops 30000001024 | bytes 16777216 | tf_op jit(solution)/shard_map/pallas_call | solution.py:144
  803.2 13.8 %shard_map.63.mine_ref = f32[1024,1024]{1,0:T(8,128)} custom-call(f32[256,1024]{1,0:T(8,128)} %get-tuple-element.97.refs_0_, f32[256,1024]{1,0:T(8,128)} %copy-done.10, f32[256,1024]{1,0:T(8,128)} %collective-permute-done.47.refs_2_, f32[256,1024]{1,0:T(8,128)} %collective-permute-done.48.refs_3_, f32[1024,1024]{1,0:T(8,128)} %get-tuple-element.95.x_ref.refs_4_), custom_call_target="tpu_custom_call" | custom-call | flops 8053063680 | bytes 12582912 | tf_op jit(solution)/shard_map/pallas_call | solution.py:238
  819.5 24.3 %collective-permute-done.44.top = f32[1024,256]{1,0:T(8,128)S(1)} collective-permute-done((f32[1024,256]{1,0:T(8,128)S(1)}, f32[1024,256]{1,0:T(8,128)S(1)}, u32[]{:S(2)}, u32[]{:S(2)}) %collective-permute-start.44) | collective-permute-done | bytes 1048608 | tf_op jit(solution)/shard_map/ppermute | solution.py:409
  845.9 23.1 %shard_map.61 = (f32[2048,1024]{1,0:T(8,128)}, f32[2048,256]{1,0:T(8,128)}) custom-call(f32[2048,256]{1,0:T(8,128)} %get-tuple-element.87.own, f32[2048,256]{1,0:T(8,128)} %copy-done.5, f32[2048,256]{1,0:T(8,128)} %collective-permute-done.42.z, f32[1024,256]{1,0:T(8,128)} %copy-done.11, f32[1024,256]{1,0:T(8,128)} %copy-done.12, ...), custom_call_target="tpu_custom_call" | custom-call | flops 16106127360 | bytes 25165824 | tf_op jit(solution)/shard_map/pallas_call | solution.py:205
  868.9 73.9 %shard_map.64 = (f32[3072,2048]{1,0:T(8,128)}, f32[24576,128]{1,0:T(8,128)}) custom-call(s32[1]{0:T(128)} %bitcast.core_ref.refs_0_, f32[3072,2048]{1,0:T(8,128)} %shard_map.59.trail_ref, f32[2048,1024]{1,0:T(8,128)} %get-tuple-element.96.l_ref, f32[1024,1024]{1,0:T(8,128)} %shard_map.63.mine_ref, ...), custom_call_target="tpu_custom_call", output_to_operand_aliasing={{0}: (1, {})} | custom-call | flops 57982058496 | bytes 37748736 | tf_op jit(solution)/shard_map/pallas_call | solution.py:350
  (141 shorter events, 31.1 us)
Async XLA Ops:
  7.2 380.1 %all-gather.7.cloned.1.call-start = ((), (), s32[]{:S(2)}) async-start(), calls=%async_computation | async-start | bytes 4456448 | tf_op jit(solution)/shard_map/all_gather | solution.py:399
  13.9 108.1 %collective-permute-start.1 = (f32[2816,256]{1,0:T(8,128)S(1)}, f32[2816,256]{1,0:T(8,128)}, u32[]{:S(2)}, u32[]{:S(2)}) collective-permute-start(f32[2816,256]{1,0:T(8,128)S(1)} %bitcast.28), channel_id=1, source_target_pairs={{0,8},{8,0},{4,12},{12,4},{1,9},{9,1},{5,13},{13,5},{2,10},{10,2},... | collective-permute-start | bytes 8650760 | tf_op jit(solution)/shard_map/ppermute | solution.py:401
  17.2 104.8 %collective-permute-start = (f32[2816,256]{1,0:T(8,128)S(1)}, f32[2816,256]{1,0:T(8,128)}, u32[]{:S(2)}, u32[]{:S(2)}) collective-permute-start(f32[2816,256]{1,0:T(8,128)S(1)} %bitcast.29), channel_id=1, source_target_pairs={{0,4},{4,0},{8,12},{12,8},{1,5},{5,1},{9,13},{13,9},{2,6},{6,2},{1... | collective-permute-start | bytes 8650760 | tf_op jit(solution)/shard_map/ppermute | solution.py:400
  23.2 10.1 %collective-permute-start.9 = (f32[256,256]{1,0:T(8,128)S(1)}, f32[256,256]{1,0:T(8,128)S(1)}, u32[]{:S(2)}, u32[]{:S(2)}) collective-permute-start(f32[256,256]{1,0:T(8,128)S(1)} %bitcast.32), channel_id=1, source_target_pairs={{0,6},{1,7},{2,4},{3,5},{4,2},{5,3},{6,0},{7,1},{8,14},{9,15},{10,... | collective-permute-start | bytes 786440 | tf_op jit(solution)/shard_map/ppermute | solution.py:368
  24.7 72.0 %collective-permute-start.11 = (f32[256,256]{1,0:T(8,128)S(1)}, f32[256,256]{1,0:T(8,128)}, u32[]{:S(2)}, u32[]{:S(2)}) collective-permute-start(f32[256,256]{1,0:T(8,128)S(1)} %bitcast.33), channel_id=1, source_target_pairs={{0,8},{1,9},{2,10},{3,11},{4,12},{5,13},{6,14},{7,15},{8,0},{9,1},... | collective-permute-start | bytes 786440 | tf_op jit(solution)/shard_map/ppermute | solution.py:368
  25.2 75.1 %collective-permute-start.13 = (f32[256,256]{1,0:T(8,128)S(1)}, f32[256,256]{1,0:T(8,128)}, u32[]{:S(2)}, u32[]{:S(2)}) collective-permute-start(f32[256,256]{1,0:T(8,128)S(1)} %bitcast.34), channel_id=1, source_target_pairs={{0,10},{1,11},{2,8},{3,9},{4,14},{5,15},{6,12},{7,13},{8,2},{9,3},... | collective-permute-start | bytes 786440 | tf_op jit(solution)/shard_map/ppermute | solution.py:368
  33.3 67.5 %collective-permute-start.15 = (f32[256,256]{1,0:T(8,128)S(1)}, f32[256,256]{1,0:T(8,128)}, u32[]{:S(2)}, u32[]{:S(2)}) collective-permute-start(f32[256,256]{1,0:T(8,128)S(1)} %bitcast.35), channel_id=1, source_target_pairs={{0,12},{1,13},{2,14},{3,15},{4,8},{5,9},{6,10},{7,11},{8,4},{9,5},... | collective-permute-start | bytes 786440 | tf_op jit(solution)/shard_map/ppermute | solution.py:368
  96.7 11.0 %collective-permute-start.17 = (f32[256,256]{1,0:T(8,128)S(1)}, f32[256,256]{1,0:T(8,128)S(1)}, u32[]{:S(2)}, u32[]{:S(2)}) collective-permute-start(f32[256,256]{1,0:T(8,128)S(1)} %bitcast.36), channel_id=1, source_target_pairs={{0,14},{1,15},{2,12},{3,13},{4,10},{5,11},{6,8},{7,9},{8,6},{9,7},... | collective-permute-start | bytes 786440 | tf_op jit(solution)/shard_map/ppermute | solution.py:368
  100.3 11.5 %collective-permute-start.5 = (f32[256,256]{1,0:T(8,128)S(1)}, f32[256,256]{1,0:T(8,128)}, u32[]{:S(2)}, u32[]{:S(2)}) collective-permute-start(f32[256,256]{1,0:T(8,128)S(1)} %bitcast.37), channel_id=1, source_target_pairs={{0,2},{1,3},{2,0},{3,1},{4,6},{5,7},{6,4},{7,5},{8,10},{9,11},{10,... | collective-permute-start | bytes 786440 | tf_op jit(solution)/shard_map/ppermute | solution.py:368
  100.8 10.9 %collective-permute-start.7 = (f32[256,256]{1,0:T(8,128)S(1)}, f32[256,256]{1,0:T(8,128)}, u32[]{:S(2)}, u32[]{:S(2)}) collective-permute-start(f32[256,256]{1,0:T(8,128)S(1)} %bitcast.38), channel_id=1, source_target_pairs={{0,4},{1,5},{2,6},{3,7},{4,0},{5,1},{6,2},{7,3},{8,12},{9,13},{10,... | collective-permute-start | bytes 786440 | tf_op jit(solution)/shard_map/ppermute | solution.py:368
  113.3 5.6 collective-permute-start.16
  117.3 43.3 %collective-permute-start.24 = (f32[256,1024]{1,0:T(8,128)}, f32[256,1024]{1,0:T(8,128)}, u32[]{:S(2)}, u32[]{:S(2)}) collective-permute-start(f32[256,1024]{1,0:T(8,128)} %get-tuple-element.110), channel_id=1, source_target_pairs={{0,1},{1,0},{2,3},{3,2},{4,5},{5,4},{6,7},{7,6},{8,9},{9,8},{10,11... | collective-permute-start | bytes 3145736 | tf_op jit(solution)/shard_map/ppermute | solution.py:376
  117.4 43.7 %collective-permute-start.25 = (f32[256,1024]{1,0:T(8,128)}, f32[256,1024]{1,0:T(8,128)}, u32[]{:S(2)}, u32[]{:S(2)}) collective-permute-start(f32[256,1024]{1,0:T(8,128)} %get-tuple-element.111.refs_0_), channel_id=1, source_target_pairs={{0,2},{2,0},{1,3},{3,1},{4,6},{6,4},{5,7},{7,5},{8,10},{10,8},{9,1... | collective-permute-start | bytes 3145736 | tf_op jit(solution)/shard_map/ppermute | solution.py:376
  120.5 40.1 %collective-permute-start.20 = (f32[256,768]{1,0:T(8,128)}, f32[256,768]{1,0:T(8,128)}, u32[]{:S(2)}, u32[]{:S(2)}) collective-permute-start(f32[256,768]{1,0:T(8,128)} %pad_maximum_fusion.refs_0_), channel_id=1, source_target_pairs={{0,2},{2,0},{1,3},{3,1},{4,6},{6,4},{5,7},{7,5},{8,10},{10,8},{9,1... | collective-permute-start | bytes 2359304 | tf_op jit(solution)/shard_map/ppermute | solution.py:380
  122.0 16.2 %collective-permute-start.6 = (f32[256,256]{1,0:T(8,128)}, f32[256,256]{1,0:T(8,128)S(1)}, u32[]{:S(2)}, u32[]{:S(2)}) collective-permute-start(f32[256,256]{1,0:T(8,128)} %collective-permute-done.5.refs_2_), channel_id=1, source_target_pairs={{0,1},{1,0},{2,3},{3,2},{4,5},{5,4},{6,7},{7,6},{8,9},{9,8},{10,11... | collective-permute-start | bytes 786440 | tf_op jit(solution)/shard_map/ppermute | solution.py:371
  122.1 16.9 %collective-permute-start.8 = (f32[256,256]{1,0:T(8,128)}, f32[256,256]{1,0:T(8,128)}, u32[]{:S(2)}, u32[]{:S(2)}) collective-permute-start(f32[256,256]{1,0:T(8,128)} %collective-permute-done.7.refs_4_), channel_id=1, source_target_pairs={{0,1},{1,0},{2,3},{3,2},{4,5},{5,4},{6,7},{7,6},{8,9},{9,8},{10,11... | collective-permute-start | bytes 786440 | tf_op jit(solution)/shard_map/ppermute | solution.py:371
  138.2 72.5 %collective-permute-start.19 = (f32[256,768]{1,0:T(8,128)}, f32[256,768]{1,0:T(8,128)}, u32[]{:S(2)}, u32[]{:S(2)}) collective-permute-start(f32[256,768]{1,0:T(8,128)} %pad_maximum_fusion.refs_0_), channel_id=1, source_target_pairs={{0,1},{1,0},{2,3},{3,2},{4,5},{5,4},{6,7},{7,6},{8,9},{9,8},{10,11... | collective-permute-start | bytes 2359304 | tf_op jit(solution)/shard_map/ppermute | solution.py:381
  138.9 57.0 %collective-permute-start.26 = (f32[256,1024]{1,0:T(8,128)}, f32[256,1024]{1,0:T(8,128)S(1)}, u32[]{:S(2)}, u32[]{:S(2)}) collective-permute-start(f32[256,1024]{1,0:T(8,128)} %get-tuple-element.110), channel_id=1, source_target_pairs={{0,3},{3,0},{1,2},{2,1},{4,7},{7,4},{5,6},{6,5},{8,11},{11,8},{9,1... | collective-permute-start | bytes 3145736 | tf_op jit(solution)/shard_map/ppermute | solution.py:376
  160.6 50.1 %collective-permute-start.21 = (f32[256,768]{1,0:T(8,128)}, f32[256,768]{1,0:T(8,128)}, u32[]{:S(2)}, u32[]{:S(2)}) collective-permute-start(f32[256,768]{1,0:T(8,128)} %collective-permute-done.20.refs_2_), channel_id=1, source_target_pairs={{0,1},{1,0},{2,3},{3,2},{4,5},{5,4},{6,7},{7,6},{8,9},{9,8},{10,11... | collective-permute-start | bytes 2359304 | tf_op jit(solution)/shard_map/ppermute | solution.py:381
  160.6 61.4 %collective-permute-start.2 = (f32[1408,256]{1,0:T(8,128)S(1)}, f32[1408,256]{1,0:T(8,128)}, u32[]{:S(2)}, u32[]{:S(2)}) collective-permute-start(f32[1408,256]{1,0:T(8,128)S(1)} %slice.52), channel_id=1, source_target_pairs={{0,4},{4,0},{8,12},{12,8},{1,5},{5,1},{9,13},{13,9},{2,6},{6,2},{1... | collective-permute-start | bytes 4325384 | tf_op jit(solution)/shard_map/ppermute | solution.py:409
  161.2 60.9 %collective-permute-start.3 = (f32[1408,256]{1,0:T(8,128)S(1)}, f32[1408,256]{1,0:T(8,128)}, u32[]{:S(2)}, u32[]{:S(2)}) collective-permute-start(f32[1408,256]{1,0:T(8,128)S(1)} %slice.53), channel_id=1, source_target_pairs={{0,8},{8,0},{4,12},{12,4},{1,9},{9,1},{5,13},{13,5},{2,10},{10,2},... | collective-permute-start | bytes 4325384 | tf_op jit(solution)/shard_map/ppermute | solution.py:410
  210.7 80.4 %collective-permute-start.27 = (f32[1024,1024]{1,0:T(8,128)}, f32[1024,1024]{1,0:T(8,128)}, u32[]{:S(2)}, u32[]{:S(2)}) collective-permute-start(f32[1024,1024]{1,0:T(8,128)} %shard_map.46.mine_ref.refs_3_), channel_id=1, source_target_pairs={{0,1},{1,0},{2,3},{3,2},{4,5},{5,4},{6,7},{7,6},{8,9},{9,8},{10,11... | collective-permute-start | bytes 12582920 | tf_op jit(solution)/shard_map/ppermute | solution.py:415
  288.0 300.1 %all-gather.9.cloned.1.call-start = ((), (), s32[]{:S(2)}) async-start(), calls=%async_computation.1 | async-start | bytes 4456448 | tf_op jit(solution)/shard_map/all_gather | solution.py:399
  288.1 99.1 %collective-permute-start.22 = (f32[2560,256]{1,0:T(8,128)}, f32[2560,256]{1,0:T(8,128)}, u32[]{:S(2)}, u32[]{:S(2)}) collective-permute-start(f32[2560,256]{1,0:T(8,128)} %get-tuple-element.59.own), channel_id=1, source_target_pairs={{0,4},{4,0},{8,12},{12,8},{1,5},{5,1},{9,13},{13,9},{2,6},{6,2},{1... | collective-permute-start | bytes 7864328 | tf_op jit(solution)/shard_map/ppermute | solution.py:400
  289.5 97.7 %collective-permute-start.23 = (f32[2560,256]{1,0:T(8,128)}, f32[2560,256]{1,0:T(8,128)S(1)}, u32[]{:S(2)}, u32[]{:S(2)}) collective-permute-start(f32[2560,256]{1,0:T(8,128)} %get-tuple-element.59.own), channel_id=1, source_target_pairs={{0,8},{8,0},{4,12},{12,4},{1,9},{9,1},{5,13},{13,5},{2,10},{10,2},... | collective-permute-start | bytes 7864328 | tf_op jit(solution)/shard_map/ppermute | solution.py:401
  304.6 120.8 %collective-permute-start.30 = (f32[256,1536]{1,0:T(8,128)}, f32[256,1536]{1,0:T(8,128)}, u32[]{:S(2)}, u32[]{:S(2)}) collective-permute-start(f32[256,1536]{1,0:T(8,128)} %get-tuple-element.69), channel_id=1, source_target_pairs={{0,1},{1,0},{2,3},{3,2},{4,5},{5,4},{6,7},{7,6},{8,9},{9,8},{10,11... | collective-permute-start | bytes 4718600 | tf_op jit(solution)/shard_map/ppermute | solution.py:376
  304.6 120.9 %collective-permute-start.32 = (f32[256,1536]{1,0:T(8,128)}, f32[256,1536]{1,0:T(8,128)}, u32[]{:S(2)}, u32[]{:S(2)}) collective-permute-start(f32[256,1536]{1,0:T(8,128)} %get-tuple-element.69), channel_id=1, source_target_pairs={{0,3},{3,0},{1,2},{2,1},{4,7},{7,4},{5,6},{6,5},{8,11},{11,8},{9,1... | collective-permute-start | bytes 4718600 | tf_op jit(solution)/shard_map/ppermute | solution.py:376
  306.1 119.3 %collective-permute-start.31 = (f32[256,1536]{1,0:T(8,128)}, f32[256,1536]{1,0:T(8,128)}, u32[]{:S(2)}, u32[]{:S(2)}) collective-permute-start(f32[256,1536]{1,0:T(8,128)} %get-tuple-element.68.refs_0_), channel_id=1, source_target_pairs={{0,2},{2,0},{1,3},{3,1},{4,6},{6,4},{5,7},{7,5},{8,10},{10,8},{9,1... | collective-permute-start | bytes 4718600 | tf_op jit(solution)/shard_map/ppermute | solution.py:376
  388.8 55.9 %collective-permute-start.28 = (f32[1280,256]{1,0:T(8,128)S(1)}, f32[1280,256]{1,0:T(8,128)}, u32[]{:S(2)}, u32[]{:S(2)}) collective-permute-start(f32[1280,256]{1,0:T(8,128)S(1)} %slice.46), channel_id=1, source_target_pairs={{0,4},{4,0},{8,12},{12,8},{1,5},{5,1},{9,13},{13,9},{2,6},{6,2},{1... | collective-permute-start | bytes 3932168 | tf_op jit(solution)/shard_map/ppermute | solution.py:409
  390.5 54.2 %collective-permute-start.29 = (f32[1280,256]{1,0:T(8,128)S(1)}, f32[1280,256]{1,0:T(8,128)S(1)}, u32[]{:S(2)}, u32[]{:S(2)}) collective-permute-start(f32[1280,256]{1,0:T(8,128)S(1)} %slice.47), channel_id=1, source_target_pairs={{0,8},{8,0},{4,12},{12,4},{1,9},{9,1},{5,13},{13,5},{2,10},{10,2},... | collective-permute-start | bytes 3932168 | tf_op jit(solution)/shard_map/ppermute | solution.py:410
  444.7 55.1 %collective-permute-start.35 = (f32[1024,1024]{1,0:T(8,128)}, f32[1024,1024]{1,0:T(8,128)}, u32[]{:S(2)}, u32[]{:S(2)}) collective-permute-start(f32[1024,1024]{1,0:T(8,128)} %get-tuple-element.75.mine_ref.refs_3_), channel_id=1, source_target_pairs={{0,1},{1,0},{2,3},{3,2},{4,5},{5,4},{6,7},{7,6},{8,9},{9,8},{10,11... | collective-permute-start | bytes 12582920 | tf_op jit(solution)/shard_map/ppermute | solution.py:415
  496.7 270.8 %all-gather.11.cloned.1.call-start = ((), (), s32[]{:S(2)}) async-start(), calls=%async_computation.2 | async-start | bytes 4456448 | tf_op jit(solution)/shard_map/all_gather | solution.py:399
  496.7 91.4 %collective-permute-start.33 = (f32[2304,256]{1,0:T(8,128)}, f32[2304,256]{1,0:T(8,128)}, u32[]{:S(2)}, u32[]{:S(2)}) collective-permute-start(f32[2304,256]{1,0:T(8,128)} %get-tuple-element.72.own), channel_id=1, source_target_pairs={{0,4},{4,0},{8,12},{12,8},{1,5},{5,1},{9,13},{13,9},{2,6},{6,2},{1... | collective-permute-start | bytes 7077896 | tf_op jit(solution)/shard_map/ppermute | solution.py:400
  498.0 90.1 %collective-permute-start.34 = (f32[2304,256]{1,0:T(8,128)}, f32[2304,256]{1,0:T(8,128)S(1)}, u32[]{:S(2)}, u32[]{:S(2)}) collective-permute-start(f32[2304,256]{1,0:T(8,128)} %get-tuple-element.72.own), channel_id=1, source_target_pairs={{0,8},{8,0},{4,12},{12,4},{1,9},{9,1},{5,13},{13,5},{2,10},{10,2},... | collective-permute-start | bytes 7077896 | tf_op jit(solution)/shard_map/ppermute | solution.py:401
  512.5 113.7 %collective-permute-start.38 = (f32[256,1280]{1,0:T(8,128)}, f32[256,1280]{1,0:T(8,128)}, u32[]{:S(2)}, u32[]{:S(2)}) collective-permute-start(f32[256,1280]{1,0:T(8,128)} %get-tuple-element.84), channel_id=1, source_target_pairs={{0,1},{1,0},{2,3},{3,2},{4,5},{5,4},{6,7},{7,6},{8,9},{9,8},{10,11... | collective-permute-start | bytes 3932168 | tf_op jit(solution)/shard_map/ppermute | solution.py:376
  512.5 113.8 %collective-permute-start.40 = (f32[256,1280]{1,0:T(8,128)}, f32[256,1280]{1,0:T(8,128)}, u32[]{:S(2)}, u32[]{:S(2)}) collective-permute-start(f32[256,1280]{1,0:T(8,128)} %get-tuple-element.84), channel_id=1, source_target_pairs={{0,3},{3,0},{1,2},{2,1},{4,7},{7,4},{5,6},{6,5},{8,11},{11,8},{9,1... | collective-permute-start | bytes 3932168 | tf_op jit(solution)/shard_map/ppermute | solution.py:376
  514.0 112.3 %collective-permute-start.39 = (f32[256,1280]{1,0:T(8,128)}, f32[256,1280]{1,0:T(8,128)}, u32[]{:S(2)}, u32[]{:S(2)}) collective-permute-start(f32[256,1280]{1,0:T(8,128)} %get-tuple-element.83.refs_0_), channel_id=1, source_target_pairs={{0,2},{2,0},{1,3},{3,1},{4,6},{6,4},{5,7},{7,5},{8,10},{10,8},{9,1... | collective-permute-start | bytes 3932168 | tf_op jit(solution)/shard_map/ppermute | solution.py:376
  589.5 53.5 %collective-permute-start.36 = (f32[1152,256]{1,0:T(8,128)S(1)}, f32[1152,256]{1,0:T(8,128)}, u32[]{:S(2)}, u32[]{:S(2)}) collective-permute-start(f32[1152,256]{1,0:T(8,128)S(1)} %slice.48), channel_id=1, source_target_pairs={{0,4},{4,0},{8,12},{12,8},{1,5},{5,1},{9,13},{13,9},{2,6},{6,2},{1... | collective-permute-start | bytes 3538952 | tf_op jit(solution)/shard_map/ppermute | solution.py:409
  591.2 51.8 %collective-permute-start.37 = (f32[1152,256]{1,0:T(8,128)S(1)}, f32[1152,256]{1,0:T(8,128)S(1)}, u32[]{:S(2)}, u32[]{:S(2)}) collective-permute-start(f32[1152,256]{1,0:T(8,128)S(1)} %slice.49), channel_id=1, source_target_pairs={{0,8},{8,0},{4,12},{12,4},{1,9},{9,1},{5,13},{13,5},{2,10},{10,2},... | collective-permute-start | bytes 3538952 | tf_op jit(solution)/shard_map/ppermute | solution.py:410
  643.0 43.5 %collective-permute-start.43 = (f32[1024,1024]{1,0:T(8,128)}, f32[1024,1024]{1,0:T(8,128)}, u32[]{:S(2)}, u32[]{:S(2)}) collective-permute-start(f32[1024,1024]{1,0:T(8,128)} %get-tuple-element.89.mine_ref.refs_3_), channel_id=1, source_target_pairs={{0,1},{1,0},{2,3},{3,2},{4,5},{5,4},{6,7},{7,6},{8,9},{9,8},{10,11... | collective-permute-start | bytes 12582920 | tf_op jit(solution)/shard_map/ppermute | solution.py:415
  683.4 84.0 %collective-permute-start.41 = (f32[2048,256]{1,0:T(8,128)}, f32[2048,256]{1,0:T(8,128)S(1)}, u32[]{:S(2)}, u32[]{:S(2)}) collective-permute-start(f32[2048,256]{1,0:T(8,128)} %get-tuple-element.87.own), channel_id=1, source_target_pairs={{0,4},{4,0},{8,12},{12,8},{1,5},{5,1},{9,13},{13,9},{2,6},{6,2},{1... | collective-permute-start | bytes 6291464 | tf_op jit(solution)/shard_map/ppermute | solution.py:400
  684.7 82.7 %collective-permute-start.42 = (f32[2048,256]{1,0:T(8,128)}, f32[2048,256]{1,0:T(8,128)}, u32[]{:S(2)}, u32[]{:S(2)}) collective-permute-start(f32[2048,256]{1,0:T(8,128)} %get-tuple-element.87.own), channel_id=1, source_target_pairs={{0,8},{8,0},{4,12},{12,4},{1,9},{9,1},{5,13},{13,5},{2,10},{10,2},... | collective-permute-start | bytes 6291464 | tf_op jit(solution)/shard_map/ppermute | solution.py:401
  699.0 103.1 %collective-permute-start.46 = (f32[256,1024]{1,0:T(8,128)}, f32[256,1024]{1,0:T(8,128)S(1)}, u32[]{:S(2)}, u32[]{:S(2)}) collective-permute-start(f32[256,1024]{1,0:T(8,128)} %get-tuple-element.98), channel_id=1, source_target_pairs={{0,1},{1,0},{2,3},{3,2},{4,5},{5,4},{6,7},{7,6},{8,9},{9,8},{10,11... | collective-permute-start | bytes 3145736 | tf_op jit(solution)/shard_map/ppermute | solution.py:376
  699.0 103.2 %collective-permute-start.48 = (f32[256,1024]{1,0:T(8,128)}, f32[256,1024]{1,0:T(8,128)}, u32[]{:S(2)}, u32[]{:S(2)}) collective-permute-start(f32[256,1024]{1,0:T(8,128)} %get-tuple-element.98), channel_id=1, source_target_pairs={{0,3},{3,0},{1,2},{2,1},{4,7},{7,4},{5,6},{6,5},{8,11},{11,8},{9,1... | collective-permute-start | bytes 3145736 | tf_op jit(solution)/shard_map/ppermute | solution.py:376
  700.5 101.7 %collective-permute-start.47 = (f32[256,1024]{1,0:T(8,128)}, f32[256,1024]{1,0:T(8,128)}, u32[]{:S(2)}, u32[]{:S(2)}) collective-permute-start(f32[256,1024]{1,0:T(8,128)} %get-tuple-element.97.refs_0_), channel_id=1, source_target_pairs={{0,2},{2,0},{1,3},{3,1},{4,6},{6,4},{5,7},{7,5},{8,10},{10,8},{9,1... | collective-permute-start | bytes 3145736 | tf_op jit(solution)/shard_map/ppermute | solution.py:376
  816.9 52.0 %collective-permute-start.49 = (f32[1024,1024]{1,0:T(8,128)}, f32[1024,1024]{1,0:T(8,128)}, u32[]{:S(2)}, u32[]{:S(2)}) collective-permute-start(f32[1024,1024]{1,0:T(8,128)} %shard_map.63.mine_ref), channel_id=1, source_target_pairs={{0,1},{1,0},{2,3},{3,2},{4,5},{5,4},{6,7},{7,6},{8,9},{9,8},{10,11... | collective-permute-start | bytes 12582920 | tf_op jit(solution)/shard_map/ppermute | solution.py:415
  818.2 25.6 %collective-permute-start.44 = (f32[1024,256]{1,0:T(8,128)S(1)}, f32[1024,256]{1,0:T(8,128)S(1)}, u32[]{:S(2)}, u32[]{:S(2)}) collective-permute-start(f32[1024,256]{1,0:T(8,128)S(1)} %slice.50), channel_id=1, source_target_pairs={{0,4},{4,0},{8,12},{12,8},{1,5},{5,1},{9,13},{13,9},{2,6},{6,2},{1... | collective-permute-start | bytes 3145736 | tf_op jit(solution)/shard_map/ppermute | solution.py:409
  818.8 25.3 %collective-permute-start.45 = (f32[1024,256]{1,0:T(8,128)S(1)}, f32[1024,256]{1,0:T(8,128)S(1)}, u32[]{:S(2)}, u32[]{:S(2)}) collective-permute-start(f32[1024,256]{1,0:T(8,128)S(1)} %slice.51), channel_id=1, source_target_pairs={{0,8},{8,0},{4,12},{12,4},{1,9},{9,1},{5,13},{13,5},{2,10},{10,2},... | collective-permute-start | bytes 3145736 | tf_op jit(solution)/shard_map/ppermute | solution.py:410
  (25 other events, 371.8 us)
Sparse Core Ops, SparseCore 0:
  288.1 49.9 all-gather.6
  496.8 49.9 all-gather.8
  683.6 49.8 all-gather.10

commit v2 on v1

--- a/solution.py
+++ b/solution.py
@@ -13,7 +13,7 @@
 HIGH = lax.Precision.HIGHEST
 NB = 256
 SUP = 1024
-VMEM_LIMIT = 60 * 1024 * 1024
+MIB = 1024 * 1024
 
 
 def dot(a, b):
@@ -35,7 +35,7 @@
     return high, mid, (rest - mid.astype(F32)).astype(BF16)
 
 
-def panel32(work, p):
+def panel32(work, p, filler=lambda k: None):
     r0 = 32 * p
     diag_tile = p // 4
     lane0 = r0 % 128
@@ -54,6 +54,8 @@
         for sg in range(u // 8, 4):
             col[u, sg] = over_lanes(u, sg)
     for g in range(4):
+        if g < 3:
+            filler(g)
         for t in range(8 * g, 8 * g + 8):
             tt = t - 8 * g
             rs = lax.rsqrt(over_sublanes(col[t, g], tt))
@@ -78,78 +80,178 @@
         for sg in range(4):
             work[r0 + 8 * sg:r0 + 8 * sg + 8, 128 * ti:128 * ti + 128] = rows[ti][sg]
     if p == 7:
+        filler(3)
         return
     high, mid, low = split3(jnp.concatenate([jnp.concatenate(rows[ti], axis=0) for ti in tiles], axis=1))
     first = (r0 + 32 - 128 * diag_tile) // 128 * 128
     rhs = jnp.concatenate([high, mid, high, mid, low, high], axis=0)
     lhs = jnp.concatenate([high, high, mid, mid, high, low], axis=0)[:, first:256 - 128 * diag_tile]
     upd = lax.dot_general(lhs, rhs, (((0,), (0,)), ((), ())), preferred_element_type=F32)
+    filler(3)
     skip = r0 + 32 - first - 128 * diag_tile
     for j, ti in enumerate(tiles):
         lanes = slice(128 * ti, 128 * ti + 128)
         work[r0 + 32:256, lanes] = work[r0 + 32:256, lanes] - upd[skip:, 128 * j:128 * j + 128]
 
 
+def spread_factor(b, u_ref, x_ref, work):
+    row = lax.broadcasted_iota(jnp.int32, (NB, NB), 0)
+    col = lax.broadcasted_iota(jnp.int32, (NB, NB), 1)
+    a, e = NB * b, NB * b + NB
+    xbb = jnp.where(col <= row, work[:, NB:], 0.0)
+    u_ref[a:e, a:e] = jnp.where(col >= row, work[:, :NB], 0.0)
+    if b > 0:
+        x_ref[a:e, :a] = dot(xbb, x_ref[a:e, :a])
+        u_ref[a:e, :a] = jnp.zeros((NB, a), F32)
+    x_ref[a:e, a:e] = xbb
+    if b < 3:
+        urow = dot(xbb, u_ref[a:e, e:])
+        u_ref[a:e, e:] = urow
+        for c in range(b + 1, 4):
+            lo = NB * c
+            uc = urow[:, lo - e:lo - e + NB]
+            u_ref[lo:lo + NB, lo:] = u_ref[lo:lo + NB, lo:] - dot_tn(uc, urow[:, lo - e:])
+            x_ref[lo:lo + NB, :e] = x_ref[lo:lo + NB, :e] - dot_tn(uc, x_ref[a:e, :e])
+
+
+def factor_block(b, u_ref, x_ref, own_l_ref, own_diag_ref, work, filler=lambda p, k: None):
+    row = lax.broadcasted_iota(jnp.int32, (NB, NB), 0)
+    col = lax.broadcasted_iota(jnp.int32, (NB, NB), 1)
+    at = pl.ds(pl.multiple_of(b * NB, NB), NB)
+    work[:, :NB] = u_ref[at, at]
+    work[:, NB:] = jnp.where(row == col, 1.0, 0.0)
+    for p in range(8):
+        panel32(work, p, functools.partial(filler, p))
+    for n in range(4):
+        pl.when(b == n)(lambda n=n: spread_factor(n, u_ref, x_ref, work))
+
+    @pl.when(b == 3)
+    def _():
+        at_row, at_col = (pl.ds(pl.multiple_of(lax.axis_index(name) * NB, NB), NB) for name in ("pr", "pc"))
+        own_l_ref[...] = u_ref[at_col, at_row].T
+        own_diag_ref[...] = u_ref[at_row, at_row]
+
+
 def factor_kernel(*refs):
     blocks, (x_ref, own_l_ref, own_diag_ref, u_ref, work) = refs[:-5], refs[-5:]
     my_col, my_row = lax.axis_index("pc"), lax.axis_index("pr")
-    row = lax.broadcasted_iota(jnp.int32, (NB, NB), 0)
-    col = lax.broadcasted_iota(jnp.int32, (NB, NB), 1)
-    for c in range(4):
-        for r in range(4):
-            if len(blocks) == 1:
-                u_ref[NB * r:NB * r + NB, NB * c:NB * c + NB] = blocks[0][4 * c + r]
-            else:
+    b = pl.program_id(0)
+
+    @pl.when(b == 0)
+    def _():
+        for c in range(4):
+            for r in range(4):
                 at_row, at_col = (pl.ds(pl.multiple_of(v * NB, NB), NB) for v in (my_row ^ r, my_col ^ c))
-                u_ref[at_row, at_col] = blocks[4 * c + r][...]
-    x_ref[...] = jnp.zeros_like(x_ref)
-    for b in range(4):
-        a, e = NB * b, NB * b + NB
-        work[:, :NB] = u_ref[a:e, a:e]
-        work[:, NB:] = jnp.where(row == col, 1.0, 0.0)
-        for p in range(8):
-            panel32(work, p)
-        ubb = jnp.where(col >= row, work[:, :NB], 0.0)
-        xbb = jnp.where(col <= row, work[:, NB:], 0.0)
-        u_ref[a:e, a:e] = ubb
-        if b > 0:
-            x_ref[a:e, :a] = dot(xbb, x_ref[a:e, :a])
-            u_ref[a:e, :a] = jnp.zeros((NB, a), F32)
-        x_ref[a:e, a:e] = xbb
-        if b < 3:
-            urow = dot(xbb, u_ref[a:e, e:])
-            u_ref[a:e, e:] = urow
-            for c in range(b + 1, 4):
-                lo = NB * c
-                uc = urow[:, lo - e:lo - e + NB]
-                u_ref[lo:lo + NB, lo:] = u_ref[lo:lo + NB, lo:] - dot_tn(uc, urow[:, lo - e:])
-                x_ref[lo:lo + NB, :e] = x_ref[lo:lo + NB, :e] - dot_tn(uc, x_ref[a:e, :e])
-    at_row = pl.ds(pl.multiple_of(my_row * NB, NB), NB)
-    at_col = pl.ds(pl.multiple_of(my_col * NB, NB), NB)
-    own_l_ref[...] = u_ref[at_col, at_row].T
-    own_diag_ref[...] = u_ref[at_row, at_row]
-
-
-def call(kernel, flops, moved, **kw):
+                u_ref[at_row, at_col] = blocks[r % 2][c + 4 * (r // 2)]
+        x_ref[...] = jnp.zeros_like(x_ref)
+
+    factor_block(b, u_ref, x_ref, own_l_ref, own_diag_ref, work)
+
+
+def call(kernel, flops, moved, vmem, **kw):
     cost = pl.CostEstimate(flops=flops, bytes_accessed=moved, transcendentals=0)
-    return pl.pallas_call(kernel, cost_estimate=cost, compiler_params=pltpu.CompilerParams(vmem_limit_bytes=VMEM_LIMIT), **kw)
+    return pl.pallas_call(kernel, cost_estimate=cost, compiler_params=pltpu.CompilerParams(vmem_limit_bytes=vmem * MIB), **kw)
+
+
+def in_hbm(x):
+    return pltpu.with_memory_space_constraint(x, pltpu.HBM)
 
 
 def shape(*dims):
+    return pltpu.HBM(dims, F32)
+
+
+def near(*dims):
     return jax.ShapeDtypeStruct(dims, F32)
 
 
 def factor(blocks):
     vmem = pl.BlockSpec(memory_space=pltpu.VMEM)
     return call(
-        factor_kernel, 30_000_000_000, 1 << 24,
-        out_shape=(shape(SUP, SUP), shape(NB, NB), shape(NB, NB)), in_specs=[vmem] * len(blocks), out_specs=(vmem,) * 3,
+        factor_kernel, 30_000_000_000, 1 << 24, 20, grid=(4,),
+        out_shape=(near(SUP, SUP), shape(NB, NB), shape(NB, NB)), in_specs=[vmem] * len(blocks), out_specs=(vmem,) * 3,
         scratch_shapes=[pltpu.VMEM((SUP, SUP), F32), pltpu.VMEM((NB, 2 * NB), F32)],
     )(*blocks)
 
 
 def flat_panel(panel):
     return panel.reshape(-1, 4, 2, 128).transpose(0, 2, 1, 3).reshape(-1, 128)
+
+
+def dot_parts(a, b):
+    total = None
+    for i, j in ((2, 0), (0, 2), (1, 1), (1, 0), (0, 1), (0, 0)):
+        product = lax.dot_general(a(i), b(j), (((1,), (0,)), ((), ())), preferred_element_type=F32)
+        total = product if total is None else total + product
+    return total
+
+
+def fused_kernel(s_ref, trail_ref, l_ref, mine_ref, theirs_ref, *rest):
+    x_ref, own_l_ref, own_diag_ref, out_ref, u_ref, work, u_parts, l_parts, landing, block_sem, land_sem = rest[-11:]
+    b = pl.program_id(0)
+    my_row = lax.axis_index("pr")
+
+    def landing_copy(k, w):
+        at = pl.ds(128 * k, 128)
+        return pltpu.make_async_copy((mine_ref, theirs_ref)[w].at[at], landing.at[w, at], land_sem.at[2 * k + w])
+
+    def block_copy(n):
+        return pltpu.make_async_copy(s_ref.at[n], u_ref.at[pl.ds(n % 4 * NB, NB), pl.ds(n // 4 * NB, NB)], block_sem.at[n])
+
+    @pl.when(b == 0)
+    def _():
+        half = my_row % 2
+        for k in range(8):
+            for w in range(2):
+                landing_copy(k, w).start()
+        for n in range(16):
+            block_copy(n).start()
+        x_ref[...] = jnp.zeros_like(x_ref)
+        for k in range(8):
+            for w in range(2):
+                landing_copy(k, w).wait()
+
+                def split_rows(i, carry, k=k, w=w):
+                    at = pl.ds(pl.multiple_of(128 * k + 32 * i, 32), 32)
+                    for n, part in enumerate(split3(landing[w, at, :])):
+                        u_parts[n, at, pl.ds(pl.multiple_of((half ^ w) * SUP, SUP), SUP)] = part
+                    return carry
+
+                lax.fori_loop(0, 4, split_rows, 0)
+        for n in range(16):
+            block_copy(n).wait()
+
+    for n, part in enumerate(split3(l_ref[...])):
+        l_parts[n] = part
+
+    def piece(q, k):
+        deep, lanes = slice(NB * k, NB * k + NB), slice(NB * q, NB * q + NB)
+        total = dot_parts(lambda i: l_parts[i, :, deep], lambda j: u_parts[j, deep, lanes])
+        out_ref[:, lanes] = (trail_ref if k == 0 else out_ref)[:, lanes] - total
+
+    factor_block(b, u_ref, x_ref, own_l_ref, own_diag_ref, work, piece)
+
+
+def factor_beside(blocks, source, trail, l_rows, mine, theirs):
+    rows, cols = trail.shape
+    last = rows // NB - 4
+    ahead = l_rows.shape[0] // NB - 4
+    vmem = pl.BlockSpec(memory_space=pltpu.VMEM)
+    at = pl.BlockSpec((NB, cols), lambda b: (last + b, 0))
+    anywhere = pl.BlockSpec(memory_space=pl.ANY)
+    operands = [in_hbm(blocks), trail if source is None else source, in_hbm(l_rows), in_hbm(mine), in_hbm(theirs)]
+    specs = [anywhere, at, pl.BlockSpec((NB, SUP), lambda b: (ahead + b, 0)), anywhere, anywhere]
+    if source is not None:
+        operands.append(trail)
+        specs.append(anywhere)
+    scratch = [pltpu.VMEM((SUP, SUP), F32), pltpu.VMEM((NB, 2 * NB), F32), pltpu.VMEM((3, SUP, cols), BF16), pltpu.VMEM((3, NB, SUP), BF16),
+               pltpu.VMEM((2, SUP, SUP), F32), pltpu.SemaphoreType.DMA((16,)), pltpu.SemaphoreType.DMA((16,))]
+    return call(
+        fused_kernel, 100_000_000_000, 1 << 25, 48, grid=(4,),
+        out_shape=(near(SUP, SUP), shape(NB, NB), shape(NB, NB), shape(rows, cols)), in_specs=specs, out_specs=(vmem, vmem, vmem, at),
+        scratch_shapes=scratch,
+        input_output_aliases={1 if source is None else 5: 3},
+    )(*operands)
 
 
 def unpack_kernel(in_ref, rest_ref):
@@ -161,7 +263,7 @@
 def unpack(panel):
     rows = panel.shape[0] - NB
     return call(
-        unpack_kernel, 1_000_000, 8 * rows * SUP, grid=(rows // NB,), out_shape=shape(rows, 3 * NB),
+        unpack_kernel, 1_000_000, 8 * rows * SUP, 12, grid=(rows // NB,), out_shape=shape(rows, 3 * NB),
         in_specs=[pl.BlockSpec((8 * NB, 128), lambda i: (i + 1, 0))], out_specs=pl.BlockSpec((NB, 3 * NB), lambda i: (i, 0)),
     )(flat_panel(panel))
 
@@ -197,19 +299,19 @@
 
 
 def solve_rows(pieces, x):
-    own, _, _, _, _ = pieces
+    own, y, z, top, bottom = pieces
     rows = own.shape[0]
     tile = rows // 4
     split = 2
     block = pl.BlockSpec((tile, NB), lambda i: (i, 0))
     return call(
-        functools.partial(rows_kernel, split), 30 * rows * SUP * SUP // 4, 12 * rows * SUP, grid=(4,),
+        functools.partial(rows_kernel, split), 30 * rows * SUP * SUP // 4, 12 * rows * SUP, 34, grid=(4,),
         out_shape=(shape(rows, SUP), shape(rows, NB)),
         in_specs=[block, block, block, pl.BlockSpec((tile, NB), lambda i: (jnp.minimum(i, split - 1), 0)),
                   pl.BlockSpec((tile, NB), lambda i: (jnp.maximum(i - split, 0), 0)), pl.BlockSpec((SUP, SUP), lambda i: (0, 0))],
         out_specs=(pl.BlockSpec((tile, SUP), lambda i: (i, 0)), block),
         scratch_shapes=[pltpu.VMEM((tile, SUP), F32)],
-    )(*pieces, x)
+    )(in_hbm(own), y, z, top, bottom, x)
 
 
 def cols_kernel(*refs):
@@ -219,10 +321,11 @@
     for j in range(4):
         tall[pl.ds(pl.multiple_of((my_row ^ j) * NB, NB), NB), :] = pieces[j][...]
 
+    parts = [dot(x_ref[NB * k:NB * k + NB, :NB * k + NB], tall[:NB * k + NB, :]) for k in range(4)]
+
     def put(ref):
         for k in range(4):
-            e = NB * (k + 1)
-            ref[NB * k:e, :] = dot(x_ref[NB * k:e, :e], tall[:e, :])
+            ref[NB * k:NB * k + NB, :] = parts[k]
 
     if len(outs) == 1:
         put(outs[0])
@@ -233,10 +336,10 @@
 
 def solve_cols(pieces, x):
     cols = pieces[0].shape[1]
-    outs = [shape(SUP, min(SUP, cols))] + ([shape(SUP, cols - SUP)] if cols > SUP else [])
+    outs = [shape(SUP, min(SUP, cols))] + ([near(SUP, cols - SUP)] if cols > SUP else [])
     specs = [pl.BlockSpec((SUP, NB), lambda i: (0, jnp.minimum(i, min(SUP, cols) // NB - 1))), pl.BlockSpec((SUP, NB), lambda i: (0, jnp.maximum(i - 4, 0)))]
     return call(
-        cols_kernel, 30 * cols * SUP * SUP // 4, 12 * cols * SUP, grid=(cols // NB,), out_shape=outs,
+        cols_kernel, 30 * cols * SUP * SUP // 4, 12 * cols * SUP, 20, grid=(cols // NB,), out_shape=outs,
         in_specs=[pl.BlockSpec((NB, NB), lambda i: (0, i))] * 4 + [pl.BlockSpec((SUP, SUP), lambda i: (0, 0))],
         out_specs=specs[:len(outs)], scratch_shapes=[pltpu.VMEM((SUP, NB), F32)],
     )(*pieces, x)
@@ -271,74 +374,95 @@
     if keep:
         specs += [pl.BlockSpec((NB, keep), zero), pl.BlockSpec((NB, keep), below)]
     return call(
-        panel_kernel, 12 * rows * width * SUP, 8 * rows * width + 4 * rows * SUP, grid=(rows // NB,), out_shape=outs,
+        panel_kernel, 12 * rows * width * SUP, 8 * rows * width + 4 * rows * SUP, 20, grid=(rows // NB,), out_shape=outs,
         in_specs=[pl.BlockSpec((NB, width), lambda i: (i, 0)), pl.BlockSpec((NB, SUP), lambda i: (i, 0)), pl.BlockSpec((SUP, width), zero)],
         out_specs=specs,
-    )(rest, l_rows, u_panel)
+    )(in_hbm(rest), in_hbm(l_rows), u_panel)
 
 
 def row_kernel(*refs):
     trail_ref, l_ref, mine_ref, theirs_ref = refs[1:5]
-    keep_ref, send_ref = refs[-2:]
+    keep_ref, send_ref, landing, sem = refs[-4:]
     j = pl.program_id(0)
+    copies = [pltpu.make_async_copy(ref, landing.at[n], sem.at[n]) for n, ref in enumerate((mine_ref, theirs_ref))]
 
     @pl.when(j == 0)
     def _():
-        keep_ref[:, :SUP] = trail_ref[...] - dot(l_ref[...], mine_ref[...])
-        if len(refs) == 8:
+        for copy in copies:
+            copy.start()
+        if len(refs) == 10:
             keep_ref[:, SUP:] = refs[5][...]
             send_ref[:, SUP:] = refs[5][...]
 
+    for n, copy in enumerate(copies):
+        pl.when(j == n)(copy.wait)
+    new = trail_ref[...] - dot(l_ref[...], landing[j])
+
+    @pl.when(j == 0)
+    def _():
+        keep_ref[:, :SUP] = new
+
     @pl.when(j == 1)
     def _():
-        send_ref[:, :SUP] = trail_ref[...] - dot(l_ref[...], theirs_ref[...])
+        send_ref[:, :SUP] = new
 
 
 def update_row(core, trail, l_rows, mine, theirs, panel_row, step):
     extra = [] if panel_row is None else [panel_row]
     width = SUP + (0 if panel_row is None else panel_row.shape[1])
-    whole = lambda a: pl.BlockSpec(a.shape, lambda j, h: (0, 0))
     out = pl.BlockSpec((NB, width), lambda j, h: (0, 0))
-    return call(
-        row_kernel, 24 * NB * SUP * SUP, 12 * SUP * SUP,
+    anywhere = pl.BlockSpec(memory_space=pl.ANY)
+    return call(
+        row_kernel, 24 * NB * SUP * SUP, 12 * SUP * SUP, 30,
         grid_spec=pltpu.PrefetchScalarGridSpec(
             num_scalar_prefetch=1, grid=(2,),
             in_specs=[pl.BlockSpec((NB, SUP), lambda j, h: (step + 1, h[0] ^ j)), pl.BlockSpec((NB, SUP), lambda j, h: (0, 0)),
-                      whole(mine), whole(theirs)] + [whole(a) for a in extra],
-            out_specs=(out, out)),
+                      anywhere, anywhere] + [pl.BlockSpec(a.shape, lambda j, h: (0, 0)) for a in extra],
+            out_specs=(out, out), scratch_shapes=[pltpu.VMEM((2, SUP, SUP), F32), pltpu.SemaphoreType.DMA((2,))]),
         out_shape=(shape(NB, width), shape(NB, width)),
-    )(core, trail, l_rows, mine, theirs, *extra)
+    )(core, trail, in_hbm(l_rows), in_hbm(mine), in_hbm(theirs), *extra)
 
 
 def trail_kernel(core_ref, trail_ref, l_ref, mine_ref, theirs_ref, diag_ref, *rest):
+    rest, (landing, u_parts, l_parts, sem) = rest[:-4], rest[-4:]
     my_row = lax.axis_index("pr")
     j, i = pl.program_id(0), pl.program_id(1)
+    copies = [pltpu.make_async_copy(ref, landing, sem.at[n]) for n, ref in enumerate((mine_ref, theirs_ref))]
     out_ref = rest[0]
     if len(rest) > 1:
         out_ref = rest[8]
         pack_rows(jnp.minimum(j * pl.num_programs(1) + i, pl.num_programs(1) + 2), rest[:4], rest[4:8], rest[9])
 
-    def go(u_ref):
-        @pl.when(i == 0)
-        def _():
-            own = u_ref[pl.ds(pl.multiple_of(my_row * NB, NB), NB), :]
-            out_ref[...] = dot_tn(diag_ref[...], own)
-
-        @pl.when(i > 0)
-        def _():
-            out_ref[...] = trail_ref[...] - dot(l_ref[...], u_ref[...])
-
-    pl.when(j == 0)(lambda: go(mine_ref))
-    pl.when(j == 1)(lambda: go(theirs_ref))
+    @pl.when(i == 0)
+    def _():
+        pl.when(j == 0)(copies[0].start)
+        pl.when(j == 0)(copies[0].wait)
+        pl.when(j == 1)(copies[1].wait)
+
+        def split_rows(k, carry):
+            at = pl.ds(pl.multiple_of(k * 64, 64), 64)
+            for n, part in enumerate(split3(landing[at, :])):
+                u_parts[n, at, :] = part
+            return carry
+
+        lax.fori_loop(0, SUP // 64, split_rows, 0)
+        out_ref[...] = dot_tn(diag_ref[...], landing[pl.ds(pl.multiple_of(my_row * NB, NB), NB), :])
+
+    @pl.when(i > 0)
+    def _():
+        pl.when((i == 1) & (j == 0))(copies[1].start)
+        for n, part in enumerate(split3(l_ref[...])):
+            l_parts[n] = part
+        out_ref[...] = trail_ref[...] - dot_parts(lambda n: l_parts[n], lambda n: u_parts[n])
 
 
 def update_trail(core, trail, l_rows, mine, theirs, own_diag, step, out_cols=(), out_diags=()):
     rows, cols = trail.shape
     off = 1 if step < 3 else 0
-    count = rows // NB - step - off
+    count = rows // NB - step - off - (4 if step < 3 else 0)
     at = pl.BlockSpec((NB, SUP), lambda j, i, h: (jnp.where(i == 0, step, step + off + i), h[0] ^ j))
-    whole = pl.BlockSpec((SUP, SUP), lambda j, i, h: (0, 0))
-    ins = [at, pl.BlockSpec((NB, SUP), lambda j, i, h: (jnp.maximum(i, 1) - 1 + off, 0)), whole, whole,
+    anywhere = pl.BlockSpec(memory_space=pl.ANY)
+    ins = [at, pl.BlockSpec((NB, SUP), lambda j, i, h: (jnp.maximum(i, 1) - 1 + off, 0)), anywhere, anywhere,
            pl.BlockSpec((NB, NB), lambda j, i, h: (0, 0))]
     outs, shapes = [at], [shape(rows, cols)]
     if out_cols:
@@ -348,10 +472,11 @@
         outs.append(pl.BlockSpec((8 * NB, 128), lambda j, i, h: (block(j, i), 0)))
         shapes.append(shape(rows * 8, 128))
     return call(
-        trail_kernel, 12 * count * NB * cols * SUP, 8 * count * NB * cols,
-        grid_spec=pltpu.PrefetchScalarGridSpec(num_scalar_prefetch=1, grid=(2, count), in_specs=ins, out_specs=outs),
+        trail_kernel, 12 * count * NB * cols * SUP, 8 * count * NB * cols, 32,
+        grid_spec=pltpu.PrefetchScalarGridSpec(num_scalar_prefetch=1, grid=(2, count), in_specs=ins, out_specs=outs, scratch_shapes=[
+            pltpu.VMEM((SUP, SUP), F32), pltpu.VMEM((3, SUP, SUP), BF16), pltpu.VMEM((3, NB, SUP), BF16), pltpu.SemaphoreType.DMA((2,))]),
         out_shape=shapes, input_output_aliases={1: 0} if step else {},
-    )(core, trail, l_rows, mine, theirs, own_diag, *out_cols, *out_diags)
+    )(core, trail, in_hbm(l_rows), in_hbm(mine), in_hbm(theirs), *(in_hbm(a) for a in (own_diag, *out_cols, *out_diags)))
 
 
 FLIP1 = [(0, 1), (1, 0), (2, 3), (3, 2)]
@@ -360,16 +485,10 @@
 
 
 def gather_diag(block):
-    got = {(0, 0): block}
-    for jc in range(4):
-        for jr in (0, 2):
-            if (jc, jr) != (0, 0):
-                perm = [(4 * c + r, 4 * (c ^ jc) + (r ^ jr)) for c in range(4) for r in range(4)]
-                got[jc, jr] = lax.ppermute(block, ("pc", "pr"), perm)
-    for jc in range(4):
-        for jr in (0, 2):
-            got[jc, jr + 1] = lax.ppermute(got[jc, jr], "pr", FLIP1)
-    return [got[jc, jr] for jc in range(4) for jr in range(4)]
+    have = block[None]
+    for axis, perm in (("pc", FLIP1), ("pc", FLIP2), ("pr", FLIP2)):
+        have = jnp.concatenate([have, lax.ppermute(have, axis, perm)], axis=0)
+    return [have, lax.ppermute(have, "pr", FLIP1)]
 
 
 def gather_cols(keep, send):
@@ -378,7 +497,8 @@
 
 def gather_all(panel):
     x = lax.ppermute(panel, "pr", FLIP2)
-    return [panel, lax.ppermute(panel, "pr", FLIP1), x, lax.ppermute(x, "pr", FLIP1)]
+    other = lax.ppermute(panel, "pr", FLIP1)
+    return [panel, other, x, lax.ppermute(x, "pr", FLIP1)]
 
 
 def solution(mesh):
@@ -390,10 +510,11 @@
         out_cols, out_diags = [], []
         for step in range(4):
             if step == 0:
-                blocks = gather_diag(panel_tile[:NB, 0, :])
-                col_panel = panel_tile[NB:, 0, :]
+                diag_block, later = lax.optimization_barrier((panel_tile[:NB, 0, :], panel_tile))
+                blocks = gather_diag(diag_block)
+                col_panel = later[NB:, 0, :]
                 keep, send = (lax.dynamic_slice(trail_tile, (0, SUP * h), (NB, SUP)) for h in (half, 1 - half))
-                panel_row = jnp.concatenate([panel_tile[:NB, s, :] for s in (3, 2, 1)], axis=1)
+                panel_row = jnp.concatenate([later[:NB, s, :] for s in (3, 2, 1)], axis=1)
                 rest = unpack(panel_tile)
             else:
                 blocks = [lax.all_gather(diag_block, ("pc", "pr"))]
@@ -403,12 +524,16 @@
             if step == 0:
                 row_pieces = gather_all(panel_row)
             if step:
+                source = trail if step == 1 else None
                 trail, = update_trail(core, trail, l_rows, mine, theirs, own_diag, step - 1)
                 blocks, y, z, trail = lax.optimization_barrier((blocks, y, z, trail))
             split = col_panel.shape[0] // 2
             top = lax.ppermute(z[:split], "pc", FLIP1)
             bottom = lax.ppermute(y[split:], "pc", FLIP2)
-            x_sup, own_l, own_diag = factor(blocks)
+            if step == 0:
+                x_sup, own_l, own_diag = factor(blocks)
+            else:
+                x_sup, own_l, own_diag, trail = factor_beside(*blocks, source, trail, l_rows, mine, theirs)
             mine, *more = solve_cols(col_pieces, x_sup)
             if step == 0:
                 more = solve_cols(row_pieces, x_sup)

time: 954 us -> 870 us (0.912)
  Pallas kernels: 737 us -> 669 us
  waiting for transfers between devices: 128 us -> 108 us
    pallas_call x17, Pallas kernels: 558 us -> 501 us  [the longest x4 204 us: update_trail(): call(trail_kernel, 12 * count * NB * cols * SUP, 8 * count * NB * cols, 3...]
    ppermute x17 -> x6, waiting for transfers between devices: 81.9 us -> 29.6 us  [the longest x3 29.6 us: gather_diag(): have = jnp.concatenate([have, lax.ppermute(have, axis, perm)], axis=0)]
    ppermute x4, waiting for transfers between devices: 0.01 us -> 36.9 us  [local_part(): z = lax.ppermute(col_panel, 'pc', FLIP2)]
    ppermute x1, waiting for transfers between devices: 21.4 us -> 2.93 us  [gather_all(): x = lax.ppermute(panel, 'pr', FLIP2)]
    optimization_barrier x0 -> x1, local copies, waits for them, and re-layouts: none -> 11.8 us  [local_part(): lax.optimization_barrier((panel_tile[:NB, 0, :], panel_tile))]
  transfers between devices with their start and end apart: 53 -> 42, of which waited for: 9 -> 13; matrix products, arithmetic and copies ran while one was open for 2% -> 3% of each run, Pallas kernels for 68% -> 63%
where the time goes in v2:
time: 870 us; the launch traced here: 865 us
  Pallas kernels  669 us (77%)
  waiting for transfers between devices  108 us (12%)
  local copies, waits for them, and re-layouts  40.6 us (5%)
  starting transfers between devices  32.7 us (4%)
  between operations  14.4 us (2%)
    pallas_call x4, Pallas kernels, update_trail(): call(trail_kernel, 12 * count * NB * cols * SUP, 8 * count * NB * cols, 3...  204 us
    pallas_call x3, Pallas kernels, factor_beside(): call(fused_kernel, 100000000000, 1 << 25, 48, grid=(4,), out_shape=(near(...  152 us
    pallas_call x4, Pallas kernels, solve_rows(): call(functools.partial(rows_kernel, split), 30 * rows * SUP * SUP // 4, 1...  98 us
    pallas_call x3, Pallas kernels, update_panel(): call(panel_kernel, 12 * rows * width * SUP, 8 * rows * width + 4 * rows *...  70.3 us
    pallas_call x5, Pallas kernels, solve_cols(): call(cols_kernel, 30 * cols * SUP * SUP // 4, 12 * cols * SUP, 20, grid=(...  65.8 us
    pallas_call x3, Pallas kernels, update_row(): call(row_kernel, 24 * NB * SUP * SUP, 12 * SUP * SUP, 30, grid_spec=pltpu...  37.8 us
    ppermute x4, waiting for transfers between devices, local_part(): z = lax.ppermute(col_panel, 'pc', FLIP2)  36.9 us
    pallas_call x1, Pallas kernels, factor(): call(factor_kernel, 30000000000, 1 << 24, 20, grid=(4,), out_shape=(near(...  34.6 us
  transfers between devices with their start and end apart: 42, of which 13 were waited for; matrix products, arithmetic and copies ran while one was open for 3% of the time, Pallas kernels for 63%

profile of v2, /device:TPU:0, one launch (start us, length us, event | category | flops | bytes accessed | tf_op | source)
XLA Modules:
  0.0 865.1 jit_solution(18323085942427992202)
XLA Ops:
  8.6 3.3 collective-permute-start.4
  11.9 11.8 %copy.12 = f32[3072,4,256]{2,0,1:T(8,128)} copy(f32[3072,4,256]{2,1,0:T(4,128)} %param.2) | data formatting | bytes 25165824 | tf_op jit(solution)/shard_map/optimization_barrier | solution.py:513
  23.7 1.6 collective-permute-start.5
  25.3 3.5 slice_bitcast_fusion.own
  29.3 9.2 %collective-permute-done.5 = f32[2,256,256]{2,1,0:T(8,128)S(1)} collective-permute-done((f32[2,256,256]{2,1,0:T(8,128)S(1)}, f32[2,256,256]{2,1,0:T(8,128)S(1)}, u32[]{:S(2)}, u32[]{:S(2)}) %collective-permute-start.5) | collective-permute-done | bytes 524320 | tf_op jit(solution)/shard_map/ppermute | solution.py:490
  40.7 20.4 %collective-permute-done.6 = f32[4,256,256]{2,1,0:T(8,128)S(1)} collective-permute-done((f32[4,256,256]{2,1,0:T(8,128)S(1)}, f32[4,256,256]{2,1,0:T(8,128)S(1)}, u32[]{:S(2)}, u32[]{:S(2)}) %collective-permute-start.6) | collective-permute-done | bytes 1048608 | tf_op jit(solution)/shard_map/ppermute | solution.py:490
  61.3 1.8 constant_dynamic-slice_fusion
  66.3 32.7 %collective-permute-done.1.z = f32[2816,256]{1,0:T(8,128)} collective-permute-done((f32[2816,256]{1,0:T(8,128)}, f32[2816,256]{1,0:T(8,128)}, u32[]{:S(2)}, u32[]{:S(2)}) %collective-permute-start.1) | collective-permute-done | bytes 2883616 | tf_op jit(solution)/shard_map/ppermute | solution.py:522
  100.5 4.6 copy-done
  105.1 6.2 shard_map.41.refs_0_
  114.3 2.9 collective-permute-done.9.refs_2_
  117.2 1.6 collective-permute-start.10
  119.3 1.6 collective-permute-start.3
  120.9 34.6 %shard_map.42 = (f32[1024,1024]{1,0:T(8,128)S(1)}, f32[256,256]{1,0:T(8,128)}, f32[256,256]{1,0:T(8,128)}) custom-call(f32[8,256,256]{2,1,0:T(8,128)S(1)} %pad_maximum_fusion.refs_0_, f32[8,256,256]{2,1,0:T(8,128)} %collective-permute-done.7.refs_1_), custom_call_target="tpu_custom_call" | custom-call | flops 30000001024 | bytes 16777216 | tf_op jit(solution)/shard_map/pallas_call | solution.py:170
  155.5 11.5 %shard_map.46.mine_ref.refs_3_ = f32[1024,1024]{1,0:T(8,128)} custom-call(f32[256,1024]{1,0:T(8,128)S(1)} %get-tuple-element.121.refs_0_, f32[256,1024]{1,0:T(8,128)S(1)} %collective-permute-done.13.refs_1_, f32[256,1024]{1,0:T(8,128)S(1)} %collective-permute-done.14.refs_2_, f32[256,1024]{1,0:T(8,128)S(1)} %collective-permute-done.15.refs_3_, ...), custom_call_target="tpu_custom_call" | custom-call | flops 8053063680 | bytes 12582912 | tf_op jit(solution)/shard_map/pallas_call | solution.py:341
  167.0 8.8 %shard_map.44.refs_2_ = f32[1024,768]{1,0:T(8,128)} custom-call(f32[256,768]{1,0:T(8,128)S(1)} %pad_maximum_fusion.2.refs_0_, f32[256,768]{1,0:T(8,128)S(1)} %collective-permute-done.8.refs_1_, f32[256,768]{1,0:T(8,128)S(1)} %collective-permute-done.9.refs_2_, f32[256,768]{1,0:T(8,128)S(1)} %collective-permute-done.10.refs_3_, ...), custom_call_target="tpu_custom_call" | custom-call | flops 6039797760 | bytes 9437184 | tf_op jit(solution)/shard_map/pallas_call | solution.py:341
  175.8 28.2 %shard_map.43 = (f32[2816,1024]{1,0:T(8,128)}, f32[2816,256]{1,0:T(8,128)}) custom-call(f32[2816,256]{1,0:T(8,128)} %slice_bitcast_fusion.own, f32[2816,256]{1,0:T(8,128)} %collective-permute-done.y, f32[2816,256]{1,0:T(8,128)} %collective-permute-done.1.z, f32[1408,256]{1,0:T(8,128)S(1)} %collective-permute-done.2.top, ...), custom_call_target="tpu_custom_call" | custom-call | flops 22145925120 | bytes 34603008 | tf_op jit(solution)/shard_map/pallas_call | solution.py:307
  204.1 34.8 %shard_map.45 = (f32[256,256]{1,0:T(8,128)}, f32[2560,256]{1,0:T(8,128)}, f32[256,512]{1,0:T(8,128)}, f32[2560,512]{1,0:T(8,128)}) custom-call(f32[2816,768]{1,0:T(8,128)} %shard_map.41.refs_0_, f32[2816,1024]{1,0:T(8,128)} %get-tuple-element.64.refs_1_.l_ref.refs_2_, f32[1024,768]{1,0:T(8,128)S(1)} %copy-done.6), custom_call_target="tpu_custom_call" | custom-call | flops 26575110144 | bytes 28835840 | tf_op jit(solution)/shard_map/pallas_call | solution.py:376
  242.1 12.8 %shard_map.50 = (f32[256,1536]{1,0:T(8,128)}, f32[256,1536]{1,0:T(8,128)}) custom-call(s32[1]{0:T(128)} %bitcast.core_ref.refs_0_, f32[3072,2048]{1,0:T(8,128)} %refs_1_.1, f32[2816,1024]{1,0:T(8,128)} %get-tuple-element.64.refs_1_.l_ref.refs_2_, f32[1024,1024]{1,0:T(8,128)} %shard_map.46.mine_ref.refs_3_, ...), custom_call_target="tpu_custom_call" | custom-call | flops 6442450944 | bytes 12582912 | tf_op jit(solution)/shard_map/pallas_call | solution.py:415
  255.5 1.6 collective-permute-start.20
  257.1 50.9 %shard_map.47.rest_0_ = f32[3072,2048]{1,0:T(8,128)} custom-call(s32[1]{0:T(128)} %bitcast.core_ref.refs_0_, f32[3072,2048]{1,0:T(8,128)} %refs_1_.1, f32[2816,1024]{1,0:T(8,128)} %get-tuple-element.64.refs_1_.l_ref.refs_2_, f32[1024,1024]{1,0:T(8,128)} %shard_map.46.mine_ref.refs_3_, f32[1024,1024]{1,0:T(8,128)} %collective-permute-done.16.theirs_ref.refs_4_, ...), custom_call_target="tpu_custom_call" | custom-call | flops 45097156608 | bytes 29360128 | tf_op jit(solution)/shard_map/pallas_call | solution.py:474
  308.0 3.7 collective-permute-done.11.y
  313.0 2.5 slice.46
  317.6 50.8 %shard_map.48 = (f32[1024,1024]{1,0:T(8,128)S(1)}, f32[256,256]{1,0:T(8,128)}, f32[256,256]{1,0:T(8,128)}, f32[3072,2048]{1,0:T(8,128)}) custom-call(f32[16,256,256]{2,1,0:T(8,128)} %bitcast.32, f32[3072,2048]{1,0:T(8,128)} %refs_1_.1, f32[2816,1024]{1,0:T(8,128)} %get-tuple-element.64.refs_1_.l_ref.refs_2_, ...), custom_call_target="tpu_custom_call", output_to_operand_aliasing={{3}: (5, {})} | custom-call | flops 99999997952 | bytes 33554432 | tf_op jit(solution)/shard_map/pallas_call | solution.py:249
  368.4 18.0 %shard_map.51 = (f32[1024,1024]{1,0:T(8,128)}, f32[1024,512]{1,0:T(8,128)S(1)}) custom-call(f32[256,1536]{1,0:T(8,128)S(1)} %copy-done.3, f32[256,1536]{1,0:T(8,128)} %collective-permute-done.19.refs_1_, f32[256,1536]{1,0:T(8,128)} %collective-permute-done.20.refs_2_, f32[256,1536]{1,0:T(8,128)} %collective-permute-done.21.refs_3_, ...), custom_call_target="tpu_custom_call" | custom-call | flops 12079595520 | bytes 18874368 | tf_op jit(solution)/shard_map/pallas_call | solution.py:341
  386.4 25.5 %shard_map.49 = (f32[2560,1024]{1,0:T(8,128)}, f32[2560,256]{1,0:T(8,128)}) custom-call(f32[2560,256]{1,0:T(8,128)} %get-tuple-element.66.own, f32[2560,256]{1,0:T(8,128)S(1)} %collective-permute-done.11.y, f32[2560,256]{1,0:T(8,128)} %collective-permute-done.12.z, f32[1280,256]{1,0:T(8,128)S(1)} %collective-permute-done.17.top, ...), custom_call_target="tpu_custom_call" | custom-call | flops 20132659200 | bytes 31457280 | tf_op jit(solution)/shard_map/pallas_call | solution.py:307
  411.9 22.0 %shard_map.52 = (f32[256,256]{1,0:T(8,128)}, f32[2304,256]{1,0:T(8,128)}, f32[256,256]{1,0:T(8,128)}, f32[2304,256]{1,0:T(8,128)}) custom-call(f32[2560,512]{1,0:T(8,128)} %get-tuple-element.65.refs_0_, f32[2560,1024]{1,0:T(8,128)} %get-tuple-element.74.refs_1_.l_ref.refs_2_, f32[1024,512]{1,0:T(8,128)S(1)} %get-tuple-element.78.refs_2_), custom_call_target="tpu_custom_call" | custom-call | flops 16106127360 | bytes 20971520 | tf_op jit(solution)/shard_map/pallas_call | solution.py:376
  434.0 1.6 collective-permute-start.22
  435.6 1.6 collective-permute-start.23
  438.2 12.6 %shard_map.56 = (f32[256,1280]{1,0:T(8,128)}, f32[256,1280]{1,0:T(8,128)}) custom-call(s32[1]{0:T(128)} %bitcast.core_ref.refs_0_, f32[3072,2048]{1,0:T(8,128)} %get-tuple-element.82.trail_ref.refs_1_, f32[2560,1024]{1,0:T(8,128)} %get-tuple-element.74.refs_1_.l_ref.refs_2_, f32[1024,1024]{1,0:T(8,128)} %get-tuple-element.83.mine_ref.refs_3_, ...), custom_call_target="tpu_custom_call" | custom-call | flops 6442450944 | bytes 12582912 | tf_op jit(solution)/shard_map/pallas_call | solution.py:415
  451.4 1.6 collective-permute-start.28
  453.0 43.9 %shard_map.53.trail_ref = f32[3072,2048]{1,0:T(8,128)} custom-call(s32[1]{0:T(128)} %bitcast.core_ref.refs_0_, f32[3072,2048]{1,0:T(8,128)} %get-tuple-element.82.trail_ref.refs_1_, f32[2560,1024]{1,0:T(8,128)} %get-tuple-element.74.refs_1_.l_ref.refs_2_, f32[1024,1024]{1,0:T(8,128)} %get-tuple-element.83.mine_ref.refs_3_, ...), custom_call_target="tpu_custom_call", output_to_operand_aliasing={{}: (1, {})} | custom-call | flops 38654705664 | bytes 25165824 | tf_op jit(solution)/shard_map/pallas_call | solution.py:474
  496.9 4.2 collective-permute-done.22.y
  505.5 1.6 collective-permute-start.26
  507.0 50.8 %shard_map.54 = (f32[1024,1024]{1,0:T(8,128)S(1)}, f32[256,256]{1,0:T(8,128)}, f32[256,256]{1,0:T(8,128)}, f32[3072,2048]{1,0:T(8,128)}) custom-call(f32[16,256,256]{2,1,0:T(8,128)} %bitcast.31, f32[3072,2048]{1,0:T(8,128)} %shard_map.53.trail_ref, f32[2560,1024]{1,0:T(8,128)} %get-tuple-element.74.refs_1_.l_ref.refs_2_, ...), custom_call_target="tpu_custom_call", output_to_operand_aliasing={{3}: (1, {})} | custom-call | flops 99999997952 | bytes 33554432 | tf_op jit(solution)/shard_map/pallas_call | solution.py:249
  557.9 15.2 %shard_map.57 = (f32[1024,1024]{1,0:T(8,128)}, f32[1024,256]{1,0:T(8,128)S(1)}) custom-call(f32[256,1280]{1,0:T(8,128)S(1)} %copy-done.4, f32[256,1280]{1,0:T(8,128)} %collective-permute-done.27.refs_1_, f32[256,1280]{1,0:T(8,128)} %collective-permute-done.28.refs_2_, f32[256,1280]{1,0:T(8,128)} %collective-permute-done.29.refs_3_, ...), custom_call_target="tpu_custom_call" | custom-call | flops 10066329600 | bytes 15728640 | tf_op jit(solution)/shard_map/pallas_call | solution.py:341
  573.1 23.3 %shard_map.55 = (f32[2304,1024]{1,0:T(8,128)}, f32[2304,256]{1,0:T(8,128)}) custom-call(f32[2304,256]{1,0:T(8,128)} %get-tuple-element.80.own, f32[2304,256]{1,0:T(8,128)S(1)} %collective-permute-done.22.y, f32[2304,256]{1,0:T(8,128)} %collective-permute-done.23.z, f32[1152,256]{1,0:T(8,128)S(1)} %collective-permute-done.25.top, ...), custom_call_target="tpu_custom_call" | custom-call | flops 18119393280 | bytes 28311552 | tf_op jit(solution)/shard_map/pallas_call | solution.py:307
  596.3 13.4 %shard_map.58 = (f32[256,256]{1,0:T(8,128)}, f32[2048,256]{1,0:T(8,128)}) custom-call(f32[2304,256]{1,0:T(8,128)} %get-tuple-element.79.refs_0_, f32[2304,1024]{1,0:T(8,128)} %get-tuple-element.90.refs_1_.l_ref.refs_2_, f32[1024,256]{1,0:T(8,128)S(1)} %get-tuple-element.94.refs_2_), custom_call_target="tpu_custom_call" | custom-call | flops 7247757312 | bytes 14155776 | tf_op jit(solution)/shard_map/pallas_call | solution.py:376
  611.9 5.3 collective-permute-done.32.theirs_ref.refs_4_
  617.2 2.1 copy-done.7
  619.3 12.3 %shard_map.62 = (f32[256,1024]{1,0:T(8,128)}, f32[256,1024]{1,0:T(8,128)}) custom-call(s32[1]{0:T(128)} %bitcast.core_ref.refs_0_, f32[3072,2048]{1,0:T(8,128)} %get-tuple-element.97.trail_ref.refs_1_, f32[2304,1024]{1,0:T(8,128)} %get-tuple-element.90.refs_1_.l_ref.refs_2_, f32[1024,1024]{1,0:T(8,128)} %get-tuple-element.98.mine_ref.refs_3_, ...), custom_call_target="tpu_custom_call" | custom-call | flops 6442450944 | bytes 12582912 | tf_op jit(solution)/shard_map/pallas_call | solution.py:415
  633.8 37.0 %shard_map.59.trail_ref = f32[3072,2048]{1,0:T(8,128)} custom-call(s32[1]{0:T(128)} %bitcast.core_ref.refs_0_, f32[3072,2048]{1,0:T(8,128)} %get-tuple-element.97.trail_ref.refs_1_, f32[2304,1024]{1,0:T(8,128)} %get-tuple-element.90.refs_1_.l_ref.refs_2_, f32[1024,1024]{1,0:T(8,128)} %get-tuple-element.98.mine_ref.refs_3_, ...), custom_call_target="tpu_custom_call", output_to_operand_aliasing={{}: (1, {})} | custom-call | flops 32212254720 | bytes 20971520 | tf_op jit(solution)/shard_map/pallas_call | solution.py:474
  672.6 50.7 %shard_map.60 = (f32[1024,1024]{1,0:T(8,128)S(1)}, f32[256,256]{1,0:T(8,128)}, f32[256,256]{1,0:T(8,128)}, f32[3072,2048]{1,0:T(8,128)}) custom-call(f32[16,256,256]{2,1,0:T(8,128)} %bitcast.33, f32[3072,2048]{1,0:T(8,128)} %shard_map.59.trail_ref, f32[2304,1024]{1,0:T(8,128)} %get-tuple-element.90.refs_1_.l_ref.refs_2_, ...), custom_call_target="tpu_custom_call", output_to_operand_aliasing={{3}: (1, {})} | custom-call | flops 99999997952 | bytes 33554432 | tf_op jit(solution)/shard_map/pallas_call | solution.py:249
  723.3 12.3 %shard_map.63.mine_ref = f32[1024,1024]{1,0:T(8,128)} custom-call(f32[256,1024]{1,0:T(8,128)S(1)} %copy-done.5, f32[256,1024]{1,0:T(8,128)S(1)} %collective-permute-done.35.refs_1_, f32[256,1024]{1,0:T(8,128)} %collective-permute-done.36.refs_2_, f32[256,1024]{1,0:T(8,128)} %collective-permute-done.37.refs_3_, f32[1024,1024]{1,0:T(8,128)S(1)} %get-tuple-element.105.x_ref.refs_4_), custom_call_target="tpu_custom_call" | custom-call | flops 8053063680 | bytes 12582912 | tf_op jit(solution)/shard_map/pallas_call | solution.py:341
  738.1 24.5 %collective-permute-done.33.top = f32[1024,256]{1,0:T(8,128)S(1)} collective-permute-done((f32[1024,256]{1,0:T(8,128)S(1)}, f32[1024,256]{1,0:T(8,128)S(1)}, u32[]{:S(2)}, u32[]{:S(2)}) %collective-permute-start.33) | collective-permute-done | bytes 1048608 | tf_op jit(solution)/shard_map/ppermute | solution.py:531
  762.9 21.0 %shard_map.61 = (f32[2048,1024]{1,0:T(8,128)}, f32[2048,256]{1,0:T(8,128)}) custom-call(f32[2048,256]{1,0:T(8,128)} %get-tuple-element.96.own, f32[2048,256]{1,0:T(8,128)S(1)} %collective-permute-done.30.y, f32[2048,256]{1,0:T(8,128)} %collective-permute-done.31.z, f32[1024,256]{1,0:T(8,128)S(1)} %collective-permute-done.33.top, ...), custom_call_target="tpu_custom_call" | custom-call | flops 16106127360 | bytes 25165824 | tf_op jit(solution)/shard_map/pallas_call | solution.py:307
  783.9 1.9 copy-done.8
  785.8 72.5 %shard_map.64 = (f32[3072,2048]{1,0:T(8,128)}, f32[24576,128]{1,0:T(8,128)}) custom-call(s32[1]{0:T(128)} %bitcast.core_ref.refs_0_, f32[3072,2048]{1,0:T(8,128)} %get-tuple-element.102.trail_ref, f32[2048,1024]{1,0:T(8,128)} %get-tuple-element.106.l_ref, f32[1024,1024]{1,0:T(8,128)} %shard_map.63.mine_ref, ...), custom_call_target="tpu_custom_call", output_to_operand_aliasing={{0}: (1, {})} | custom-call | flops 57982058496 | bytes 37748736 | tf_op jit(solution)/shard_map/pallas_call | solution.py:474
  (99 shorter events, 34.6 us)
Async XLA Ops:
  7.2 305.8 %all-gather.7.cloned.1.call-start = ((), (), s32[]{:S(2)}) async-start(), calls=%async_computation | async-start | bytes 4456448 | tf_op jit(solution)/shard_map/all_gather | solution.py:520
  8.6 15.0 %collective-permute-start.4 = (f32[1,256,256]{2,1,0:T(8,128)S(1)}, f32[1,256,256]{2,1,0:T(8,128)S(1)}, u32[]{:S(2)}, u32[]{:S(2)}) collective-permute-start(f32[1,256,256]{2,1,0:T(8,128)S(1)} %bitcast.27), channel_id=1, source_target_pairs={{0,4},{4,0},{8,12},{12,8},{1,5},{5,1},{9,13},{13,9},{2,6},{6,2},{1... | collective-permute-start | bytes 786440 | tf_op jit(solution)/shard_map/ppermute | solution.py:490
  23.7 14.8 %collective-permute-start.5 = (f32[2,256,256]{2,1,0:T(8,128)S(1)}, f32[2,256,256]{2,1,0:T(8,128)S(1)}, u32[]{:S(2)}, u32[]{:S(2)}) collective-permute-start(f32[2,256,256]{2,1,0:T(8,128)S(1)} %pad_maximum_fusion.3), channel_id=1, source_target_pairs={{0,8},{8,0},{4,12},{12,4},{1,9},{9,1},{5,13},{13,5},{2,10},{10,2},... | collective-permute-start | bytes 1572872 | tf_op jit(solution)/shard_map/ppermute | solution.py:490
  28.9 70.2 %collective-permute-start.1 = (f32[2816,256]{1,0:T(8,128)}, f32[2816,256]{1,0:T(8,128)}, u32[]{:S(2)}, u32[]{:S(2)}) collective-permute-start(f32[2816,256]{1,0:T(8,128)} %slice_bitcast_fusion.own), channel_id=1, source_target_pairs={{0,8},{8,0},{4,12},{12,4},{1,9},{9,1},{5,13},{13,5},{2,10},{10,2},... | collective-permute-start | bytes 8650760 | tf_op jit(solution)/shard_map/ppermute | solution.py:522
  38.6 22.4 %collective-permute-start.6 = (f32[4,256,256]{2,1,0:T(8,128)S(1)}, f32[4,256,256]{2,1,0:T(8,128)S(1)}, u32[]{:S(2)}, u32[]{:S(2)}) collective-permute-start(f32[4,256,256]{2,1,0:T(8,128)S(1)} %pad_maximum_fusion.1), channel_id=1, source_target_pairs={{0,2},{2,0},{1,3},{3,1},{4,6},{6,4},{5,7},{7,5},{8,10},{10,8},{9,1... | collective-permute-start | bytes 3145736 | tf_op jit(solution)/shard_map/ppermute | solution.py:490
  40.2 72.6 %collective-permute-start = (f32[2816,256]{1,0:T(8,128)}, f32[2816,256]{1,0:T(8,128)}, u32[]{:S(2)}, u32[]{:S(2)}) collective-permute-start(f32[2816,256]{1,0:T(8,128)} %slice_bitcast_fusion.own), channel_id=1, source_target_pairs={{0,4},{4,0},{8,12},{12,8},{1,5},{5,1},{9,13},{13,9},{2,6},{6,2},{1... | collective-permute-start | bytes 8650760 | tf_op jit(solution)/shard_map/ppermute | solution.py:521
  61.3 58.1 %collective-permute-start.7 = (f32[8,256,256]{2,1,0:T(8,128)S(1)}, f32[8,256,256]{2,1,0:T(8,128)}, u32[]{:S(2)}, u32[]{:S(2)}) collective-permute-start(f32[8,256,256]{2,1,0:T(8,128)S(1)} %pad_maximum_fusion.refs_0_), channel_id=1, source_target_pairs={{0,1},{1,0},{2,3},{3,2},{4,5},{5,4},{6,7},{7,6},{8,9},{9,8},{10,11... | collective-permute-start | bytes 6291464 | tf_op jit(solution)/shard_map/ppermute | solution.py:491
  63.1 54.1 %collective-permute-start.13 = (f32[256,1024]{1,0:T(8,128)S(1)}, f32[256,1024]{1,0:T(8,128)S(1)}, u32[]{:S(2)}, u32[]{:S(2)}) collective-permute-start(f32[256,1024]{1,0:T(8,128)S(1)} %get-tuple-element.120), channel_id=1, source_target_pairs={{0,1},{1,0},{2,3},{3,2},{4,5},{5,4},{6,7},{7,6},{8,9},{9,8},{10,11... | collective-permute-start | bytes 3145736 | tf_op jit(solution)/shard_map/ppermute | solution.py:495
  63.6 55.2 %collective-permute-start.14 = (f32[256,1024]{1,0:T(8,128)S(1)}, f32[256,1024]{1,0:T(8,128)S(1)}, u32[]{:S(2)}, u32[]{:S(2)}) collective-permute-start(f32[256,1024]{1,0:T(8,128)S(1)} %get-tuple-element.121.refs_0_), channel_id=1, source_target_pairs={{0,2},{2,0},{1,3},{3,1},{4,6},{6,4},{5,7},{7,5},{8,10},{10,8},{9,1... | collective-permute-start | bytes 3145736 | tf_op jit(solution)/shard_map/ppermute | solution.py:495
  99.0 18.1 %collective-permute-start.9 = (f32[256,768]{1,0:T(8,128)S(1)}, f32[256,768]{1,0:T(8,128)S(1)}, u32[]{:S(2)}, u32[]{:S(2)}) collective-permute-start(f32[256,768]{1,0:T(8,128)S(1)} %pad_maximum_fusion.2.refs_0_), channel_id=1, source_target_pairs={{0,2},{2,0},{1,3},{3,1},{4,6},{6,4},{5,7},{7,5},{8,10},{10,8},{9,1... | collective-permute-start | bytes 2359304 | tf_op jit(solution)/shard_map/ppermute | solution.py:499
  100.5 4.6 copy-start
  112.8 54.2 %collective-permute-start.8 = (f32[256,768]{1,0:T(8,128)S(1)}, f32[256,768]{1,0:T(8,128)S(1)}, u32[]{:S(2)}, u32[]{:S(2)}) collective-permute-start(f32[256,768]{1,0:T(8,128)S(1)} %pad_maximum_fusion.2.refs_0_), channel_id=1, source_target_pairs={{0,1},{1,0},{2,3},{3,2},{4,5},{5,4},{6,7},{7,6},{8,9},{9,8},{10,11... | collective-permute-start | bytes 2359304 | tf_op jit(solution)/shard_map/ppermute | solution.py:500
  117.2 38.3 %collective-permute-start.15 = (f32[256,1024]{1,0:T(8,128)S(1)}, f32[256,1024]{1,0:T(8,128)S(1)}, u32[]{:S(2)}, u32[]{:S(2)}) collective-permute-start(f32[256,1024]{1,0:T(8,128)S(1)} %get-tuple-element.120), channel_id=1, source_target_pairs={{0,3},{3,0},{1,2},{2,1},{4,7},{7,4},{5,6},{6,5},{8,11},{11,8},{9,1... | collective-permute-start | bytes 3145736 | tf_op jit(solution)/shard_map/ppermute | solution.py:495
  117.2 49.8 %collective-permute-start.10 = (f32[256,768]{1,0:T(8,128)S(1)}, f32[256,768]{1,0:T(8,128)S(1)}, u32[]{:S(2)}, u32[]{:S(2)}) collective-permute-start(f32[256,768]{1,0:T(8,128)S(1)} %collective-permute-done.9.refs_2_), channel_id=1, source_target_pairs={{0,1},{1,0},{2,3},{3,2},{4,5},{5,4},{6,7},{7,6},{8,9},{9,8},{10,11... | collective-permute-start | bytes 2359304 | tf_op jit(solution)/shard_map/ppermute | solution.py:501
  118.8 57.0 %collective-permute-start.2 = (f32[1408,256]{1,0:T(8,128)S(1)}, f32[1408,256]{1,0:T(8,128)S(1)}, u32[]{:S(2)}, u32[]{:S(2)}) collective-permute-start(f32[1408,256]{1,0:T(8,128)S(1)} %slice.53), channel_id=1, source_target_pairs={{0,4},{4,0},{8,12},{12,8},{1,5},{5,1},{9,13},{13,9},{2,6},{6,2},{1... | collective-permute-start | bytes 4325384 | tf_op jit(solution)/shard_map/ppermute | solution.py:531
  119.3 56.5 %collective-permute-start.3 = (f32[1408,256]{1,0:T(8,128)S(1)}, f32[1408,256]{1,0:T(8,128)S(1)}, u32[]{:S(2)}, u32[]{:S(2)}) collective-permute-start(f32[1408,256]{1,0:T(8,128)S(1)} %slice.54), channel_id=1, source_target_pairs={{0,8},{8,0},{4,12},{12,4},{1,9},{9,1},{5,13},{13,5},{2,10},{10,2},... | collective-permute-start | bytes 4325384 | tf_op jit(solution)/shard_map/ppermute | solution.py:532
  167.0 74.0 %collective-permute-start.16 = (f32[1024,1024]{1,0:T(8,128)}, f32[1024,1024]{1,0:T(8,128)}, u32[]{:S(2)}, u32[]{:S(2)}) collective-permute-start(f32[1024,1024]{1,0:T(8,128)} %shard_map.46.mine_ref.refs_3_), channel_id=1, source_target_pairs={{0,1},{1,0},{2,3},{3,2},{4,5},{5,4},{6,7},{7,6},{8,9},{9,8},{10,11... | collective-permute-start | bytes 12582920 | tf_op jit(solution)/shard_map/ppermute | solution.py:540
  175.8 28.3 %copy-start.6 = (f32[1024,768]{1,0:T(8,128)S(1)}, f32[1024,768]{1,0:T(8,128)}, u32[]{:S(2)}) copy-start(f32[1024,768]{1,0:T(8,128)} %shard_map.44.refs_2_) | copy-start | bytes 9437188
  239.0 263.5 %all-gather.9.cloned.1.call-start = ((), (), s32[]{:S(2)}) async-start(), calls=%async_computation.1 | async-start | bytes 4456448 | tf_op jit(solution)/shard_map/all_gather | solution.py:520
  239.0 72.6 %collective-permute-start.11 = (f32[2560,256]{1,0:T(8,128)}, f32[2560,256]{1,0:T(8,128)S(1)}, u32[]{:S(2)}, u32[]{:S(2)}) collective-permute-start(f32[2560,256]{1,0:T(8,128)} %get-tuple-element.66.own), channel_id=1, source_target_pairs={{0,4},{4,0},{8,12},{12,8},{1,5},{5,1},{9,13},{13,9},{2,6},{6,2},{1... | collective-permute-start | bytes 7864328 | tf_op jit(solution)/shard_map/ppermute | solution.py:521
  240.6 72.4 %collective-permute-start.12 = (f32[2560,256]{1,0:T(8,128)}, f32[2560,256]{1,0:T(8,128)}, u32[]{:S(2)}, u32[]{:S(2)}) collective-permute-start(f32[2560,256]{1,0:T(8,128)} %get-tuple-element.66.own), channel_id=1, source_target_pairs={{0,8},{8,0},{4,12},{12,4},{1,9},{9,1},{5,13},{13,5},{2,10},{10,2},... | collective-permute-start | bytes 7864328 | tf_op jit(solution)/shard_map/ppermute | solution.py:522
  254.9 113.5 %collective-permute-start.19 = (f32[256,1536]{1,0:T(8,128)}, f32[256,1536]{1,0:T(8,128)}, u32[]{:S(2)}, u32[]{:S(2)}) collective-permute-start(f32[256,1536]{1,0:T(8,128)} %get-tuple-element.77), channel_id=1, source_target_pairs={{0,1},{1,0},{2,3},{3,2},{4,5},{5,4},{6,7},{7,6},{8,9},{9,8},{10,11... | collective-permute-start | bytes 4718600 | tf_op jit(solution)/shard_map/ppermute | solution.py:495
  254.9 113.4 %collective-permute-start.21 = (f32[256,1536]{1,0:T(8,128)}, f32[256,1536]{1,0:T(8,128)}, u32[]{:S(2)}, u32[]{:S(2)}) collective-permute-start(f32[256,1536]{1,0:T(8,128)} %get-tuple-element.77), channel_id=1, source_target_pairs={{0,3},{3,0},{1,2},{2,1},{4,7},{7,4},{5,6},{6,5},{8,11},{11,8},{9,1... | collective-permute-start | bytes 4718600 | tf_op jit(solution)/shard_map/ppermute | solution.py:495
  255.5 112.9 %collective-permute-start.20 = (f32[256,1536]{1,0:T(8,128)}, f32[256,1536]{1,0:T(8,128)}, u32[]{:S(2)}, u32[]{:S(2)}) collective-permute-start(f32[256,1536]{1,0:T(8,128)} %get-tuple-element.76.refs_0_), channel_id=1, source_target_pairs={{0,2},{2,0},{1,3},{3,1},{4,6},{6,4},{5,7},{7,5},{8,10},{10,8},{9,1... | collective-permute-start | bytes 4718600 | tf_op jit(solution)/shard_map/ppermute | solution.py:495
  315.5 70.9 %collective-permute-start.17 = (f32[1280,256]{1,0:T(8,128)}, f32[1280,256]{1,0:T(8,128)S(1)}, u32[]{:S(2)}, u32[]{:S(2)}) collective-permute-start(f32[1280,256]{1,0:T(8,128)} %slice.46), channel_id=1, source_target_pairs={{0,4},{4,0},{8,12},{12,8},{1,5},{5,1},{9,13},{13,9},{2,6},{6,2},{1... | collective-permute-start | bytes 3932168 | tf_op jit(solution)/shard_map/ppermute | solution.py:531
  317.1 51.3 %copy-start.3 = (f32[256,1536]{1,0:T(8,128)S(1)}, f32[256,1536]{1,0:T(8,128)}, u32[]{:S(2)}) copy-start(f32[256,1536]{1,0:T(8,128)} %get-tuple-element.76.refs_0_) | copy-start | bytes 4718596
  317.1 69.3 %collective-permute-start.18 = (f32[1280,256]{1,0:T(8,128)}, f32[1280,256]{1,0:T(8,128)S(1)}, u32[]{:S(2)}, u32[]{:S(2)}) collective-permute-start(f32[1280,256]{1,0:T(8,128)} %slice.47), channel_id=1, source_target_pairs={{0,8},{8,0},{4,12},{12,4},{1,9},{9,1},{5,13},{13,5},{2,10},{10,2},... | collective-permute-start | bytes 3932168 | tf_op jit(solution)/shard_map/ppermute | solution.py:532
  386.4 50.9 %collective-permute-start.24 = (f32[1024,1024]{1,0:T(8,128)}, f32[1024,1024]{1,0:T(8,128)}, u32[]{:S(2)}, u32[]{:S(2)}) collective-permute-start(f32[1024,1024]{1,0:T(8,128)} %get-tuple-element.83.mine_ref.refs_3_), channel_id=1, source_target_pairs={{0,1},{1,0},{2,3},{3,2},{4,5},{5,4},{6,7},{7,6},{8,9},{9,8},{10,11... | collective-permute-start | bytes 12582920 | tf_op jit(solution)/shard_map/ppermute | solution.py:540
  434.0 238.6 %all-gather.11.cloned.1.call-start = ((), (), s32[]{:S(2)}) async-start(), calls=%async_computation.2 | async-start | bytes 4456448 | tf_op jit(solution)/shard_map/all_gather | solution.py:520
  434.0 67.0 %collective-permute-start.22 = (f32[2304,256]{1,0:T(8,128)}, f32[2304,256]{1,0:T(8,128)S(1)}, u32[]{:S(2)}, u32[]{:S(2)}) collective-permute-start(f32[2304,256]{1,0:T(8,128)} %get-tuple-element.80.own), channel_id=1, source_target_pairs={{0,4},{4,0},{8,12},{12,8},{1,5},{5,1},{9,13},{13,9},{2,6},{6,2},{1... | collective-permute-start | bytes 7077896 | tf_op jit(solution)/shard_map/ppermute | solution.py:521
  435.6 66.9 %collective-permute-start.23 = (f32[2304,256]{1,0:T(8,128)}, f32[2304,256]{1,0:T(8,128)}, u32[]{:S(2)}, u32[]{:S(2)}) collective-permute-start(f32[2304,256]{1,0:T(8,128)} %get-tuple-element.80.own), channel_id=1, source_target_pairs={{0,8},{8,0},{4,12},{12,4},{1,9},{9,1},{5,13},{13,5},{2,10},{10,2},... | collective-permute-start | bytes 7077896 | tf_op jit(solution)/shard_map/ppermute | solution.py:522
  450.9 107.0 %collective-permute-start.27 = (f32[256,1280]{1,0:T(8,128)}, f32[256,1280]{1,0:T(8,128)}, u32[]{:S(2)}, u32[]{:S(2)}) collective-permute-start(f32[256,1280]{1,0:T(8,128)} %get-tuple-element.93), channel_id=1, source_target_pairs={{0,1},{1,0},{2,3},{3,2},{4,5},{5,4},{6,7},{7,6},{8,9},{9,8},{10,11... | collective-permute-start | bytes 3932168 | tf_op jit(solution)/shard_map/ppermute | solution.py:495
  450.9 106.9 %collective-permute-start.29 = (f32[256,1280]{1,0:T(8,128)}, f32[256,1280]{1,0:T(8,128)}, u32[]{:S(2)}, u32[]{:S(2)}) collective-permute-start(f32[256,1280]{1,0:T(8,128)} %get-tuple-element.93), channel_id=1, source_target_pairs={{0,3},{3,0},{1,2},{2,1},{4,7},{7,4},{5,6},{6,5},{8,11},{11,8},{9,1... | collective-permute-start | bytes 3932168 | tf_op jit(solution)/shard_map/ppermute | solution.py:495
  451.4 106.4 %collective-permute-start.28 = (f32[256,1280]{1,0:T(8,128)}, f32[256,1280]{1,0:T(8,128)}, u32[]{:S(2)}, u32[]{:S(2)}) collective-permute-start(f32[256,1280]{1,0:T(8,128)} %get-tuple-element.92.refs_0_), channel_id=1, source_target_pairs={{0,2},{2,0},{1,3},{3,1},{4,6},{6,4},{5,7},{7,5},{8,10},{10,8},{9,1... | collective-permute-start | bytes 3932168 | tf_op jit(solution)/shard_map/ppermute | solution.py:495
  503.8 69.2 %collective-permute-start.25 = (f32[1152,256]{1,0:T(8,128)S(1)}, f32[1152,256]{1,0:T(8,128)S(1)}, u32[]{:S(2)}, u32[]{:S(2)}) collective-permute-start(f32[1152,256]{1,0:T(8,128)S(1)} %slice.48), channel_id=1, source_target_pairs={{0,4},{4,0},{8,12},{12,8},{1,5},{5,1},{9,13},{13,9},{2,6},{6,2},{1... | collective-permute-start | bytes 3538952 | tf_op jit(solution)/shard_map/ppermute | solution.py:531
  505.5 52.4 %copy-start.4 = (f32[256,1280]{1,0:T(8,128)S(1)}, f32[256,1280]{1,0:T(8,128)}, u32[]{:S(2)}) copy-start(f32[256,1280]{1,0:T(8,128)} %get-tuple-element.92.refs_0_) | copy-start | bytes 3932164
  505.5 67.6 %collective-permute-start.26 = (f32[1152,256]{1,0:T(8,128)}, f32[1152,256]{1,0:T(8,128)S(1)}, u32[]{:S(2)}, u32[]{:S(2)}) collective-permute-start(f32[1152,256]{1,0:T(8,128)} %slice.49), channel_id=1, source_target_pairs={{0,8},{8,0},{4,12},{12,4},{1,9},{9,1},{5,13},{13,5},{2,10},{10,2},... | collective-permute-start | bytes 3538952 | tf_op jit(solution)/shard_map/ppermute | solution.py:532
  609.8 7.4 collective-permute-start.32
  609.8 61.3 %collective-permute-start.30 = (f32[2048,256]{1,0:T(8,128)}, f32[2048,256]{1,0:T(8,128)S(1)}, u32[]{:S(2)}, u32[]{:S(2)}) collective-permute-start(f32[2048,256]{1,0:T(8,128)} %get-tuple-element.96.own), channel_id=1, source_target_pairs={{0,4},{4,0},{8,12},{12,8},{1,5},{5,1},{9,13},{13,9},{2,6},{6,2},{1... | collective-permute-start | bytes 6291464 | tf_op jit(solution)/shard_map/ppermute | solution.py:521
  611.4 61.2 %collective-permute-start.31 = (f32[2048,256]{1,0:T(8,128)}, f32[2048,256]{1,0:T(8,128)}, u32[]{:S(2)}, u32[]{:S(2)}) collective-permute-start(f32[2048,256]{1,0:T(8,128)} %get-tuple-element.96.own), channel_id=1, source_target_pairs={{0,8},{8,0},{4,12},{12,4},{1,9},{9,1},{5,13},{13,5},{2,10},{10,2},... | collective-permute-start | bytes 6291464 | tf_op jit(solution)/shard_map/ppermute | solution.py:522
  617.2 2.1 copy-start.7
  631.6 91.7 %collective-permute-start.35 = (f32[256,1024]{1,0:T(8,128)}, f32[256,1024]{1,0:T(8,128)S(1)}, u32[]{:S(2)}, u32[]{:S(2)}) collective-permute-start(f32[256,1024]{1,0:T(8,128)} %get-tuple-element.108), channel_id=1, source_target_pairs={{0,1},{1,0},{2,3},{3,2},{4,5},{5,4},{6,7},{7,6},{8,9},{9,8},{10,11... | collective-permute-start | bytes 3145736 | tf_op jit(solution)/shard_map/ppermute | solution.py:495
  631.8 91.5 %collective-permute-start.37 = (f32[256,1024]{1,0:T(8,128)}, f32[256,1024]{1,0:T(8,128)}, u32[]{:S(2)}, u32[]{:S(2)}) collective-permute-start(f32[256,1024]{1,0:T(8,128)} %get-tuple-element.108), channel_id=1, source_target_pairs={{0,3},{3,0},{1,2},{2,1},{4,7},{7,4},{5,6},{6,5},{8,11},{11,8},{9,1... | collective-permute-start | bytes 3145736 | tf_op jit(solution)/shard_map/ppermute | solution.py:495
  632.3 91.0 %collective-permute-start.36 = (f32[256,1024]{1,0:T(8,128)}, f32[256,1024]{1,0:T(8,128)}, u32[]{:S(2)}, u32[]{:S(2)}) collective-permute-start(f32[256,1024]{1,0:T(8,128)} %get-tuple-element.107.refs_0_), channel_id=1, source_target_pairs={{0,2},{2,0},{1,3},{3,1},{4,6},{6,4},{5,7},{7,5},{8,10},{10,8},{9,1... | collective-permute-start | bytes 3145736 | tf_op jit(solution)/shard_map/ppermute | solution.py:495
  672.6 50.7 %copy-start.5 = (f32[256,1024]{1,0:T(8,128)S(1)}, f32[256,1024]{1,0:T(8,128)}, u32[]{:S(2)}) copy-start(f32[256,1024]{1,0:T(8,128)} %get-tuple-element.107.refs_0_) | copy-start | bytes 3145732
  735.6 48.2 %collective-permute-start.38 = (f32[1024,1024]{1,0:T(8,128)}, f32[1024,1024]{1,0:T(8,128)S(1)}, u32[]{:S(2)}, u32[]{:S(2)}) collective-permute-start(f32[1024,1024]{1,0:T(8,128)} %shard_map.63.mine_ref), channel_id=1, source_target_pairs={{0,1},{1,0},{2,3},{3,2},{4,5},{5,4},{6,7},{7,6},{8,9},{9,8},{10,11... | collective-permute-start | bytes 12582920 | tf_op jit(solution)/shard_map/ppermute | solution.py:540
  736.9 25.6 %collective-permute-start.33 = (f32[1024,256]{1,0:T(8,128)S(1)}, f32[1024,256]{1,0:T(8,128)S(1)}, u32[]{:S(2)}, u32[]{:S(2)}) collective-permute-start(f32[1024,256]{1,0:T(8,128)S(1)} %slice.50), channel_id=1, source_target_pairs={{0,4},{4,0},{8,12},{12,8},{1,5},{5,1},{9,13},{13,9},{2,6},{6,2},{1... | collective-permute-start | bytes 3145736 | tf_op jit(solution)/shard_map/ppermute | solution.py:531
  737.6 25.3 %collective-permute-start.34 = (f32[1024,256]{1,0:T(8,128)S(1)}, f32[1024,256]{1,0:T(8,128)S(1)}, u32[]{:S(2)}, u32[]{:S(2)}) collective-permute-start(f32[1024,256]{1,0:T(8,128)S(1)} %slice.51), channel_id=1, source_target_pairs={{0,8},{8,0},{4,12},{12,4},{1,9},{9,1},{5,13},{13,5},{2,10},{10,2},... | collective-permute-start | bytes 3145736 | tf_op jit(solution)/shard_map/ppermute | solution.py:532
  (3 other events, 3.9 us)
Sparse Core Ops, SparseCore 0:
  239.1 48.1 all-gather.6
  434.1 49.1 all-gather.8
  609.9 47.9 all-gather.10

commit v3 on v2

--- a/solution.py
+++ b/solution.py
@@ -279,7 +279,8 @@
         pl.when(i > s)(lambda s=s: put(cols[s][...]))
 
 
-def rows_kernel(split, own, y, z, top, bottom, x_ref, out_ref, own_ref, wide):
+def rows_kernel(*refs):
+    (own, y, z, *far), (x_ref, out_ref, own_ref, wide) = refs[:-4], refs[-4:]
     my_col = lax.axis_index("pc")
     i = pl.program_id(0)
 
@@ -289,8 +290,11 @@
     place(0, own)
     place(1, y)
     place(2, z)
-    pl.when(i < split)(lambda: place(3, top))
-    pl.when(i >= split)(lambda: place(3, bottom))
+    if len(far) == 1:
+        place(3, far[0])
+    else:
+        pl.when(i < 2)(lambda: place(3, far[0]))
+        pl.when(i >= 2)(lambda: place(3, far[1]))
     for k in range(4):
         lanes = slice(NB * k, NB * k + NB)
         part = dot_nt(wide[:, lanes], x_ref[NB * k:, lanes])
@@ -299,19 +303,19 @@
 
 
 def solve_rows(pieces, x):
-    own, y, z, top, bottom = pieces
+    own, y, z, *far = pieces
     rows = own.shape[0]
     tile = rows // 4
-    split = 2
     block = pl.BlockSpec((tile, NB), lambda i: (i, 0))
-    return call(
-        functools.partial(rows_kernel, split), 30 * rows * SUP * SUP // 4, 12 * rows * SUP, 34, grid=(4,),
+    far_blocks = [block] if len(far) == 1 else [
+        pl.BlockSpec((tile, NB), lambda i: (jnp.minimum(i, 1), 0)), pl.BlockSpec((tile, NB), lambda i: (jnp.maximum(i - 2, 0), 0))]
+    return call(
+        rows_kernel, 30 * rows * SUP * SUP // 4, 12 * rows * SUP, 34, grid=(4,),
         out_shape=(shape(rows, SUP), shape(rows, NB)),
-        in_specs=[block, block, block, pl.BlockSpec((tile, NB), lambda i: (jnp.minimum(i, split - 1), 0)),
-                  pl.BlockSpec((tile, NB), lambda i: (jnp.maximum(i - split, 0), 0)), pl.BlockSpec((SUP, SUP), lambda i: (0, 0))],
+        in_specs=[block] * 3 + far_blocks + [pl.BlockSpec((SUP, SUP), lambda i: (0, 0))],
         out_specs=(pl.BlockSpec((tile, SUP), lambda i: (i, 0)), block),
         scratch_shapes=[pltpu.VMEM((tile, SUP), F32)],
-    )(in_hbm(own), y, z, top, bottom, x)
+    )(in_hbm(own), y, z, *far, x)
 
 
 def cols_kernel(*refs):
@@ -347,9 +351,23 @@
 
 def panel_kernel(*refs):
     rest_ref, l_ref, u_ref, diag_ref, col_ref = refs[:5]
+    l_parts, u_parts = refs[-2:]
     keep = rest_ref.shape[1] - NB
-    new = rest_ref[...] - dot(l_ref[...], u_ref[...])
     i = pl.program_id(0)
+
+    @pl.when(i == 0)
+    def _():
+        def split_rows(k, carry):
+            at = pl.ds(pl.multiple_of(k * 64, 64), 64)
+            for n, part in enumerate(split3(u_ref[at, :])):
+                u_parts[n, at, :] = part
+            return carry
+
+        lax.fori_loop(0, SUP // 64, split_rows, 0)
+
+    for n, part in enumerate(split3(l_ref[...])):
+        l_parts[n] = part
+    new = rest_ref[...] - dot_parts(lambda n: l_parts[n], lambda n: u_parts[n])
 
     @pl.when(i == 0)
     def _():
@@ -374,9 +392,9 @@
     if keep:
         specs += [pl.BlockSpec((NB, keep), zero), pl.BlockSpec((NB, keep), below)]
     return call(
-        panel_kernel, 12 * rows * width * SUP, 8 * rows * width + 4 * rows * SUP, 20, grid=(rows // NB,), out_shape=outs,
+        panel_kernel, 12 * rows * width * SUP, 8 * rows * width + 4 * rows * SUP, 26, grid=(rows // NB,), out_shape=outs,
         in_specs=[pl.BlockSpec((NB, width), lambda i: (i, 0)), pl.BlockSpec((NB, SUP), lambda i: (i, 0)), pl.BlockSpec((SUP, width), zero)],
-        out_specs=specs,
+        out_specs=specs, scratch_shapes=[pltpu.VMEM((3, NB, SUP), BF16), pltpu.VMEM((3, SUP, width), BF16)],
     )(in_hbm(rest), in_hbm(l_rows), u_panel)
 
 
@@ -510,9 +528,9 @@
         out_cols, out_diags = [], []
         for step in range(4):
             if step == 0:
-                diag_block, later = lax.optimization_barrier((panel_tile[:NB, 0, :], panel_tile))
+                diag_block, later = lax.optimization_barrier((panel_tile[:NB, 0, :], panel_tile[:NB]))
                 blocks = gather_diag(diag_block)
-                col_panel = later[NB:, 0, :]
+                col_panel = panel_tile[NB:, 0, :]
                 keep, send = (lax.dynamic_slice(trail_tile, (0, SUP * h), (NB, SUP)) for h in (half, 1 - half))
                 panel_row = jnp.concatenate([later[:NB, s, :] for s in (3, 2, 1)], axis=1)
                 rest = unpack(panel_tile)
@@ -526,10 +544,12 @@
             if step:
                 source = trail if step == 1 else None
                 trail, = update_trail(core, trail, l_rows, mine, theirs, own_diag, step - 1)
-                blocks, y, z, trail = lax.optimization_barrier((blocks, y, z, trail))
-            split = col_panel.shape[0] // 2
-            top = lax.ppermute(z[:split], "pc", FLIP1)
-            bottom = lax.ppermute(y[split:], "pc", FLIP2)
+                blocks, trail = lax.optimization_barrier((blocks, trail))
+            if step:
+                far = [lax.ppermute(col_panel, "pc", FLIP3)]
+            else:
+                split = col_panel.shape[0] // 2
+                far = [lax.ppermute(z[:split], "pc", FLIP1), lax.ppermute(y[split:], "pc", FLIP2)]
             if step == 0:
                 x_sup, own_l, own_diag = factor(blocks)
             else:
@@ -538,7 +558,7 @@
             if step == 0:
                 more = solve_cols(row_pieces, x_sup)
             theirs = lax.ppermute(mine, "pr", FLIP1)
-            l_rows, own_col = solve_rows([col_panel, y, z, top, bottom], x_sup)
+            l_rows, own_col = solve_rows([col_panel, y, z, *far], x_sup)
             out_cols.append(own_col)
             out_diags.append(own_l)
             if step < 3:

time: 870 us -> 914 us (1.051)
  waiting for transfers between devices: 108 us -> 171 us
  local copies, waits for them, and re-layouts: 40.6 us -> 25.3 us
    ppermute x4, waiting for transfers between devices: 8.25 us -> 45 us  [local_part(): y = lax.ppermute(col_panel, 'pc', FLIP1)]
    ppermute x8 -> x5, waiting for transfers between devices: 24.9 us -> 48.8 us  [the longest x3 48.8 us: local_part(): far = [lax.ppermute(col_panel, 'pc', FLIP3)]]
    optimization_barrier x1, local copies, waits for them, and re-layouts: 11.8 us -> 0.2 us  [local_part(): lax.optimization_barrier((panel_tile[:NB, 0, :], panel_tile[:NB]))]
  transfers between devices with their start and end apart: 42 -> 39, of which waited for: 13 -> 11; matrix products, arithmetic and copies ran while one was open for 3% -> 1% of each run, Pallas kernels for 63% -> 61%
where the time goes in v3:
time: 914 us; the launch traced here: 910 us
  Pallas kernels  666 us (73%)
  waiting for transfers between devices  171 us (19%)
  starting transfers between devices  33 us (4%)
  local copies, waits for them, and re-layouts  25.3 us (3%)
  between operations  14.4 us (2%)
    pallas_call x4, Pallas kernels, update_trail(): call(trail_kernel, 12 * count * NB * cols * SUP, 8 * count * NB * cols, 3...  204 us
    pallas_call x3, Pallas kernels, factor_beside(): call(fused_kernel, 100000000000, 1 << 25, 48, grid=(4,), out_shape=(near(...  152 us
    pallas_call x4, Pallas kernels, solve_rows(): call(rows_kernel, 30 * rows * SUP * SUP // 4, 12 * rows * SUP, 34, grid=(...  98 us
    pallas_call x3, Pallas kernels, update_panel(): call(panel_kernel, 12 * rows * width * SUP, 8 * rows * width + 4 * rows *...  68.3 us
    pallas_call x5, Pallas kernels, solve_cols(): call(cols_kernel, 30 * cols * SUP * SUP // 4, 12 * cols * SUP, 20, grid=(...  64.9 us
    ppermute x3, waiting for transfers between devices, local_part(): far = [lax.ppermute(col_panel, 'pc', FLIP3)]  48.8 us
    ppermute x4, waiting for transfers between devices, local_part(): y = lax.ppermute(col_panel, 'pc', FLIP1)  45 us
    pallas_call x3, Pallas kernels, update_row(): call(row_kernel, 24 * NB * SUP * SUP, 12 * SUP * SUP, 30, grid_spec=pltpu...  37.6 us
  transfers between devices with their start and end apart: 39, of which 11 were waited for; matrix products, arithmetic and copies ran while one was open for 1% of the time, Pallas kernels for 61%

profile of v3, /device:TPU:0, one launch (start us, length us, event | category | flops | bytes accessed | tf_op | source)
XLA Modules:
  0.0 910.3 jit_solution(9415611603013872626)
XLA Ops:
  9.0 3.3 collective-permute-start.4
  12.2 6.3 collective-permute-done.4
  18.6 1.8 collective-permute-start.5
  20.4 6.5 slice.24
  26.9 1.7 copy.20
  28.8 4.4 collective-permute-done.5
  34.8 1.5 collective-permute-start
  36.3 19.0 %collective-permute-done.6 = f32[4,256,256]{2,1,0:T(8,128)S(1)} collective-permute-done((f32[4,256,256]{2,1,0:T(8,128)S(1)}, f32[4,256,256]{2,1,0:T(8,128)S(1)}, u32[]{:S(2)}, u32[]{:S(2)}) %collective-permute-start.6) | collective-permute-done | bytes 1048608 | tf_op jit(solution)/shard_map/ppermute | solution.py:508
  55.6 1.8 constant_dynamic-slice_fusion
  59.1 34.4 %collective-permute-done.1.refs_2_ = f32[2816,256]{1,0:T(8,128)} collective-permute-done((f32[2816,256]{1,0:T(8,128)}, f32[2816,256]{1,0:T(8,128)}, u32[]{:S(2)}, u32[]{:S(2)}) %collective-permute-start.1) | collective-permute-done | bytes 2883616 | tf_op jit(solution)/shard_map/ppermute | solution.py:540
  95.0 4.6 copy-done
  99.6 6.2 shard_map.41.refs_0_
  108.7 2.8 collective-permute-done.9.refs_2_
  111.6 1.6 collective-permute-start.10
  113.2 1.5 collective-permute-start.2
  115.8 34.5 %shard_map.42 = (f32[1024,1024]{1,0:T(8,128)S(1)}, f32[256,256]{1,0:T(8,128)}, f32[256,256]{1,0:T(8,128)}) custom-call(f32[8,256,256]{2,1,0:T(8,128)S(1)} %pad_maximum_fusion.refs_0_, f32[8,256,256]{2,1,0:T(8,128)} %collective-permute-done.7.refs_1_), custom_call_target="tpu_custom_call" | custom-call | flops 30000001024 | bytes 16777216 | tf_op jit(solution)/shard_map/pallas_call | solution.py:170
  150.4 11.5 %shard_map.46.mine_ref.refs_3_ = f32[1024,1024]{1,0:T(8,128)} custom-call(f32[256,1024]{1,0:T(8,128)S(1)} %get-tuple-element.109.refs_0_, f32[256,1024]{1,0:T(8,128)S(1)} %collective-permute-done.14.refs_1_, f32[256,1024]{1,0:T(8,128)S(1)} %collective-permute-done.15.refs_2_, f32[256,1024]{1,0:T(8,128)S(1)} %collective-permute-done.16.refs_3_, ...), custom_call_target="tpu_custom_call" | custom-call | flops 8053063680 | bytes 12582912 | tf_op jit(solution)/shard_map/pallas_call | solution.py:345
  161.9 8.8 shard_map.44.refs_2_
  170.7 28.2 %shard_map.43 = (f32[2816,1024]{1,0:T(8,128)}, f32[2816,256]{1,0:T(8,128)}) custom-call(f32[2816,256]{1,0:T(8,128)} %bitcast.25.refs_0_, f32[2816,256]{1,0:T(8,128)} %collective-permute-done.refs_1_, f32[2816,256]{1,0:T(8,128)} %collective-permute-done.1.refs_2_, f32[1408,256]{1,0:T(8,128)S(1)} %collective-permute-done.2.refs_3_, ...), custom_call_target="tpu_custom_call" | custom-call | flops 22145925120 | bytes 34603008 | tf_op jit(solution)/shard_map/pallas_call | solution.py:312
  199.0 33.7 %shard_map.45 = (f32[256,256]{1,0:T(8,128)}, f32[2560,256]{1,0:T(8,128)}, f32[256,512]{1,0:T(8,128)}, f32[2560,512]{1,0:T(8,128)}) custom-call(f32[2816,768]{1,0:T(8,128)} %shard_map.41.refs_0_, f32[2816,1024]{1,0:T(8,128)} %get-tuple-element.57.refs_1_.l_ref.refs_2_, f32[1024,768]{1,0:T(8,128)S(1)} %copy-done.6), custom_call_target="tpu_custom_call" | custom-call | flops 26575110144 | bytes 28835840 | tf_op jit(solution)/shard_map/pallas_call | solution.py:394
  234.2 2.1 collective-permute-start.13
  237.3 12.8 %shard_map.50 = (f32[256,1536]{1,0:T(8,128)}, f32[256,1536]{1,0:T(8,128)}) custom-call(s32[1]{0:T(128)} %bitcast.core_ref.refs_0_, f32[3072,2048]{1,0:T(8,128)} %refs_1_.1, f32[2816,1024]{1,0:T(8,128)} %get-tuple-element.57.refs_1_.l_ref.refs_2_, f32[1024,1024]{1,0:T(8,128)} %shard_map.46.mine_ref.refs_3_, ...), custom_call_target="tpu_custom_call" | custom-call | flops 6442450944 | bytes 12582912 | tf_op jit(solution)/shard_map/pallas_call | solution.py:433
  250.8 51.0 %shard_map.47.rest_0_ = f32[3072,2048]{1,0:T(8,128)} custom-call(s32[1]{0:T(128)} %bitcast.core_ref.refs_0_, f32[3072,2048]{1,0:T(8,128)} %refs_1_.1, f32[2816,1024]{1,0:T(8,128)} %get-tuple-element.57.refs_1_.l_ref.refs_2_, f32[1024,1024]{1,0:T(8,128)} %shard_map.46.mine_ref.refs_3_, f32[1024,1024]{1,0:T(8,128)} %collective-permute-done.17.theirs_ref.refs_4_, ...), custom_call_target="tpu_custom_call" | custom-call | flops 45097156608 | bytes 29360128 | tf_op jit(solution)/shard_map/pallas_call | solution.py:492
  303.4 50.8 %shard_map.48 = (f32[1024,1024]{1,0:T(8,128)S(1)}, f32[256,256]{1,0:T(8,128)}, f32[256,256]{1,0:T(8,128)}, f32[3072,2048]{1,0:T(8,128)}) custom-call(f32[16,256,256]{2,1,0:T(8,128)} %bitcast.32, f32[3072,2048]{1,0:T(8,128)} %refs_1_.1, f32[2816,1024]{1,0:T(8,128)} %get-tuple-element.57.refs_1_.l_ref.refs_2_, ...), custom_call_target="tpu_custom_call", output_to_operand_aliasing={{3}: (5, {})} | custom-call | flops 99999997952 | bytes 33554432 | tf_op jit(solution)/shard_map/pallas_call | solution.py:249
  354.2 18.0 %shard_map.51 = (f32[1024,1024]{1,0:T(8,128)}, f32[1024,512]{1,0:T(8,128)S(1)}) custom-call(f32[256,1536]{1,0:T(8,128)S(1)} %copy-done.3, f32[256,1536]{1,0:T(8,128)S(1)} %collective-permute-done.18.refs_1_, f32[256,1536]{1,0:T(8,128)S(1)} %collective-permute-done.19.refs_2_, f32[256,1536]{1,0:T(8,128)} %collective-permute-done.20.refs_3_, ...), custom_call_target="tpu_custom_call" | custom-call | flops 12079595520 | bytes 18874368 | tf_op jit(solution)/shard_map/pallas_call | solution.py:345
  372.2 25.7 %shard_map.49 = (f32[2560,1024]{1,0:T(8,128)}, f32[2560,256]{1,0:T(8,128)}) custom-call(f32[2560,256]{1,0:T(8,128)} %get-tuple-element.60.refs_0_, f32[2560,256]{1,0:T(8,128)} %collective-permute-done.11.refs_1_, f32[2560,256]{1,0:T(8,128)} %collective-permute-done.12.refs_2_, f32[2560,256]{1,0:T(8,128)} %collective-permute-done.13.refs_3_, ...), custom_call_target="tpu_custom_call" | custom-call | flops 20132659200 | bytes 31457280 | tf_op jit(solution)/shard_map/pallas_call | solution.py:312
  397.9 21.5 %shard_map.52 = (f32[256,256]{1,0:T(8,128)}, f32[2304,256]{1,0:T(8,128)}, f32[256,256]{1,0:T(8,128)}, f32[2304,256]{1,0:T(8,128)}) custom-call(f32[2560,512]{1,0:T(8,128)} %get-tuple-element.59.refs_0_, f32[2560,1024]{1,0:T(8,128)} %get-tuple-element.66.refs_1_.l_ref.refs_2_, f32[1024,512]{1,0:T(8,128)S(1)} %get-tuple-element.70.refs_2_), custom_call_target="tpu_custom_call" | custom-call | flops 16106127360 | bytes 20971520 | tf_op jit(solution)/shard_map/pallas_call | solution.py:394
  421.0 2.0 collective-permute-start.23
  424.0 12.6 %shard_map.56 = (f32[256,1280]{1,0:T(8,128)}, f32[256,1280]{1,0:T(8,128)}) custom-call(s32[1]{0:T(128)} %bitcast.core_ref.refs_0_, f32[3072,2048]{1,0:T(8,128)} %get-tuple-element.74.trail_ref.refs_1_, f32[2560,1024]{1,0:T(8,128)} %get-tuple-element.66.refs_1_.l_ref.refs_2_, f32[1024,1024]{1,0:T(8,128)} %get-tuple-element.75.mine_ref.refs_3_, ...), custom_call_target="tpu_custom_call" | custom-call | flops 6442450944 | bytes 12582912 | tf_op jit(solution)/shard_map/pallas_call | solution.py:433
  437.4 43.9 %shard_map.53.trail_ref = f32[3072,2048]{1,0:T(8,128)} custom-call(s32[1]{0:T(128)} %bitcast.core_ref.refs_0_, f32[3072,2048]{1,0:T(8,128)} %get-tuple-element.74.trail_ref.refs_1_, f32[2560,1024]{1,0:T(8,128)} %get-tuple-element.66.refs_1_.l_ref.refs_2_, f32[1024,1024]{1,0:T(8,128)} %get-tuple-element.75.mine_ref.refs_3_, ...), custom_call_target="tpu_custom_call", output_to_operand_aliasing={{}: (1, {})} | custom-call | flops 38654705664 | bytes 25165824 | tf_op jit(solution)/shard_map/pallas_call | solution.py:492
  481.3 50.9 %shard_map.54 = (f32[1024,1024]{1,0:T(8,128)S(1)}, f32[256,256]{1,0:T(8,128)}, f32[256,256]{1,0:T(8,128)}, f32[3072,2048]{1,0:T(8,128)}) custom-call(f32[16,256,256]{2,1,0:T(8,128)} %bitcast.33, f32[3072,2048]{1,0:T(8,128)} %shard_map.53.trail_ref, f32[2560,1024]{1,0:T(8,128)} %get-tuple-element.66.refs_1_.l_ref.refs_2_, ...), custom_call_target="tpu_custom_call", output_to_operand_aliasing={{3}: (1, {})} | custom-call | flops 99999997952 | bytes 33554432 | tf_op jit(solution)/shard_map/pallas_call | solution.py:249
  533.7 3.8 collective-permute-done.23.refs_3_
  537.5 23.4 %shard_map.55 = (f32[2304,1024]{1,0:T(8,128)}, f32[2304,256]{1,0:T(8,128)}) custom-call(f32[2304,256]{1,0:T(8,128)} %get-tuple-element.72.refs_0_, f32[2304,256]{1,0:T(8,128)} %collective-permute-done.21.refs_1_, f32[2304,256]{1,0:T(8,128)} %collective-permute-done.22.refs_2_, f32[2304,256]{1,0:T(8,128)} %collective-permute-done.23.refs_3_, ...), custom_call_target="tpu_custom_call" | custom-call | flops 18119393280 | bytes 28311552 | tf_op jit(solution)/shard_map/pallas_call | solution.py:312
  560.9 2.2 collective-permute-done.26.refs_2_
  563.1 15.1 %shard_map.57 = (f32[1024,1024]{1,0:T(8,128)}, f32[1024,256]{1,0:T(8,128)S(1)}) custom-call(f32[256,1280]{1,0:T(8,128)S(1)} %copy-done.4, f32[256,1280]{1,0:T(8,128)} %collective-permute-done.25.refs_1_, f32[256,1280]{1,0:T(8,128)S(1)} %collective-permute-done.26.refs_2_, f32[256,1280]{1,0:T(8,128)} %collective-permute-done.27.refs_3_, ...), custom_call_target="tpu_custom_call" | custom-call | flops 10066329600 | bytes 15728640 | tf_op jit(solution)/shard_map/pallas_call | solution.py:345
  578.2 13.2 %shard_map.58 = (f32[256,256]{1,0:T(8,128)}, f32[2048,256]{1,0:T(8,128)}) custom-call(f32[2304,256]{1,0:T(8,128)} %get-tuple-element.71.refs_0_, f32[2304,1024]{1,0:T(8,128)} %get-tuple-element.80.refs_1_.l_ref.refs_2_, f32[1024,256]{1,0:T(8,128)S(1)} %get-tuple-element.84.refs_2_), custom_call_target="tpu_custom_call" | custom-call | flops 7247757312 | bytes 14155776 | tf_op jit(solution)/shard_map/pallas_call | solution.py:394
  591.4 7.4 collective-permute-done.28.theirs_ref.refs_4_
  598.8 2.1 copy-done.7
  600.9 12.2 %shard_map.62 = (f32[256,1024]{1,0:T(8,128)}, f32[256,1024]{1,0:T(8,128)}) custom-call(s32[1]{0:T(128)} %bitcast.core_ref.refs_0_, f32[3072,2048]{1,0:T(8,128)} %get-tuple-element.86.trail_ref.refs_1_, f32[2304,1024]{1,0:T(8,128)} %get-tuple-element.80.refs_1_.l_ref.refs_2_, f32[1024,1024]{1,0:T(8,128)} %get-tuple-element.87.mine_ref.refs_3_, ...), custom_call_target="tpu_custom_call" | custom-call | flops 6442450944 | bytes 12582912 | tf_op jit(solution)/shard_map/pallas_call | solution.py:433
  615.3 37.0 %shard_map.59.trail_ref = f32[3072,2048]{1,0:T(8,128)} custom-call(s32[1]{0:T(128)} %bitcast.core_ref.refs_0_, f32[3072,2048]{1,0:T(8,128)} %get-tuple-element.86.trail_ref.refs_1_, f32[2304,1024]{1,0:T(8,128)} %get-tuple-element.80.refs_1_.l_ref.refs_2_, f32[1024,1024]{1,0:T(8,128)} %get-tuple-element.87.mine_ref.refs_3_, ...), custom_call_target="tpu_custom_call", output_to_operand_aliasing={{}: (1, {})} | custom-call | flops 32212254720 | bytes 20971520 | tf_op jit(solution)/shard_map/pallas_call | solution.py:492
  652.3 50.7 %shard_map.60 = (f32[1024,1024]{1,0:T(8,128)S(1)}, f32[256,256]{1,0:T(8,128)}, f32[256,256]{1,0:T(8,128)}, f32[3072,2048]{1,0:T(8,128)}) custom-call(f32[16,256,256]{2,1,0:T(8,128)} %bitcast.34, f32[3072,2048]{1,0:T(8,128)} %shard_map.59.trail_ref, f32[2304,1024]{1,0:T(8,128)} %get-tuple-element.80.refs_1_.l_ref.refs_2_, ...), custom_call_target="tpu_custom_call", output_to_operand_aliasing={{3}: (1, {})} | custom-call | flops 99999997952 | bytes 33554432 | tf_op jit(solution)/shard_map/pallas_call | solution.py:249
  703.1 11.4 %shard_map.63.mine_ref = f32[1024,1024]{1,0:T(8,128)} custom-call(f32[256,1024]{1,0:T(8,128)S(1)} %copy-done.5, f32[256,1024]{1,0:T(8,128)S(1)} %collective-permute-done.32.refs_1_, f32[256,1024]{1,0:T(8,128)S(1)} %collective-permute-done.33.refs_2_, f32[256,1024]{1,0:T(8,128)S(1)} %collective-permute-done.34.refs_3_, f32[1024,1024]{1,0:T(8,128)S(1)} %get-tuple-element.93.refs_4_), custom_call_target="tpu_custom_call" | custom-call | flops 8053063680 | bytes 12582912 | tf_op jit(solution)/shard_map/pallas_call | solution.py:345
  716.1 1.9 collective-permute-start.31
  718.0 45.0 %collective-permute-done.29.refs_1_ = f32[2048,256]{1,0:T(8,128)S(1)} collective-permute-done((f32[2048,256]{1,0:T(8,128)S(1)}, f32[2048,256]{1,0:T(8,128)S(1)}, u32[]{:S(2)}, u32[]{:S(2)}) %collective-permute-start.29) | collective-permute-done | bytes 2097184 | tf_op jit(solution)/shard_map/ppermute | solution.py:539
  763.4 45.0 %collective-permute-done.31.refs_3_ = f32[2048,256]{1,0:T(8,128)S(1)} collective-permute-done((f32[2048,256]{1,0:T(8,128)S(1)}, f32[2048,256]{1,0:T(8,128)S(1)}, u32[]{:S(2)}, u32[]{:S(2)}) %collective-permute-start.31) | collective-permute-done | bytes 2097184 | tf_op jit(solution)/shard_map/ppermute | solution.py:549
  808.4 20.6 %shard_map.61 = (f32[2048,1024]{1,0:T(8,128)}, f32[2048,256]{1,0:T(8,128)}) custom-call(f32[2048,256]{1,0:T(8,128)} %get-tuple-element.92.refs_0_, f32[2048,256]{1,0:T(8,128)S(1)} %collective-permute-done.29.refs_1_, f32[2048,256]{1,0:T(8,128)S(1)} %collective-permute-done.30.refs_2_, f32[2048,256]{1,0:T(8,128)S(1)} %collective-permute-done.31.refs_3_, ...), custom_call_target="tpu_custom_call" | custom-call | flops 16106127360 | bytes 25165824 | tf_op jit(solution)/shard_map/pallas_call | solution.py:312
  829.1 1.9 copy-done.8
  831.0 72.5 %shard_map.64 = (f32[3072,2048]{1,0:T(8,128)}, f32[24576,128]{1,0:T(8,128)}) custom-call(s32[1]{0:T(128)} %bitcast.core_ref.refs_0_, f32[3072,2048]{1,0:T(8,128)} %get-tuple-element.91.trail_ref, f32[2048,1024]{1,0:T(8,128)} %get-tuple-element.94.l_ref, f32[1024,1024]{1,0:T(8,128)} %shard_map.63.mine_ref, ...), custom_call_target="tpu_custom_call", output_to_operand_aliasing={{0}: (1, {})} | custom-call | flops 57982058496 | bytes 37748736 | tf_op jit(solution)/shard_map/pallas_call | solution.py:492
  (92 shorter events, 24.9 us)
Async XLA Ops:
  7.2 1.6 slice-start
  7.2 294.7 %all-gather.7.cloned.1.call-start = ((), (), s32[]{:S(2)}) async-start(), calls=%async_computation | async-start | bytes 4456448 | tf_op jit(solution)/shard_map/all_gather | solution.py:538
  9.0 9.6 %collective-permute-start.4 = (f32[1,256,256]{2,1,0:T(8,128)S(1)}, f32[1,256,256]{2,1,0:T(8,128)S(1)}, u32[]{:S(2)}, u32[]{:S(2)}) collective-permute-start(f32[1,256,256]{2,1,0:T(8,128)S(1)} %bitcast.28), channel_id=1, source_target_pairs={{0,4},{4,0},{8,12},{12,8},{1,5},{5,1},{9,13},{13,9},{2,6},{6,2},{1... | collective-permute-start | bytes 786440 | tf_op jit(solution)/shard_map/ppermute | solution.py:508
  18.6 14.7 %collective-permute-start.5 = (f32[2,256,256]{2,1,0:T(8,128)S(1)}, f32[2,256,256]{2,1,0:T(8,128)S(1)}, u32[]{:S(2)}, u32[]{:S(2)}) collective-permute-start(f32[2,256,256]{2,1,0:T(8,128)S(1)} %pad_maximum_fusion.3), channel_id=1, source_target_pairs={{0,8},{8,0},{4,12},{12,4},{1,9},{9,1},{5,13},{13,5},{2,10},{10,2},... | collective-permute-start | bytes 1572872 | tf_op jit(solution)/shard_map/ppermute | solution.py:508
  28.6 65.0 %collective-permute-start.1 = (f32[2816,256]{1,0:T(8,128)}, f32[2816,256]{1,0:T(8,128)}, u32[]{:S(2)}, u32[]{:S(2)}) collective-permute-start(f32[2816,256]{1,0:T(8,128)} %bitcast.25.refs_0_), channel_id=1, source_target_pairs={{0,8},{8,0},{4,12},{12,4},{1,9},{9,1},{5,13},{13,5},{2,10},{10,2},... | collective-permute-start | bytes 8650760 | tf_op jit(solution)/shard_map/ppermute | solution.py:540
  33.4 21.9 %collective-permute-start.6 = (f32[4,256,256]{2,1,0:T(8,128)S(1)}, f32[4,256,256]{2,1,0:T(8,128)S(1)}, u32[]{:S(2)}, u32[]{:S(2)}) collective-permute-start(f32[4,256,256]{2,1,0:T(8,128)S(1)} %pad_maximum_fusion.1), channel_id=1, source_target_pairs={{0,2},{2,0},{1,3},{3,1},{4,6},{6,4},{5,7},{7,5},{8,10},{10,8},{9,1... | collective-permute-start | bytes 3145736 | tf_op jit(solution)/shard_map/ppermute | solution.py:508
  34.8 72.5 %collective-permute-start = (f32[2816,256]{1,0:T(8,128)}, f32[2816,256]{1,0:T(8,128)}, u32[]{:S(2)}, u32[]{:S(2)}) collective-permute-start(f32[2816,256]{1,0:T(8,128)} %bitcast.25.refs_0_), channel_id=1, source_target_pairs={{0,4},{4,0},{8,12},{12,8},{1,5},{5,1},{9,13},{13,9},{2,6},{6,2},{1... | collective-permute-start | bytes 8650760 | tf_op jit(solution)/shard_map/ppermute | solution.py:539
  55.5 59.2 %collective-permute-start.7 = (f32[8,256,256]{2,1,0:T(8,128)S(1)}, f32[8,256,256]{2,1,0:T(8,128)}, u32[]{:S(2)}, u32[]{:S(2)}) collective-permute-start(f32[8,256,256]{2,1,0:T(8,128)S(1)} %pad_maximum_fusion.refs_0_), channel_id=1, source_target_pairs={{0,1},{1,0},{2,3},{3,2},{4,5},{5,4},{6,7},{7,6},{8,9},{9,8},{10,11... | collective-permute-start | bytes 6291464 | tf_op jit(solution)/shard_map/ppermute | solution.py:509
  57.4 54.2 %collective-permute-start.14 = (f32[256,1024]{1,0:T(8,128)S(1)}, f32[256,1024]{1,0:T(8,128)S(1)}, u32[]{:S(2)}, u32[]{:S(2)}) collective-permute-start(f32[256,1024]{1,0:T(8,128)S(1)} %get-tuple-element.108), channel_id=1, source_target_pairs={{0,1},{1,0},{2,3},{3,2},{4,5},{5,4},{6,7},{7,6},{8,9},{9,8},{10,11... | collective-permute-start | bytes 3145736 | tf_op jit(solution)/shard_map/ppermute | solution.py:513
  57.9 55.3 %collective-permute-start.15 = (f32[256,1024]{1,0:T(8,128)S(1)}, f32[256,1024]{1,0:T(8,128)S(1)}, u32[]{:S(2)}, u32[]{:S(2)}) collective-permute-start(f32[256,1024]{1,0:T(8,128)S(1)} %get-tuple-element.109.refs_0_), channel_id=1, source_target_pairs={{0,2},{2,0},{1,3},{3,1},{4,6},{6,4},{5,7},{7,5},{8,10},{10,8},{9,1... | collective-permute-start | bytes 3145736 | tf_op jit(solution)/shard_map/ppermute | solution.py:513
  93.6 18.0 %collective-permute-start.9 = (f32[256,768]{1,0:T(8,128)S(1)}, f32[256,768]{1,0:T(8,128)S(1)}, u32[]{:S(2)}, u32[]{:S(2)}) collective-permute-start(f32[256,768]{1,0:T(8,128)S(1)} %pad_maximum_fusion.2.refs_0_), channel_id=1, source_target_pairs={{0,2},{2,0},{1,3},{3,1},{4,6},{6,4},{5,7},{7,5},{8,10},{10,8},{9,1... | collective-permute-start | bytes 2359304 | tf_op jit(solution)/shard_map/ppermute | solution.py:517
  95.0 4.6 copy-start
  107.2 54.6 %collective-permute-start.8 = (f32[256,768]{1,0:T(8,128)S(1)}, f32[256,768]{1,0:T(8,128)S(1)}, u32[]{:S(2)}, u32[]{:S(2)}) collective-permute-start(f32[256,768]{1,0:T(8,128)S(1)} %pad_maximum_fusion.2.refs_0_), channel_id=1, source_target_pairs={{0,1},{1,0},{2,3},{3,2},{4,5},{5,4},{6,7},{7,6},{8,9},{9,8},{10,11... | collective-permute-start | bytes 2359304 | tf_op jit(solution)/shard_map/ppermute | solution.py:518
  111.6 38.8 %collective-permute-start.16 = (f32[256,1024]{1,0:T(8,128)S(1)}, f32[256,1024]{1,0:T(8,128)S(1)}, u32[]{:S(2)}, u32[]{:S(2)}) collective-permute-start(f32[256,1024]{1,0:T(8,128)S(1)} %get-tuple-element.108), channel_id=1, source_target_pairs={{0,3},{3,0},{1,2},{2,1},{4,7},{7,4},{5,6},{6,5},{8,11},{11,8},{9,1... | collective-permute-start | bytes 3145736 | tf_op jit(solution)/shard_map/ppermute | solution.py:513
  111.6 50.3 %collective-permute-start.10 = (f32[256,768]{1,0:T(8,128)S(1)}, f32[256,768]{1,0:T(8,128)S(1)}, u32[]{:S(2)}, u32[]{:S(2)}) collective-permute-start(f32[256,768]{1,0:T(8,128)S(1)} %collective-permute-done.9.refs_2_), channel_id=1, source_target_pairs={{0,1},{1,0},{2,3},{3,2},{4,5},{5,4},{6,7},{7,6},{8,9},{9,8},{10,11... | collective-permute-start | bytes 2359304 | tf_op jit(solution)/shard_map/ppermute | solution.py:519
  113.2 57.5 %collective-permute-start.2 = (f32[1408,256]{1,0:T(8,128)S(1)}, f32[1408,256]{1,0:T(8,128)S(1)}, u32[]{:S(2)}, u32[]{:S(2)}) collective-permute-start(f32[1408,256]{1,0:T(8,128)S(1)} %slice.32), channel_id=1, source_target_pairs={{0,4},{4,0},{8,12},{12,8},{1,5},{5,1},{9,13},{13,9},{2,6},{6,2},{1... | collective-permute-start | bytes 4325384 | tf_op jit(solution)/shard_map/ppermute | solution.py:552
  114.7 56.0 %collective-permute-start.3 = (f32[1408,256]{1,0:T(8,128)S(1)}, f32[1408,256]{1,0:T(8,128)S(1)}, u32[]{:S(2)}, u32[]{:S(2)}) collective-permute-start(f32[1408,256]{1,0:T(8,128)S(1)} %slice.33), channel_id=1, source_target_pairs={{0,8},{8,0},{4,12},{12,4},{1,9},{9,1},{5,13},{13,5},{2,10},{10,2},... | collective-permute-start | bytes 4325384 | tf_op jit(solution)/shard_map/ppermute | solution.py:552
  161.9 74.4 %collective-permute-start.17 = (f32[1024,1024]{1,0:T(8,128)}, f32[1024,1024]{1,0:T(8,128)}, u32[]{:S(2)}, u32[]{:S(2)}) collective-permute-start(f32[1024,1024]{1,0:T(8,128)} %shard_map.46.mine_ref.refs_3_), channel_id=1, source_target_pairs={{0,1},{1,0},{2,3},{3,2},{4,5},{5,4},{6,7},{7,6},{8,9},{9,8},{10,11... | collective-permute-start | bytes 12582920 | tf_op jit(solution)/shard_map/ppermute | solution.py:560
  170.7 28.3 %copy-start.6 = (f32[1024,768]{1,0:T(8,128)S(1)}, f32[1024,768]{1,0:T(8,128)}, u32[]{:S(2)}) copy-start(f32[1024,768]{1,0:T(8,128)} %shard_map.44.refs_2_) | copy-start | bytes 9437188
  232.6 248.7 %all-gather.9.cloned.1.call-start = ((), (), s32[]{:S(2)}) async-start(), calls=%async_computation.1 | async-start | bytes 4456448 | tf_op jit(solution)/shard_map/all_gather | solution.py:538
  232.7 139.5 %collective-permute-start.11 = (f32[2560,256]{1,0:T(8,128)}, f32[2560,256]{1,0:T(8,128)}, u32[]{:S(2)}, u32[]{:S(2)}) collective-permute-start(f32[2560,256]{1,0:T(8,128)} %get-tuple-element.60.refs_0_), channel_id=1, source_target_pairs={{0,4},{4,0},{8,12},{12,8},{1,5},{5,1},{9,13},{13,9},{2,6},{6,2},{1... | collective-permute-start | bytes 7864328 | tf_op jit(solution)/shard_map/ppermute | solution.py:539
  233.2 138.9 %collective-permute-start.12 = (f32[2560,256]{1,0:T(8,128)}, f32[2560,256]{1,0:T(8,128)}, u32[]{:S(2)}, u32[]{:S(2)}) collective-permute-start(f32[2560,256]{1,0:T(8,128)} %get-tuple-element.60.refs_0_), channel_id=1, source_target_pairs={{0,8},{8,0},{4,12},{12,4},{1,9},{9,1},{5,13},{13,5},{2,10},{10,2},... | collective-permute-start | bytes 7864328 | tf_op jit(solution)/shard_map/ppermute | solution.py:540
  234.2 138.0 %collective-permute-start.13 = (f32[2560,256]{1,0:T(8,128)}, f32[2560,256]{1,0:T(8,128)}, u32[]{:S(2)}, u32[]{:S(2)}) collective-permute-start(f32[2560,256]{1,0:T(8,128)} %get-tuple-element.60.refs_0_), channel_id=1, source_target_pairs={{0,12},{12,0},{4,8},{8,4},{1,13},{13,1},{5,9},{9,5},{2,14},{14,2},... | collective-permute-start | bytes 7864328 | tf_op jit(solution)/shard_map/ppermute | solution.py:549
  250.1 51.8 %collective-permute-start.18 = (f32[256,1536]{1,0:T(8,128)}, f32[256,1536]{1,0:T(8,128)S(1)}, u32[]{:S(2)}, u32[]{:S(2)}) collective-permute-start(f32[256,1536]{1,0:T(8,128)} %get-tuple-element.69), channel_id=1, source_target_pairs={{0,1},{1,0},{2,3},{3,2},{4,5},{5,4},{6,7},{7,6},{8,9},{9,8},{10,11... | collective-permute-start | bytes 4718600 | tf_op jit(solution)/shard_map/ppermute | solution.py:513
  250.1 104.0 %collective-permute-start.20 = (f32[256,1536]{1,0:T(8,128)}, f32[256,1536]{1,0:T(8,128)}, u32[]{:S(2)}, u32[]{:S(2)}) collective-permute-start(f32[256,1536]{1,0:T(8,128)} %get-tuple-element.69), channel_id=1, source_target_pairs={{0,3},{3,0},{1,2},{2,1},{4,7},{7,4},{5,6},{6,5},{8,11},{11,8},{9,1... | collective-permute-start | bytes 4718600 | tf_op jit(solution)/shard_map/ppermute | solution.py:513
  250.8 51.1 %copy-start.3 = (f32[256,1536]{1,0:T(8,128)S(1)}, f32[256,1536]{1,0:T(8,128)}, u32[]{:S(2)}) copy-start(f32[256,1536]{1,0:T(8,128)} %get-tuple-element.68.refs_0_) | copy-start | bytes 4718596
  301.9 52.3 %collective-permute-start.19 = (f32[256,1536]{1,0:T(8,128)S(1)}, f32[256,1536]{1,0:T(8,128)S(1)}, u32[]{:S(2)}, u32[]{:S(2)}) collective-permute-start(f32[256,1536]{1,0:T(8,128)S(1)} %copy-done.3), channel_id=1, source_target_pairs={{0,2},{2,0},{1,3},{3,1},{4,6},{6,4},{5,7},{7,5},{8,10},{10,8},{9,1... | collective-permute-start | bytes 4718600 | tf_op jit(solution)/shard_map/ppermute | solution.py:513
  372.2 50.9 %collective-permute-start.24 = (f32[1024,1024]{1,0:T(8,128)}, f32[1024,1024]{1,0:T(8,128)}, u32[]{:S(2)}, u32[]{:S(2)}) collective-permute-start(f32[1024,1024]{1,0:T(8,128)} %get-tuple-element.75.mine_ref.refs_3_), channel_id=1, source_target_pairs={{0,1},{1,0},{2,3},{3,2},{4,5},{5,4},{6,7},{7,6},{8,9},{9,8},{10,11... | collective-permute-start | bytes 12582920 | tf_op jit(solution)/shard_map/ppermute | solution.py:560
  419.5 232.8 %all-gather.11.cloned.1.call-start = ((), (), s32[]{:S(2)}) async-start(), calls=%async_computation.2 | async-start | bytes 4456448 | tf_op jit(solution)/shard_map/all_gather | solution.py:538
  419.5 112.8 %collective-permute-start.21 = (f32[2304,256]{1,0:T(8,128)}, f32[2304,256]{1,0:T(8,128)}, u32[]{:S(2)}, u32[]{:S(2)}) collective-permute-start(f32[2304,256]{1,0:T(8,128)} %get-tuple-element.72.refs_0_), channel_id=1, source_target_pairs={{0,4},{4,0},{8,12},{12,8},{1,5},{5,1},{9,13},{13,9},{2,6},{6,2},{1... | collective-permute-start | bytes 7077896 | tf_op jit(solution)/shard_map/ppermute | solution.py:539
  420.1 113.6 %collective-permute-start.22 = (f32[2304,256]{1,0:T(8,128)}, f32[2304,256]{1,0:T(8,128)}, u32[]{:S(2)}, u32[]{:S(2)}) collective-permute-start(f32[2304,256]{1,0:T(8,128)} %get-tuple-element.72.refs_0_), channel_id=1, source_target_pairs={{0,8},{8,0},{4,12},{12,4},{1,9},{9,1},{5,13},{13,5},{2,10},{10,2},... | collective-permute-start | bytes 7077896 | tf_op jit(solution)/shard_map/ppermute | solution.py:540
  421.0 116.5 %collective-permute-start.23 = (f32[2304,256]{1,0:T(8,128)}, f32[2304,256]{1,0:T(8,128)}, u32[]{:S(2)}, u32[]{:S(2)}) collective-permute-start(f32[2304,256]{1,0:T(8,128)} %get-tuple-element.72.refs_0_), channel_id=1, source_target_pairs={{0,12},{12,0},{4,8},{8,4},{1,13},{13,1},{5,9},{9,5},{2,14},{14,2},... | collective-permute-start | bytes 7077896 | tf_op jit(solution)/shard_map/ppermute | solution.py:549
  436.6 124.3 %collective-permute-start.25 = (f32[256,1280]{1,0:T(8,128)}, f32[256,1280]{1,0:T(8,128)}, u32[]{:S(2)}, u32[]{:S(2)}) collective-permute-start(f32[256,1280]{1,0:T(8,128)} %get-tuple-element.83), channel_id=1, source_target_pairs={{0,1},{1,0},{2,3},{3,2},{4,5},{5,4},{6,7},{7,6},{8,9},{9,8},{10,11... | collective-permute-start | bytes 3932168 | tf_op jit(solution)/shard_map/ppermute | solution.py:513
  436.7 126.4 %collective-permute-start.27 = (f32[256,1280]{1,0:T(8,128)}, f32[256,1280]{1,0:T(8,128)}, u32[]{:S(2)}, u32[]{:S(2)}) collective-permute-start(f32[256,1280]{1,0:T(8,128)} %get-tuple-element.83), channel_id=1, source_target_pairs={{0,3},{3,0},{1,2},{2,1},{4,7},{7,4},{5,6},{6,5},{8,11},{11,8},{9,1... | collective-permute-start | bytes 3932168 | tf_op jit(solution)/shard_map/ppermute | solution.py:513
  481.3 51.0 %copy-start.4 = (f32[256,1280]{1,0:T(8,128)S(1)}, f32[256,1280]{1,0:T(8,128)}, u32[]{:S(2)}) copy-start(f32[256,1280]{1,0:T(8,128)} %get-tuple-element.82.refs_0_) | copy-start | bytes 3932164
  532.3 30.8 %collective-permute-start.26 = (f32[256,1280]{1,0:T(8,128)S(1)}, f32[256,1280]{1,0:T(8,128)S(1)}, u32[]{:S(2)}, u32[]{:S(2)}) collective-permute-start(f32[256,1280]{1,0:T(8,128)S(1)} %copy-done.4), channel_id=1, source_target_pairs={{0,2},{2,0},{1,3},{3,1},{4,6},{6,4},{5,7},{7,5},{8,10},{10,8},{9,1... | collective-permute-start | bytes 3932168 | tf_op jit(solution)/shard_map/ppermute | solution.py:513
  591.4 7.4 collective-permute-start.28
  598.8 2.1 copy-start.7
  613.1 89.9 %collective-permute-start.32 = (f32[256,1024]{1,0:T(8,128)}, f32[256,1024]{1,0:T(8,128)S(1)}, u32[]{:S(2)}, u32[]{:S(2)}) collective-permute-start(f32[256,1024]{1,0:T(8,128)} %get-tuple-element.96), channel_id=1, source_target_pairs={{0,1},{1,0},{2,3},{3,2},{4,5},{5,4},{6,7},{7,6},{8,9},{9,8},{10,11... | collective-permute-start | bytes 3145736 | tf_op jit(solution)/shard_map/ppermute | solution.py:513
  613.3 89.8 %collective-permute-start.34 = (f32[256,1024]{1,0:T(8,128)}, f32[256,1024]{1,0:T(8,128)S(1)}, u32[]{:S(2)}, u32[]{:S(2)}) collective-permute-start(f32[256,1024]{1,0:T(8,128)} %get-tuple-element.96), channel_id=1, source_target_pairs={{0,3},{3,0},{1,2},{2,1},{4,7},{7,4},{5,6},{6,5},{8,11},{11,8},{9,1... | collective-permute-start | bytes 3145736 | tf_op jit(solution)/shard_map/ppermute | solution.py:513
  614.6 88.4 %collective-permute-start.33 = (f32[256,1024]{1,0:T(8,128)}, f32[256,1024]{1,0:T(8,128)S(1)}, u32[]{:S(2)}, u32[]{:S(2)}) collective-permute-start(f32[256,1024]{1,0:T(8,128)} %get-tuple-element.95.refs_0_), channel_id=1, source_target_pairs={{0,2},{2,0},{1,3},{3,1},{4,6},{6,4},{5,7},{7,5},{8,10},{10,8},{9,1... | collective-permute-start | bytes 3145736 | tf_op jit(solution)/shard_map/ppermute | solution.py:513
  652.3 50.8 %copy-start.5 = (f32[256,1024]{1,0:T(8,128)S(1)}, f32[256,1024]{1,0:T(8,128)}, u32[]{:S(2)}) copy-start(f32[256,1024]{1,0:T(8,128)} %get-tuple-element.95.refs_0_) | copy-start | bytes 3145732
  703.1 11.5 %copy-start.9 = (f32[2048,256]{1,0:T(8,128)S(1)}, f32[2048,256]{1,0:T(8,128)}, u32[]{:S(2)}) copy-start(f32[2048,256]{1,0:T(8,128)} %get-tuple-element.92.refs_0_) | copy-start | bytes 6291460
  714.5 114.5 %collective-permute-start.35 = (f32[1024,1024]{1,0:T(8,128)}, f32[1024,1024]{1,0:T(8,128)S(1)}, u32[]{:S(2)}, u32[]{:S(2)}) collective-permute-start(f32[1024,1024]{1,0:T(8,128)} %shard_map.63.mine_ref), channel_id=1, source_target_pairs={{0,1},{1,0},{2,3},{3,2},{4,5},{5,4},{6,7},{7,6},{8,9},{9,8},{10,11... | collective-permute-start | bytes 12582920 | tf_op jit(solution)/shard_map/ppermute | solution.py:560
  714.5 48.5 %collective-permute-start.29 = (f32[2048,256]{1,0:T(8,128)S(1)}, f32[2048,256]{1,0:T(8,128)S(1)}, u32[]{:S(2)}, u32[]{:S(2)}) collective-permute-start(f32[2048,256]{1,0:T(8,128)S(1)} %copy-done.9), channel_id=1, source_target_pairs={{0,4},{4,0},{8,12},{12,8},{1,5},{5,1},{9,13},{13,9},{2,6},{6,2},{1... | collective-permute-start | bytes 6291464 | tf_op jit(solution)/shard_map/ppermute | solution.py:539
  715.4 48.0 %collective-permute-start.30 = (f32[2048,256]{1,0:T(8,128)S(1)}, f32[2048,256]{1,0:T(8,128)S(1)}, u32[]{:S(2)}, u32[]{:S(2)}) collective-permute-start(f32[2048,256]{1,0:T(8,128)S(1)} %copy-done.9), channel_id=1, source_target_pairs={{0,8},{8,0},{4,12},{12,4},{1,9},{9,1},{5,13},{13,5},{2,10},{10,2},... | collective-permute-start | bytes 6291464 | tf_op jit(solution)/shard_map/ppermute | solution.py:540
  716.1 92.4 %collective-permute-start.31 = (f32[2048,256]{1,0:T(8,128)S(1)}, f32[2048,256]{1,0:T(8,128)S(1)}, u32[]{:S(2)}, u32[]{:S(2)}) collective-permute-start(f32[2048,256]{1,0:T(8,128)S(1)} %copy-done.9), channel_id=1, source_target_pairs={{0,12},{12,0},{4,8},{8,4},{1,13},{13,1},{5,9},{9,5},{2,14},{14,2},... | collective-permute-start | bytes 6291464 | tf_op jit(solution)/shard_map/ppermute | solution.py:549
  829.0 1.9 copy-start.8
  (2 other events, 2.0 us)
Sparse Core Ops, SparseCore 0:
  232.8 47.5 all-gather.6
  419.6 47.5 all-gather.8
  591.5 42.1 all-gather.10

commit v4 on v3

--- a/solution.py
+++ b/solution.py
@@ -268,15 +268,11 @@
     )(flat_panel(panel))
 
 
-def pack_rows(i, cols, diags, out_ref):
+def pack_rows(n, cols, diags, out_ref):
     for s in range(4):
-        def put(value, s=s):
-            for half in range(2):
-                out_ref[pl.ds(4 * half + s, NB, stride=8), :] = value[:, 128 * half:128 * half + 128]
-
-        pl.when(i < s)(lambda: put(jnp.zeros((NB, NB), F32)))
-        pl.when(i == s)(lambda s=s: put(diags[s][...]))
-        pl.when(i > s)(lambda s=s: put(cols[s][...]))
+        value = jnp.where(n > s, cols[s][...], jnp.where(n == s, diags[s][...], 0.0))
+        for half in range(2):
+            out_ref[pl.ds(4 * half + s, NB, stride=8), :] = value[:, 128 * half:128 * half + 128]
 
 
 def rows_kernel(*refs):
@@ -319,17 +315,19 @@
 
 
 def cols_kernel(*refs):
-    pieces, x_ref, outs, tall = refs[:4], refs[4], refs[5:-1], refs[-1]
+    pieces, x_ref, outs, tall, done = refs[:4], refs[4], refs[5:-2], refs[-2], refs[-1]
     my_row = lax.axis_index("pr")
     i = pl.program_id(0)
     for j in range(4):
         tall[pl.ds(pl.multiple_of((my_row ^ j) * NB, NB), NB), :] = pieces[j][...]
 
-    parts = [dot(x_ref[NB * k:NB * k + NB, :NB * k + NB], tall[:NB * k + NB, :]) for k in range(4)]
+    for k in range(4):
+        at = slice(NB * k, NB * k + NB)
+        part = dot(x_ref[NB * k:, at], tall[at, :])
+        done[NB * k:, :] = part if k == 0 else done[NB * k:, :] + part
 
     def put(ref):
-        for k in range(4):
-            ref[NB * k:NB * k + NB, :] = parts[k]
+        ref[...] = done[...]
 
     if len(outs) == 1:
         put(outs[0])
@@ -345,7 +343,7 @@
     return call(
         cols_kernel, 30 * cols * SUP * SUP // 4, 12 * cols * SUP, 20, grid=(cols // NB,), out_shape=outs,
         in_specs=[pl.BlockSpec((NB, NB), lambda i: (0, i))] * 4 + [pl.BlockSpec((SUP, SUP), lambda i: (0, 0))],
-        out_specs=specs[:len(outs)], scratch_shapes=[pltpu.VMEM((SUP, NB), F32)],
+        out_specs=specs[:len(outs)], scratch_shapes=[pltpu.VMEM((SUP, NB), F32), pltpu.VMEM((SUP, NB), F32)],
     )(*pieces, x)
 
 
@@ -400,43 +398,34 @@
 
 def row_kernel(*refs):
     trail_ref, l_ref, mine_ref, theirs_ref = refs[1:5]
-    keep_ref, send_ref, landing, sem = refs[-4:]
+    keep_ref, send_ref = refs[-2:]
     j = pl.program_id(0)
-    copies = [pltpu.make_async_copy(ref, landing.at[n], sem.at[n]) for n, ref in enumerate((mine_ref, theirs_ref))]
-
-    @pl.when(j == 0)
-    def _():
-        for copy in copies:
-            copy.start()
-        if len(refs) == 10:
+    lanes = pl.ds(pl.multiple_of(j % 2 * (SUP // 2), SUP // 2), SUP // 2)
+
+    @pl.when(j < 2)
+    def _():
+        keep_ref[:, lanes] = trail_ref[...] - dot(l_ref[...], mine_ref[...])
+        if len(refs) == 8:
             keep_ref[:, SUP:] = refs[5][...]
             send_ref[:, SUP:] = refs[5][...]
 
-    for n, copy in enumerate(copies):
-        pl.when(j == n)(copy.wait)
-    new = trail_ref[...] - dot(l_ref[...], landing[j])
-
-    @pl.when(j == 0)
-    def _():
-        keep_ref[:, :SUP] = new
-
-    @pl.when(j == 1)
-    def _():
-        send_ref[:, :SUP] = new
+    @pl.when(j >= 2)
+    def _():
+        send_ref[:, lanes] = trail_ref[...] - dot(l_ref[...], theirs_ref[...])
 
 
 def update_row(core, trail, l_rows, mine, theirs, panel_row, step):
     extra = [] if panel_row is None else [panel_row]
     width = SUP + (0 if panel_row is None else panel_row.shape[1])
     out = pl.BlockSpec((NB, width), lambda j, h: (0, 0))
-    anywhere = pl.BlockSpec(memory_space=pl.ANY)
     return call(
         row_kernel, 24 * NB * SUP * SUP, 12 * SUP * SUP, 30,
         grid_spec=pltpu.PrefetchScalarGridSpec(
-            num_scalar_prefetch=1, grid=(2,),
-            in_specs=[pl.BlockSpec((NB, SUP), lambda j, h: (step + 1, h[0] ^ j)), pl.BlockSpec((NB, SUP), lambda j, h: (0, 0)),
-                      anywhere, anywhere] + [pl.BlockSpec(a.shape, lambda j, h: (0, 0)) for a in extra],
-            out_specs=(out, out), scratch_shapes=[pltpu.VMEM((2, SUP, SUP), F32), pltpu.SemaphoreType.DMA((2,))]),
+            num_scalar_prefetch=1, grid=(4,),
+            in_specs=[pl.BlockSpec((NB, SUP // 2), lambda j, h: (step + 1, 2 * (h[0] ^ (j // 2)) + j % 2)), pl.BlockSpec((NB, SUP), lambda j, h: (0, 0)),
+                      pl.BlockSpec((SUP, SUP // 2), lambda j, h: (0, jnp.minimum(j, 1))), pl.BlockSpec((SUP, SUP // 2), lambda j, h: (0, jnp.maximum(j - 2, 0)))]
+            + [pl.BlockSpec(a.shape, lambda j, h: (0, 0)) for a in extra],
+            out_specs=(out, out)),
         out_shape=(shape(NB, width), shape(NB, width)),
     )(core, trail, in_hbm(l_rows), in_hbm(mine), in_hbm(theirs), *extra)
 
@@ -445,33 +434,37 @@
     rest, (landing, u_parts, l_parts, sem) = rest[:-4], rest[-4:]
     my_row = lax.axis_index("pr")
     j, i = pl.program_id(0), pl.program_id(1)
-    copies = [pltpu.make_async_copy(ref, landing, sem.at[n]) for n, ref in enumerate((mine_ref, theirs_ref))]
-    out_ref = rest[0]
-    if len(rest) > 1:
-        out_ref = rest[8]
-        pack_rows(jnp.minimum(j * pl.num_programs(1) + i, pl.num_programs(1) + 2), rest[:4], rest[4:8], rest[9])
+    quarter = SUP // 4
+    first = [pltpu.make_async_copy(mine_ref.at[at], landing.at[at], sem.at[n]) for n, at in enumerate(pl.ds(n * quarter, quarter) for n in range(4))]
+    second = pltpu.make_async_copy(theirs_ref, landing, sem.at[4])
+    out_ref = rest[8] if len(rest) > 1 else rest[0]
 
     @pl.when(i == 0)
     def _():
-        pl.when(j == 0)(copies[0].start)
-        pl.when(j == 0)(copies[0].wait)
-        pl.when(j == 1)(copies[1].wait)
-
-        def split_rows(k, carry):
-            at = pl.ds(pl.multiple_of(k * 64, 64), 64)
-            for n, part in enumerate(split3(landing[at, :])):
-                u_parts[n, at, :] = part
-            return carry
-
-        lax.fori_loop(0, SUP // 64, split_rows, 0)
+        for copy in first:
+            pl.when(j == 0)(copy.start)
+        pl.when(j == 1)(second.wait)
+        for n, copy in enumerate(first):
+            pl.when(j == 0)(copy.wait)
+
+            def split_rows(k, carry, n=n):
+                at = pl.ds(pl.multiple_of(n * quarter + k * 64, 64), 64)
+                for m, part in enumerate(split3(landing[at, :])):
+                    u_parts[m, at, :] = part
+                return carry
+
+            lax.fori_loop(0, quarter // 64, split_rows, 0)
         out_ref[...] = dot_tn(diag_ref[...], landing[pl.ds(pl.multiple_of(my_row * NB, NB), NB), :])
 
     @pl.when(i > 0)
     def _():
-        pl.when((i == 1) & (j == 0))(copies[1].start)
+        pl.when((i == 1) & (j == 0))(second.start)
         for n, part in enumerate(split3(l_ref[...])):
             l_parts[n] = part
         out_ref[...] = trail_ref[...] - dot_parts(lambda n: l_parts[n], lambda n: u_parts[n])
+        if len(rest) > 1:
+            count = pl.num_programs(1)
+            pack_rows(jnp.minimum(j * (count - 1) + i - 1, count + 2), rest[:4], rest[4:8], rest[9])
 
 
 def update_trail(core, trail, l_rows, mine, theirs, own_diag, step, out_cols=(), out_diags=()):
@@ -484,7 +477,7 @@
            pl.BlockSpec((NB, NB), lambda j, i, h: (0, 0))]
     outs, shapes = [at], [shape(rows, cols)]
     if out_cols:
-        block = lambda j, i: jnp.minimum(j * count + i, rows // NB - 1)
+        block = lambda j, i: jnp.clip(j * (count - 1) + i - 1, 0, rows // NB - 1)
         ins += [pl.BlockSpec((NB, NB), lambda j, i, h, s=s: (jnp.maximum(block(j, i) - s - 1, 0), 0)) for s in range(4)]
         ins += [pl.BlockSpec((NB, NB), lambda j, i, h: (0, 0))] * 4
         outs.append(pl.BlockSpec((8 * NB, 128), lambda j, i, h: (block(j, i), 0)))
@@ -492,7 +485,7 @@
     return call(
         trail_kernel, 12 * count * NB * cols * SUP, 8 * count * NB * cols, 32,
         grid_spec=pltpu.PrefetchScalarGridSpec(num_scalar_prefetch=1, grid=(2, count), in_specs=ins, out_specs=outs, scratch_shapes=[
-            pltpu.VMEM((SUP, SUP), F32), pltpu.VMEM((3, SUP, SUP), BF16), pltpu.VMEM((3, NB, SUP), BF16), pltpu.SemaphoreType.DMA((2,))]),
+            pltpu.VMEM((SUP, SUP), F32), pltpu.VMEM((3, SUP, SUP), BF16), pltpu.VMEM((3, NB, SUP), BF16), pltpu.SemaphoreType.DMA((5,))]),
         out_shape=shapes, input_output_aliases={1: 0} if step else {},
     )(core, trail, in_hbm(l_rows), in_hbm(mine), in_hbm(theirs), *(in_hbm(a) for a in (own_diag, *out_cols, *out_diags)))
 
@@ -503,9 +496,13 @@
 
 
 def gather_diag(block):
-    have = block[None]
-    for axis, perm in (("pc", FLIP1), ("pc", FLIP2), ("pr", FLIP2)):
-        have = jnp.concatenate([have, lax.ppermute(have, axis, perm)], axis=0)
+    y = functools.partial(lax.ppermute, axis_name="pc", perm=FLIP1)
+    z = functools.partial(lax.ppermute, axis_name="pc", perm=FLIP2)
+    x = functools.partial(lax.ppermute, axis_name="pr", perm=FLIP2)
+    at_y, at_z, at_x = y(block), z(block), x(block)
+    at_yz, at_xy, at_xz = z(at_y), x(at_y), x(at_z)
+    at_xyz = x(at_yz)
+    have = jnp.stack([block, at_y, at_z, at_yz, at_x, at_xy, at_xz, at_xyz])
     return [have, lax.ppermute(have, "pr", FLIP1)]
 
 

time: 914 us -> 950 us (1.039)
  waiting for transfers between devices: 171 us -> 206 us
    ppermute x3, waiting for transfers between devices: 48.8 us -> 0.01 us  [local_part(): far = [lax.ppermute(col_panel, 'pc', FLIP3)]]
    ppermute x3 -> x7, waiting for transfers between devices: 29.7 us -> 74.3 us  [the longest x3 64.2 us: gather_diag(): at_y, at_z, at_x = (y(block), z(block), x(block))]
    ppermute x1, waiting for transfers between devices: 2.82 us -> 27.6 us  [gather_all(): x = lax.ppermute(panel, 'pr', FLIP2)]
    ppermute x4, waiting for transfers between devices: 34.8 us -> 50 us  [local_part(): z = lax.ppermute(col_panel, 'pc', FLIP2)]
  transfers between devices with their start and end apart: 39 -> 43, of which waited for: 11 -> 10; matrix products, arithmetic and copies ran while one was open for 1% -> 2% of each run, Pallas kernels for 61% -> 58%
where the time goes in v4:
time: 950 us; the launch traced here: 946 us
  Pallas kernels  658 us (69%)
  waiting for transfers between devices  206 us (22%)
  starting transfers between devices  37.6 us (4%)
  local copies, waits for them, and re-layouts  30.8 us (3%)
  between operations  14.3 us (2%)
    pallas_call x4, Pallas kernels, update_trail(): call(trail_kernel, 12 * count * NB * cols * SUP, 8 * count * NB * cols, 3...  199 us
    pallas_call x3, Pallas kernels, factor_beside(): call(fused_kernel, 100000000000, 1 << 25, 48, grid=(4,), out_shape=(near(...  152 us
    pallas_call x4, Pallas kernels, solve_rows(): call(rows_kernel, 30 * rows * SUP * SUP // 4, 12 * rows * SUP, 34, grid=(...  97.8 us
    pallas_call x3, Pallas kernels, update_panel(): call(panel_kernel, 12 * rows * width * SUP, 8 * rows * width + 4 * rows *...  68.3 us
    ppermute x3, waiting for transfers between devices, gather_diag(): at_y, at_z, at_x = (y(block), z(block), x(block))  64.2 us
    pallas_call x5, Pallas kernels, solve_cols(): call(cols_kernel, 30 * cols * SUP * SUP // 4, 12 * cols * SUP, 20, grid=(...  61.3 us
    ppermute x4, waiting for transfers between devices, local_part(): z = lax.ppermute(col_panel, 'pc', FLIP2)  50 us
    ppermute x4, waiting for transfers between devices, local_part(): y = lax.ppermute(col_panel, 'pc', FLIP1)  45 us
  transfers between devices with their start and end apart: 43, of which 10 were waited for; matrix products, arithmetic and copies ran while one was open for 2% of the time, Pallas kernels for 58%

profile of v4, /device:TPU:0, one launch (start us, length us, event | category | flops | bytes accessed | tf_op | source)
XLA Modules:
  0.0 946.4 jit_solution(1745045109728511630)
XLA Ops:
  9.9 3.2 collective-permute-start.4
  13.1 6.5 slice.24
  19.6 1.7 copy.20
  21.3 2.1 collective-permute-start.1
  23.4 1.9 collective-permute-start.7
  26.1 1.6 collective-permute-start.6
  28.4 64.2 %collective-permute-done.5 = f32[256,256]{1,0:T(8,128)S(1)} collective-permute-done((f32[256,256]{1,0:T(8,128)S(1)}, f32[256,256]{1,0:T(8,128)S(1)}, u32[]{:S(2)}, u32[]{:S(2)}) %collective-permute-start.5) | collective-permute-done | bytes 262176 | tf_op jit(solution)/shard_map/ppermute | solution.py:502
  92.6 1.9 collective-permute-start.8
  96.8 1.6 collective-permute-start.9
  101.0 5.0 collective-permute-done.9
  106.7 3.5 collective-permute-done.10
  110.9 1.9 constant_dynamic-slice_fusion
  113.4 1.9 collective-permute-start.19
  115.6 4.6 copy-done
  120.1 6.2 shard_map.41.refs_0_
  127.9 27.6 %collective-permute-done.13.refs_2_ = f32[256,768]{1,0:T(8,128)S(1)} collective-permute-done((f32[256,768]{1,0:T(8,128)S(1)}, f32[256,768]{1,0:T(8,128)S(1)}, u32[]{:S(2)}, u32[]{:S(2)}) %collective-permute-start.13) | collective-permute-done | bytes 786464 | tf_op jit(solution)/shard_map/ppermute | solution.py:514
  160.5 35.2 %shard_map.42 = (f32[1024,1024]{1,0:T(8,128)S(1)}, f32[256,256]{1,0:T(8,128)}, f32[256,256]{1,0:T(8,128)}) custom-call(f32[8,256,256]{2,1,0:T(8,128)} %bitcast_dynamic-update-slice_fusion.refs_0_, f32[8,256,256]{2,1,0:T(8,128)} %collective-permute-done.11.refs_1_), custom_call_target="tpu_custom_call" | custom-call | flops 30000001024 | bytes 16777216 | tf_op jit(solution)/shard_map/pallas_call | solution.py:170
  195.7 10.8 %shard_map.46.mine_ref.refs_3_ = f32[1024,1024]{1,0:T(8,128)} custom-call(f32[256,1024]{1,0:T(8,128)S(1)} %get-tuple-element.109.refs_0_, f32[256,1024]{1,0:T(8,128)S(1)} %collective-permute-done.18.refs_1_, f32[256,1024]{1,0:T(8,128)S(1)} %collective-permute-done.19.refs_2_, f32[256,1024]{1,0:T(8,128)S(1)} %collective-permute-done.20.refs_3_, ...), custom_call_target="tpu_custom_call" | custom-call | flops 8053063680 | bytes 12582912 | tf_op jit(solution)/shard_map/pallas_call | solution.py:343
  206.5 8.3 shard_map.44.refs_2_
  214.8 28.0 %shard_map.43 = (f32[2816,1024]{1,0:T(8,128)}, f32[2816,256]{1,0:T(8,128)}) custom-call(f32[2816,256]{1,0:T(8,128)} %bitcast.40.refs_0_, f32[2816,256]{1,0:T(8,128)S(1)} %collective-permute-done.refs_1_, f32[2816,256]{1,0:T(8,128)} %collective-permute-done.1.refs_2_, f32[1408,256]{1,0:T(8,128)S(1)} %collective-permute-done.2.refs_3_, ...), custom_call_target="tpu_custom_call" | custom-call | flops 22145925120 | bytes 34603008 | tf_op jit(solution)/shard_map/pallas_call | solution.py:308
  242.9 33.7 %shard_map.45 = (f32[256,256]{1,0:T(8,128)}, f32[2560,256]{1,0:T(8,128)}, f32[256,512]{1,0:T(8,128)}, f32[2560,512]{1,0:T(8,128)}) custom-call(f32[2816,768]{1,0:T(8,128)} %shard_map.41.refs_0_, f32[2816,1024]{1,0:T(8,128)} %get-tuple-element.57.refs_1_.l_ref.refs_2_, f32[1024,768]{1,0:T(8,128)S(1)} %copy-done.6), custom_call_target="tpu_custom_call" | custom-call | flops 26575110144 | bytes 28835840 | tf_op jit(solution)/shard_map/pallas_call | solution.py:392
  277.7 2.5 collective-permute-start.17
  281.2 12.8 %shard_map.50 = (f32[256,1536]{1,0:T(8,128)}, f32[256,1536]{1,0:T(8,128)}) custom-call(s32[1]{0:T(128)} %bitcast.core_ref.refs_0_, f32[3072,2048]{1,0:T(8,128)} %refs_1_.1, f32[2816,1024]{1,0:T(8,128)} %get-tuple-element.57.refs_1_.l_ref.refs_2_, f32[1024,1024]{1,0:T(8,128)} %shard_map.46.mine_ref.refs_3_, ...), custom_call_target="tpu_custom_call" | custom-call | flops 6442450944 | bytes 12582912 | tf_op jit(solution)/shard_map/pallas_call | solution.py:421
  294.8 50.2 %shard_map.47.rest_0_ = f32[3072,2048]{1,0:T(8,128)} custom-call(s32[1]{0:T(128)} %bitcast.core_ref.refs_0_, f32[3072,2048]{1,0:T(8,128)} %refs_1_.1, f32[2816,1024]{1,0:T(8,128)} %get-tuple-element.57.refs_1_.l_ref.refs_2_, f32[1024,1024]{1,0:T(8,128)} %shard_map.46.mine_ref.refs_3_, f32[1024,1024]{1,0:T(8,128)} %collective-permute-done.21.theirs_ref.refs_4_, ...), custom_call_target="tpu_custom_call" | custom-call | flops 45097156608 | bytes 29360128 | tf_op jit(solution)/shard_map/pallas_call | solution.py:485
  346.4 50.8 %shard_map.48 = (f32[1024,1024]{1,0:T(8,128)S(1)}, f32[256,256]{1,0:T(8,128)}, f32[256,256]{1,0:T(8,128)}, f32[3072,2048]{1,0:T(8,128)}) custom-call(f32[16,256,256]{2,1,0:T(8,128)} %bitcast.47, f32[3072,2048]{1,0:T(8,128)} %refs_1_.1, f32[2816,1024]{1,0:T(8,128)} %get-tuple-element.57.refs_1_.l_ref.refs_2_, ...), custom_call_target="tpu_custom_call", output_to_operand_aliasing={{3}: (5, {})} | custom-call | flops 99999997952 | bytes 33554432 | tf_op jit(solution)/shard_map/pallas_call | solution.py:249
  397.3 17.0 %shard_map.51 = (f32[1024,1024]{1,0:T(8,128)}, f32[1024,512]{1,0:T(8,128)S(1)}) custom-call(f32[256,1536]{1,0:T(8,128)S(1)} %copy-done.3, f32[256,1536]{1,0:T(8,128)S(1)} %collective-permute-done.22.refs_1_, f32[256,1536]{1,0:T(8,128)S(1)} %collective-permute-done.23.refs_2_, f32[256,1536]{1,0:T(8,128)} %collective-permute-done.24.refs_3_, ...), custom_call_target="tpu_custom_call" | custom-call | flops 12079595520 | bytes 18874368 | tf_op jit(solution)/shard_map/pallas_call | solution.py:343
  414.3 25.8 %shard_map.49 = (f32[2560,1024]{1,0:T(8,128)}, f32[2560,256]{1,0:T(8,128)}) custom-call(f32[2560,256]{1,0:T(8,128)} %get-tuple-element.60.refs_0_, f32[2560,256]{1,0:T(8,128)} %collective-permute-done.15.refs_1_, f32[2560,256]{1,0:T(8,128)} %collective-permute-done.16.refs_2_, f32[2560,256]{1,0:T(8,128)} %collective-permute-done.17.refs_3_, ...), custom_call_target="tpu_custom_call" | custom-call | flops 20132659200 | bytes 31457280 | tf_op jit(solution)/shard_map/pallas_call | solution.py:308
  440.1 21.5 %shard_map.52 = (f32[256,256]{1,0:T(8,128)}, f32[2304,256]{1,0:T(8,128)}, f32[256,256]{1,0:T(8,128)}, f32[2304,256]{1,0:T(8,128)}) custom-call(f32[2560,512]{1,0:T(8,128)} %get-tuple-element.59.refs_0_, f32[2560,1024]{1,0:T(8,128)} %get-tuple-element.66.refs_1_.l_ref.refs_2_, f32[1024,512]{1,0:T(8,128)S(1)} %get-tuple-element.70.refs_2_), custom_call_target="tpu_custom_call" | custom-call | flops 16106127360 | bytes 20971520 | tf_op jit(solution)/shard_map/pallas_call | solution.py:392
  462.8 2.3 collective-permute-start.27
  466.1 12.6 %shard_map.56 = (f32[256,1280]{1,0:T(8,128)}, f32[256,1280]{1,0:T(8,128)}) custom-call(s32[1]{0:T(128)} %bitcast.core_ref.refs_0_, f32[3072,2048]{1,0:T(8,128)} %get-tuple-element.74.trail_ref.refs_1_, f32[2560,1024]{1,0:T(8,128)} %get-tuple-element.66.refs_1_.l_ref.refs_2_, f32[1024,1024]{1,0:T(8,128)} %get-tuple-element.75.mine_ref.refs_3_, ...), custom_call_target="tpu_custom_call" | custom-call | flops 6442450944 | bytes 12582912 | tf_op jit(solution)/shard_map/pallas_call | solution.py:421
  479.7 43.1 %shard_map.53.trail_ref = f32[3072,2048]{1,0:T(8,128)} custom-call(s32[1]{0:T(128)} %bitcast.core_ref.refs_0_, f32[3072,2048]{1,0:T(8,128)} %get-tuple-element.74.trail_ref.refs_1_, f32[2560,1024]{1,0:T(8,128)} %get-tuple-element.66.refs_1_.l_ref.refs_2_, f32[1024,1024]{1,0:T(8,128)} %get-tuple-element.75.mine_ref.refs_3_, ...), custom_call_target="tpu_custom_call", output_to_operand_aliasing={{}: (1, {})} | custom-call | flops 38654705664 | bytes 25165824 | tf_op jit(solution)/shard_map/pallas_call | solution.py:485
  522.8 50.9 %shard_map.54 = (f32[1024,1024]{1,0:T(8,128)S(1)}, f32[256,256]{1,0:T(8,128)}, f32[256,256]{1,0:T(8,128)}, f32[3072,2048]{1,0:T(8,128)}) custom-call(f32[16,256,256]{2,1,0:T(8,128)} %bitcast.48, f32[3072,2048]{1,0:T(8,128)} %shard_map.53.trail_ref, f32[2560,1024]{1,0:T(8,128)} %get-tuple-element.66.refs_1_.l_ref.refs_2_, ...), custom_call_target="tpu_custom_call", output_to_operand_aliasing={{3}: (1, {})} | custom-call | flops 99999997952 | bytes 33554432 | tf_op jit(solution)/shard_map/pallas_call | solution.py:249
  575.0 4.7 collective-permute-done.26.refs_2_
  579.7 23.4 %shard_map.55 = (f32[2304,1024]{1,0:T(8,128)}, f32[2304,256]{1,0:T(8,128)}) custom-call(f32[2304,256]{1,0:T(8,128)} %get-tuple-element.72.refs_0_, f32[2304,256]{1,0:T(8,128)} %collective-permute-done.25.refs_1_, f32[2304,256]{1,0:T(8,128)} %collective-permute-done.26.refs_2_, f32[2304,256]{1,0:T(8,128)} %collective-permute-done.27.refs_3_, ...), custom_call_target="tpu_custom_call" | custom-call | flops 18119393280 | bytes 28311552 | tf_op jit(solution)/shard_map/pallas_call | solution.py:308
  604.4 14.4 %shard_map.57 = (f32[1024,1024]{1,0:T(8,128)}, f32[1024,256]{1,0:T(8,128)S(1)}) custom-call(f32[256,1280]{1,0:T(8,128)S(1)} %copy-done.4, f32[256,1280]{1,0:T(8,128)} %collective-permute-done.29.refs_1_, f32[256,1280]{1,0:T(8,128)S(1)} %collective-permute-done.30.refs_2_, f32[256,1280]{1,0:T(8,128)} %collective-permute-done.31.refs_3_, ...), custom_call_target="tpu_custom_call" | custom-call | flops 10066329600 | bytes 15728640 | tf_op jit(solution)/shard_map/pallas_call | solution.py:343
  618.8 13.1 %shard_map.58 = (f32[256,256]{1,0:T(8,128)}, f32[2048,256]{1,0:T(8,128)}) custom-call(f32[2304,256]{1,0:T(8,128)} %get-tuple-element.71.refs_0_, f32[2304,1024]{1,0:T(8,128)} %get-tuple-element.80.refs_1_.l_ref.refs_2_, f32[1024,256]{1,0:T(8,128)S(1)} %get-tuple-element.84.refs_2_), custom_call_target="tpu_custom_call" | custom-call | flops 7247757312 | bytes 14155776 | tf_op jit(solution)/shard_map/pallas_call | solution.py:392
  632.0 7.4 collective-permute-done.32.theirs_ref.refs_4_
  639.4 2.1 copy-done.7
  641.5 12.3 %shard_map.62 = (f32[256,1024]{1,0:T(8,128)}, f32[256,1024]{1,0:T(8,128)}) custom-call(s32[1]{0:T(128)} %bitcast.core_ref.refs_0_, f32[3072,2048]{1,0:T(8,128)} %get-tuple-element.86.trail_ref.refs_1_, f32[2304,1024]{1,0:T(8,128)} %get-tuple-element.80.refs_1_.l_ref.refs_2_, f32[1024,1024]{1,0:T(8,128)} %get-tuple-element.87.mine_ref.refs_3_, ...), custom_call_target="tpu_custom_call" | custom-call | flops 6442450944 | bytes 12582912 | tf_op jit(solution)/shard_map/pallas_call | solution.py:421
  655.9 36.1 %shard_map.59.trail_ref = f32[3072,2048]{1,0:T(8,128)} custom-call(s32[1]{0:T(128)} %bitcast.core_ref.refs_0_, f32[3072,2048]{1,0:T(8,128)} %get-tuple-element.86.trail_ref.refs_1_, f32[2304,1024]{1,0:T(8,128)} %get-tuple-element.80.refs_1_.l_ref.refs_2_, f32[1024,1024]{1,0:T(8,128)} %get-tuple-element.87.mine_ref.refs_3_, ...), custom_call_target="tpu_custom_call", output_to_operand_aliasing={{}: (1, {})} | custom-call | flops 32212254720 | bytes 20971520 | tf_op jit(solution)/shard_map/pallas_call | solution.py:485
  692.1 50.7 %shard_map.60 = (f32[1024,1024]{1,0:T(8,128)S(1)}, f32[256,256]{1,0:T(8,128)}, f32[256,256]{1,0:T(8,128)}, f32[3072,2048]{1,0:T(8,128)}) custom-call(f32[16,256,256]{2,1,0:T(8,128)} %bitcast.49, f32[3072,2048]{1,0:T(8,128)} %shard_map.59.trail_ref, f32[2304,1024]{1,0:T(8,128)} %get-tuple-element.80.refs_1_.l_ref.refs_2_, ...), custom_call_target="tpu_custom_call", output_to_operand_aliasing={{3}: (1, {})} | custom-call | flops 99999997952 | bytes 33554432 | tf_op jit(solution)/shard_map/pallas_call | solution.py:249
  742.9 10.8 %shard_map.63.mine_ref = f32[1024,1024]{1,0:T(8,128)} custom-call(f32[256,1024]{1,0:T(8,128)S(1)} %copy-done.5, f32[256,1024]{1,0:T(8,128)S(1)} %collective-permute-done.36.refs_1_, f32[256,1024]{1,0:T(8,128)S(1)} %collective-permute-done.37.refs_2_, f32[256,1024]{1,0:T(8,128)S(1)} %collective-permute-done.38.refs_3_, f32[1024,1024]{1,0:T(8,128)S(1)} %get-tuple-element.93.refs_4_), custom_call_target="tpu_custom_call" | custom-call | flops 8053063680 | bytes 12582912 | tf_op jit(solution)/shard_map/pallas_call | solution.py:343
  754.8 2.3 collective-permute-start.35
  757.1 45.0 %collective-permute-done.33.refs_1_ = f32[2048,256]{1,0:T(8,128)S(1)} collective-permute-done((f32[2048,256]{1,0:T(8,128)S(1)}, f32[2048,256]{1,0:T(8,128)S(1)}, u32[]{:S(2)}, u32[]{:S(2)}) %collective-permute-start.33) | collective-permute-done | bytes 2097184 | tf_op jit(solution)/shard_map/ppermute | solution.py:536
  802.2 45.3 %collective-permute-done.34.refs_2_ = f32[2048,256]{1,0:T(8,128)S(1)} collective-permute-done((f32[2048,256]{1,0:T(8,128)S(1)}, f32[2048,256]{1,0:T(8,128)S(1)}, u32[]{:S(2)}, u32[]{:S(2)}) %collective-permute-start.34) | collective-permute-done | bytes 2097184 | tf_op jit(solution)/shard_map/ppermute | solution.py:537
  847.4 20.6 %shard_map.61 = (f32[2048,1024]{1,0:T(8,128)}, f32[2048,256]{1,0:T(8,128)}) custom-call(f32[2048,256]{1,0:T(8,128)} %get-tuple-element.92.refs_0_, f32[2048,256]{1,0:T(8,128)S(1)} %collective-permute-done.33.refs_1_, f32[2048,256]{1,0:T(8,128)S(1)} %collective-permute-done.34.refs_2_, f32[2048,256]{1,0:T(8,128)S(1)} %collective-permute-done.35.refs_3_, ...), custom_call_target="tpu_custom_call" | custom-call | flops 16106127360 | bytes 25165824 | tf_op jit(solution)/shard_map/pallas_call | solution.py:308
  868.0 2.0 copy-done.9
  870.0 69.7 %shard_map.64 = (f32[3072,2048]{1,0:T(8,128)}, f32[24576,128]{1,0:T(8,128)}) custom-call(s32[1]{0:T(128)} %bitcast.core_ref.refs_0_, f32[3072,2048]{1,0:T(8,128)} %get-tuple-element.91.trail_ref, f32[2048,1024]{1,0:T(8,128)} %get-tuple-element.94.l_ref, f32[1024,1024]{1,0:T(8,128)} %shard_map.63.mine_ref, ...), custom_call_target="tpu_custom_call", output_to_operand_aliasing={{0}: (1, {})} | custom-call | flops 57982058496 | bytes 37748736 | tf_op jit(solution)/shard_map/pallas_call | solution.py:485
  (107 shorter events, 31.4 us)
Async XLA Ops:
  7.2 337.8 %all-gather.7.cloned.1.call-start = ((), (), s32[]{:S(2)}) async-start(), calls=%async_computation | async-start | bytes 4456448 | tf_op jit(solution)/shard_map/all_gather | solution.py:535
  9.9 16.2 %collective-permute-start.4 = (f32[256,256]{1,0:T(8,128)S(1)}, f32[256,256]{1,0:T(8,128)S(1)}, u32[]{:S(2)}, u32[]{:S(2)}) collective-permute-start(f32[256,256]{1,0:T(8,128)S(1)} %bitcast.43), channel_id=1, source_target_pairs={{0,4},{4,0},{8,12},{12,8},{1,5},{5,1},{9,13},{13,9},{2,6},{6,2},{1... | collective-permute-start | bytes 786440 | tf_op jit(solution)/shard_map/ppermute | solution.py:502
  21.3 106.4 %collective-permute-start = (f32[2816,256]{1,0:T(8,128)}, f32[2816,256]{1,0:T(8,128)S(1)}, u32[]{:S(2)}, u32[]{:S(2)}) collective-permute-start(f32[2816,256]{1,0:T(8,128)} %bitcast.40.refs_0_), channel_id=1, source_target_pairs={{0,4},{4,0},{8,12},{12,8},{1,5},{5,1},{9,13},{13,9},{2,6},{6,2},{1... | collective-permute-start | bytes 8650760 | tf_op jit(solution)/shard_map/ppermute | solution.py:536
  21.3 94.1 %collective-permute-start.1 = (f32[2816,256]{1,0:T(8,128)}, f32[2816,256]{1,0:T(8,128)}, u32[]{:S(2)}, u32[]{:S(2)}) collective-permute-start(f32[2816,256]{1,0:T(8,128)} %bitcast.40.refs_0_), channel_id=1, source_target_pairs={{0,8},{8,0},{4,12},{12,4},{1,9},{9,1},{5,13},{13,5},{2,10},{10,2},... | collective-permute-start | bytes 8650760 | tf_op jit(solution)/shard_map/ppermute | solution.py:537
  23.4 69.2 %collective-permute-start.5 = (f32[256,256]{1,0:T(8,128)S(1)}, f32[256,256]{1,0:T(8,128)S(1)}, u32[]{:S(2)}, u32[]{:S(2)}) collective-permute-start(f32[256,256]{1,0:T(8,128)S(1)} %bitcast.44), channel_id=1, source_target_pairs={{0,8},{8,0},{4,12},{12,4},{1,9},{9,1},{5,13},{13,5},{2,10},{10,2},... | collective-permute-start | bytes 786440 | tf_op jit(solution)/shard_map/ppermute | solution.py:502
  23.4 75.7 %collective-permute-start.7 = (f32[256,256]{1,0:T(8,128)S(1)}, f32[256,256]{1,0:T(8,128)S(1)}, u32[]{:S(2)}, u32[]{:S(2)}) collective-permute-start(f32[256,256]{1,0:T(8,128)S(1)} %bitcast.45), channel_id=1, source_target_pairs={{0,2},{2,0},{1,3},{3,1},{4,6},{6,4},{5,7},{7,5},{8,10},{10,8},{9,1... | collective-permute-start | bytes 786440 | tf_op jit(solution)/shard_map/ppermute | solution.py:502
  26.1 70.7 %collective-permute-start.6 = (f32[256,256]{1,0:T(8,128)S(1)}, f32[256,256]{1,0:T(8,128)S(1)}, u32[]{:S(2)}, u32[]{:S(2)}) collective-permute-start(f32[256,256]{1,0:T(8,128)S(1)} %collective-permute-done.4), channel_id=1, source_target_pairs={{0,8},{8,0},{4,12},{12,4},{1,9},{9,1},{5,13},{13,5},{2,10},{10,2},... | collective-permute-start | bytes 786440 | tf_op jit(solution)/shard_map/ppermute | solution.py:503
  92.6 7.7 collective-permute-start.8
  96.8 9.2 collective-permute-start.9
  99.2 11.1 %collective-permute-start.10 = (f32[256,256]{1,0:T(8,128)S(1)}, f32[256,256]{1,0:T(8,128)S(1)}, u32[]{:S(2)}, u32[]{:S(2)}) collective-permute-start(f32[256,256]{1,0:T(8,128)S(1)} %collective-permute-done.6), channel_id=1, source_target_pairs={{0,2},{2,0},{1,3},{3,1},{4,6},{6,4},{5,7},{7,5},{8,10},{10,8},{9,1... | collective-permute-start | bytes 786440 | tf_op jit(solution)/shard_map/ppermute | solution.py:504
  110.9 47.9 %collective-permute-start.11 = (f32[8,256,256]{2,1,0:T(8,128)}, f32[8,256,256]{2,1,0:T(8,128)}, u32[]{:S(2)}, u32[]{:S(2)}) collective-permute-start(f32[8,256,256]{2,1,0:T(8,128)} %bitcast_dynamic-update-slice_fusion.refs_0_), channel_id=1, source_target_pairs={{0,1},{1,0},{2,3},{3,2},{4,5},{5,4},{6,7},{7,6},{8,9},{9,8},{10,11... | collective-permute-start | bytes 6291464 | tf_op jit(solution)/shard_map/ppermute | solution.py:506
  112.8 43.2 %collective-permute-start.18 = (f32[256,1024]{1,0:T(8,128)S(1)}, f32[256,1024]{1,0:T(8,128)S(1)}, u32[]{:S(2)}, u32[]{:S(2)}) collective-permute-start(f32[256,1024]{1,0:T(8,128)S(1)} %get-tuple-element.108), channel_id=1, source_target_pairs={{0,1},{1,0},{2,3},{3,2},{4,5},{5,4},{6,7},{7,6},{8,9},{9,8},{10,11... | collective-permute-start | bytes 3145736 | tf_op jit(solution)/shard_map/ppermute | solution.py:510
  113.4 44.0 %collective-permute-start.19 = (f32[256,1024]{1,0:T(8,128)S(1)}, f32[256,1024]{1,0:T(8,128)S(1)}, u32[]{:S(2)}, u32[]{:S(2)}) collective-permute-start(f32[256,1024]{1,0:T(8,128)S(1)} %get-tuple-element.109.refs_0_), channel_id=1, source_target_pairs={{0,2},{2,0},{1,3},{3,1},{4,6},{6,4},{5,7},{7,5},{8,10},{10,8},{9,1... | collective-permute-start | bytes 3145736 | tf_op jit(solution)/shard_map/ppermute | solution.py:510
  115.4 40.1 %collective-permute-start.13 = (f32[256,768]{1,0:T(8,128)S(1)}, f32[256,768]{1,0:T(8,128)S(1)}, u32[]{:S(2)}, u32[]{:S(2)}) collective-permute-start(f32[256,768]{1,0:T(8,128)S(1)} %pad_maximum_fusion.refs_0_), channel_id=1, source_target_pairs={{0,2},{2,0},{1,3},{3,1},{4,6},{6,4},{5,7},{7,5},{8,10},{10,8},{9,1... | collective-permute-start | bytes 2359304 | tf_op jit(solution)/shard_map/ppermute | solution.py:514
  127.8 78.7 %collective-permute-start.12 = (f32[256,768]{1,0:T(8,128)S(1)}, f32[256,768]{1,0:T(8,128)S(1)}, u32[]{:S(2)}, u32[]{:S(2)}) collective-permute-start(f32[256,768]{1,0:T(8,128)S(1)} %pad_maximum_fusion.refs_0_), channel_id=1, source_target_pairs={{0,1},{1,0},{2,3},{3,2},{4,5},{5,4},{6,7},{7,6},{8,9},{9,8},{10,11... | collective-permute-start | bytes 2359304 | tf_op jit(solution)/shard_map/ppermute | solution.py:515
  155.5 40.2 %collective-permute-start.20 = (f32[256,1024]{1,0:T(8,128)S(1)}, f32[256,1024]{1,0:T(8,128)S(1)}, u32[]{:S(2)}, u32[]{:S(2)}) collective-permute-start(f32[256,1024]{1,0:T(8,128)S(1)} %get-tuple-element.108), channel_id=1, source_target_pairs={{0,3},{3,0},{1,2},{2,1},{4,7},{7,4},{5,6},{6,5},{8,11},{11,8},{9,1... | collective-permute-start | bytes 3145736 | tf_op jit(solution)/shard_map/ppermute | solution.py:510
  156.0 50.4 %collective-permute-start.14 = (f32[256,768]{1,0:T(8,128)S(1)}, f32[256,768]{1,0:T(8,128)S(1)}, u32[]{:S(2)}, u32[]{:S(2)}) collective-permute-start(f32[256,768]{1,0:T(8,128)S(1)} %collective-permute-done.13.refs_2_), channel_id=1, source_target_pairs={{0,1},{1,0},{2,3},{3,2},{4,5},{5,4},{6,7},{7,6},{8,9},{9,8},{10,11... | collective-permute-start | bytes 2359304 | tf_op jit(solution)/shard_map/ppermute | solution.py:516
  157.4 57.5 %collective-permute-start.2 = (f32[1408,256]{1,0:T(8,128)S(1)}, f32[1408,256]{1,0:T(8,128)S(1)}, u32[]{:S(2)}, u32[]{:S(2)}) collective-permute-start(f32[1408,256]{1,0:T(8,128)S(1)} %slice.32), channel_id=1, source_target_pairs={{0,4},{4,0},{8,12},{12,8},{1,5},{5,1},{9,13},{13,9},{2,6},{6,2},{1... | collective-permute-start | bytes 4325384 | tf_op jit(solution)/shard_map/ppermute | solution.py:549
  158.9 55.9 %collective-permute-start.3 = (f32[1408,256]{1,0:T(8,128)S(1)}, f32[1408,256]{1,0:T(8,128)S(1)}, u32[]{:S(2)}, u32[]{:S(2)}) collective-permute-start(f32[1408,256]{1,0:T(8,128)S(1)} %slice.33), channel_id=1, source_target_pairs={{0,8},{8,0},{4,12},{12,4},{1,9},{9,1},{5,13},{13,5},{2,10},{10,2},... | collective-permute-start | bytes 4325384 | tf_op jit(solution)/shard_map/ppermute | solution.py:549
  206.5 73.7 %collective-permute-start.21 = (f32[1024,1024]{1,0:T(8,128)}, f32[1024,1024]{1,0:T(8,128)}, u32[]{:S(2)}, u32[]{:S(2)}) collective-permute-start(f32[1024,1024]{1,0:T(8,128)} %shard_map.46.mine_ref.refs_3_), channel_id=1, source_target_pairs={{0,1},{1,0},{2,3},{3,2},{4,5},{5,4},{6,7},{7,6},{8,9},{9,8},{10,11... | collective-permute-start | bytes 12582920 | tf_op jit(solution)/shard_map/ppermute | solution.py:557
  214.8 28.0 %copy-start.6 = (f32[1024,768]{1,0:T(8,128)S(1)}, f32[1024,768]{1,0:T(8,128)}, u32[]{:S(2)}) copy-start(f32[1024,768]{1,0:T(8,128)} %shard_map.44.refs_2_) | copy-start | bytes 9437188
  276.6 246.2 %all-gather.9.cloned.1.call-start = ((), (), s32[]{:S(2)}) async-start(), calls=%async_computation.1 | async-start | bytes 4456448 | tf_op jit(solution)/shard_map/all_gather | solution.py:535
  276.6 137.7 %collective-permute-start.15 = (f32[2560,256]{1,0:T(8,128)}, f32[2560,256]{1,0:T(8,128)}, u32[]{:S(2)}, u32[]{:S(2)}) collective-permute-start(f32[2560,256]{1,0:T(8,128)} %get-tuple-element.60.refs_0_), channel_id=1, source_target_pairs={{0,4},{4,0},{8,12},{12,8},{1,5},{5,1},{9,13},{13,9},{2,6},{6,2},{1... | collective-permute-start | bytes 7864328 | tf_op jit(solution)/shard_map/ppermute | solution.py:536
  277.2 137.1 %collective-permute-start.16 = (f32[2560,256]{1,0:T(8,128)}, f32[2560,256]{1,0:T(8,128)}, u32[]{:S(2)}, u32[]{:S(2)}) collective-permute-start(f32[2560,256]{1,0:T(8,128)} %get-tuple-element.60.refs_0_), channel_id=1, source_target_pairs={{0,8},{8,0},{4,12},{12,4},{1,9},{9,1},{5,13},{13,5},{2,10},{10,2},... | collective-permute-start | bytes 7864328 | tf_op jit(solution)/shard_map/ppermute | solution.py:537
  277.7 136.6 %collective-permute-start.17 = (f32[2560,256]{1,0:T(8,128)}, f32[2560,256]{1,0:T(8,128)}, u32[]{:S(2)}, u32[]{:S(2)}) collective-permute-start(f32[2560,256]{1,0:T(8,128)} %get-tuple-element.60.refs_0_), channel_id=1, source_target_pairs={{0,12},{12,0},{4,8},{8,4},{1,13},{13,1},{5,9},{9,5},{2,14},{14,2},... | collective-permute-start | bytes 7864328 | tf_op jit(solution)/shard_map/ppermute | solution.py:546
  294.0 51.0 %collective-permute-start.22 = (f32[256,1536]{1,0:T(8,128)}, f32[256,1536]{1,0:T(8,128)S(1)}, u32[]{:S(2)}, u32[]{:S(2)}) collective-permute-start(f32[256,1536]{1,0:T(8,128)} %get-tuple-element.69), channel_id=1, source_target_pairs={{0,1},{1,0},{2,3},{3,2},{4,5},{5,4},{6,7},{7,6},{8,9},{9,8},{10,11... | collective-permute-start | bytes 4718600 | tf_op jit(solution)/shard_map/ppermute | solution.py:510
  294.0 103.2 %collective-permute-start.24 = (f32[256,1536]{1,0:T(8,128)}, f32[256,1536]{1,0:T(8,128)}, u32[]{:S(2)}, u32[]{:S(2)}) collective-permute-start(f32[256,1536]{1,0:T(8,128)} %get-tuple-element.69), channel_id=1, source_target_pairs={{0,3},{3,0},{1,2},{2,1},{4,7},{7,4},{5,6},{6,5},{8,11},{11,8},{9,1... | collective-permute-start | bytes 4718600 | tf_op jit(solution)/shard_map/ppermute | solution.py:510
  294.8 50.2 %copy-start.3 = (f32[256,1536]{1,0:T(8,128)S(1)}, f32[256,1536]{1,0:T(8,128)}, u32[]{:S(2)}) copy-start(f32[256,1536]{1,0:T(8,128)} %get-tuple-element.68.refs_0_) | copy-start | bytes 4718596
  345.0 52.2 %collective-permute-start.23 = (f32[256,1536]{1,0:T(8,128)S(1)}, f32[256,1536]{1,0:T(8,128)S(1)}, u32[]{:S(2)}, u32[]{:S(2)}) collective-permute-start(f32[256,1536]{1,0:T(8,128)S(1)} %copy-done.3), channel_id=1, source_target_pairs={{0,2},{2,0},{1,3},{3,1},{4,6},{6,4},{5,7},{7,5},{8,10},{10,8},{9,1... | collective-permute-start | bytes 4718600 | tf_op jit(solution)/shard_map/ppermute | solution.py:510
  414.3 50.9 %collective-permute-start.28 = (f32[1024,1024]{1,0:T(8,128)}, f32[1024,1024]{1,0:T(8,128)}, u32[]{:S(2)}, u32[]{:S(2)}) collective-permute-start(f32[1024,1024]{1,0:T(8,128)} %get-tuple-element.75.mine_ref.refs_3_), channel_id=1, source_target_pairs={{0,1},{1,0},{2,3},{3,2},{4,5},{5,4},{6,7},{7,6},{8,9},{9,8},{10,11... | collective-permute-start | bytes 12582920 | tf_op jit(solution)/shard_map/ppermute | solution.py:557
  461.6 230.5 %all-gather.11.cloned.1.call-start = ((), (), s32[]{:S(2)}) async-start(), calls=%async_computation.2 | async-start | bytes 4456448 | tf_op jit(solution)/shard_map/all_gather | solution.py:535
  461.6 112.0 %collective-permute-start.25 = (f32[2304,256]{1,0:T(8,128)}, f32[2304,256]{1,0:T(8,128)}, u32[]{:S(2)}, u32[]{:S(2)}) collective-permute-start(f32[2304,256]{1,0:T(8,128)} %get-tuple-element.72.refs_0_), channel_id=1, source_target_pairs={{0,4},{4,0},{8,12},{12,8},{1,5},{5,1},{9,13},{13,9},{2,6},{6,2},{1... | collective-permute-start | bytes 7077896 | tf_op jit(solution)/shard_map/ppermute | solution.py:536
  462.3 117.4 %collective-permute-start.26 = (f32[2304,256]{1,0:T(8,128)}, f32[2304,256]{1,0:T(8,128)}, u32[]{:S(2)}, u32[]{:S(2)}) collective-permute-start(f32[2304,256]{1,0:T(8,128)} %get-tuple-element.72.refs_0_), channel_id=1, source_target_pairs={{0,8},{8,0},{4,12},{12,4},{1,9},{9,1},{5,13},{13,5},{2,10},{10,2},... | collective-permute-start | bytes 7077896 | tf_op jit(solution)/shard_map/ppermute | solution.py:537
  462.8 116.9 %collective-permute-start.27 = (f32[2304,256]{1,0:T(8,128)}, f32[2304,256]{1,0:T(8,128)}, u32[]{:S(2)}, u32[]{:S(2)}) collective-permute-start(f32[2304,256]{1,0:T(8,128)} %get-tuple-element.72.refs_0_), channel_id=1, source_target_pairs={{0,12},{12,0},{4,8},{8,4},{1,13},{13,1},{5,9},{9,5},{2,14},{14,2},... | collective-permute-start | bytes 7077896 | tf_op jit(solution)/shard_map/ppermute | solution.py:546
  478.8 124.3 %collective-permute-start.29 = (f32[256,1280]{1,0:T(8,128)}, f32[256,1280]{1,0:T(8,128)}, u32[]{:S(2)}, u32[]{:S(2)}) collective-permute-start(f32[256,1280]{1,0:T(8,128)} %get-tuple-element.83), channel_id=1, source_target_pairs={{0,1},{1,0},{2,3},{3,2},{4,5},{5,4},{6,7},{7,6},{8,9},{9,8},{10,11... | collective-permute-start | bytes 3932168 | tf_op jit(solution)/shard_map/ppermute | solution.py:510
  478.8 125.7 %collective-permute-start.31 = (f32[256,1280]{1,0:T(8,128)}, f32[256,1280]{1,0:T(8,128)}, u32[]{:S(2)}, u32[]{:S(2)}) collective-permute-start(f32[256,1280]{1,0:T(8,128)} %get-tuple-element.83), channel_id=1, source_target_pairs={{0,3},{3,0},{1,2},{2,1},{4,7},{7,4},{5,6},{6,5},{8,11},{11,8},{9,1... | collective-permute-start | bytes 3932168 | tf_op jit(solution)/shard_map/ppermute | solution.py:510
  522.8 51.0 %copy-start.4 = (f32[256,1280]{1,0:T(8,128)S(1)}, f32[256,1280]{1,0:T(8,128)}, u32[]{:S(2)}) copy-start(f32[256,1280]{1,0:T(8,128)} %get-tuple-element.82.refs_0_) | copy-start | bytes 3932164
  573.7 30.7 %collective-permute-start.30 = (f32[256,1280]{1,0:T(8,128)S(1)}, f32[256,1280]{1,0:T(8,128)S(1)}, u32[]{:S(2)}, u32[]{:S(2)}) collective-permute-start(f32[256,1280]{1,0:T(8,128)S(1)} %copy-done.4), channel_id=1, source_target_pairs={{0,2},{2,0},{1,3},{3,1},{4,6},{6,4},{5,7},{7,5},{8,10},{10,8},{9,1... | collective-permute-start | bytes 3932168 | tf_op jit(solution)/shard_map/ppermute | solution.py:510
  631.9 7.4 collective-permute-start.32
  653.8 89.0 %collective-permute-start.36 = (f32[256,1024]{1,0:T(8,128)}, f32[256,1024]{1,0:T(8,128)S(1)}, u32[]{:S(2)}, u32[]{:S(2)}) collective-permute-start(f32[256,1024]{1,0:T(8,128)} %get-tuple-element.96), channel_id=1, source_target_pairs={{0,1},{1,0},{2,3},{3,2},{4,5},{5,4},{6,7},{7,6},{8,9},{9,8},{10,11... | collective-permute-start | bytes 3145736 | tf_op jit(solution)/shard_map/ppermute | solution.py:510
  653.9 88.9 %collective-permute-start.38 = (f32[256,1024]{1,0:T(8,128)}, f32[256,1024]{1,0:T(8,128)S(1)}, u32[]{:S(2)}, u32[]{:S(2)}) collective-permute-start(f32[256,1024]{1,0:T(8,128)} %get-tuple-element.96), channel_id=1, source_target_pairs={{0,3},{3,0},{1,2},{2,1},{4,7},{7,4},{5,6},{6,5},{8,11},{11,8},{9,1... | collective-permute-start | bytes 3145736 | tf_op jit(solution)/shard_map/ppermute | solution.py:510
  655.2 87.7 %collective-permute-start.37 = (f32[256,1024]{1,0:T(8,128)}, f32[256,1024]{1,0:T(8,128)S(1)}, u32[]{:S(2)}, u32[]{:S(2)}) collective-permute-start(f32[256,1024]{1,0:T(8,128)} %get-tuple-element.95.refs_0_), channel_id=1, source_target_pairs={{0,2},{2,0},{1,3},{3,1},{4,6},{6,4},{5,7},{7,5},{8,10},{10,8},{9,1... | collective-permute-start | bytes 3145736 | tf_op jit(solution)/shard_map/ppermute | solution.py:510
  692.1 50.8 %copy-start.5 = (f32[256,1024]{1,0:T(8,128)S(1)}, f32[256,1024]{1,0:T(8,128)}, u32[]{:S(2)}) copy-start(f32[256,1024]{1,0:T(8,128)} %get-tuple-element.95.refs_0_) | copy-start | bytes 3145732
  742.9 10.8 %copy-start.10 = (f32[2048,256]{1,0:T(8,128)S(1)}, f32[2048,256]{1,0:T(8,128)}, u32[]{:S(2)}) copy-start(f32[2048,256]{1,0:T(8,128)} %get-tuple-element.92.refs_0_) | copy-start | bytes 6291460
  753.6 114.4 %collective-permute-start.39 = (f32[1024,1024]{1,0:T(8,128)}, f32[1024,1024]{1,0:T(8,128)S(1)}, u32[]{:S(2)}, u32[]{:S(2)}) collective-permute-start(f32[1024,1024]{1,0:T(8,128)} %shard_map.63.mine_ref), channel_id=1, source_target_pairs={{0,1},{1,0},{2,3},{3,2},{4,5},{5,4},{6,7},{7,6},{8,9},{9,8},{10,11... | collective-permute-start | bytes 12582920 | tf_op jit(solution)/shard_map/ppermute | solution.py:557
  753.7 48.5 %collective-permute-start.33 = (f32[2048,256]{1,0:T(8,128)S(1)}, f32[2048,256]{1,0:T(8,128)S(1)}, u32[]{:S(2)}, u32[]{:S(2)}) collective-permute-start(f32[2048,256]{1,0:T(8,128)S(1)} %copy-done.10), channel_id=1, source_target_pairs={{0,4},{4,0},{8,12},{12,8},{1,5},{5,1},{9,13},{13,9},{2,6},{6,2},{1... | collective-permute-start | bytes 6291464 | tf_op jit(solution)/shard_map/ppermute | solution.py:536
  754.8 92.6 %collective-permute-start.34 = (f32[2048,256]{1,0:T(8,128)S(1)}, f32[2048,256]{1,0:T(8,128)S(1)}, u32[]{:S(2)}, u32[]{:S(2)}) collective-permute-start(f32[2048,256]{1,0:T(8,128)S(1)} %copy-done.10), channel_id=1, source_target_pairs={{0,8},{8,0},{4,12},{12,4},{1,9},{9,1},{5,13},{13,5},{2,10},{10,2},... | collective-permute-start | bytes 6291464 | tf_op jit(solution)/shard_map/ppermute | solution.py:537
  754.8 92.6 %collective-permute-start.35 = (f32[2048,256]{1,0:T(8,128)S(1)}, f32[2048,256]{1,0:T(8,128)S(1)}, u32[]{:S(2)}, u32[]{:S(2)}) collective-permute-start(f32[2048,256]{1,0:T(8,128)S(1)} %copy-done.10), channel_id=1, source_target_pairs={{0,12},{12,0},{4,8},{8,4},{1,13},{13,1},{5,9},{9,5},{2,14},{14,2},... | collective-permute-start | bytes 6291464 | tf_op jit(solution)/shard_map/ppermute | solution.py:546
  (7 other events, 16.6 us)
Sparse Core Ops, SparseCore 0:
  276.7 47.1 all-gather.6
  461.7 47.3 all-gather.8
  632.1 41.8 all-gather.10

commit v5 on v4

--- a/solution.py
+++ b/solution.py
@@ -12,6 +12,7 @@
 BF16 = jnp.bfloat16
 HIGH = lax.Precision.HIGHEST
 NB = 256
+LANES = 128
 SUP = 1024
 MIB = 1024 * 1024
 
@@ -35,27 +36,26 @@
     return high, mid, (rest - mid.astype(F32)).astype(BF16)
 
 
-def panel32(work, p, filler=lambda k: None):
+def panel32(work, p, filler=lambda: None):
     r0 = 32 * p
     diag_tile = p // 4
-    lane0 = r0 % 128
+    lane0 = r0 % LANES
     tiles = [0, 1, 2] if p < 4 else [1, 2, 3]
-    rows = {ti: [work[r0 + 8 * sg:r0 + 8 * sg + 8, 128 * ti:128 * ti + 128] for sg in range(4)] for ti in tiles}
-    sub_id = lax.broadcasted_iota(jnp.int32, (8, 128), 0)
+    rows = {ti: [work[r0 + 8 * sg:r0 + 8 * sg + 8, LANES * ti:LANES * ti + LANES] for sg in range(4)] for ti in tiles}
+    sub_id = lax.broadcasted_iota(jnp.int32, (8, LANES), 0)
 
     def over_lanes(u, sg):
-        return jnp.broadcast_to(rows[diag_tile][sg][:, lane0 + u:lane0 + u + 1], (8, 128))
+        return jnp.broadcast_to(rows[diag_tile][sg][:, lane0 + u:lane0 + u + 1], (8, LANES))
 
     def over_sublanes(v, i):
-        return jnp.broadcast_to(v[i:i + 1, :], (8, 128))
+        return jnp.broadcast_to(v[i:i + 1, :], (8, LANES))
 
     col, fac = {}, {}
     for u in range(16):
         for sg in range(u // 8, 4):
             col[u, sg] = over_lanes(u, sg)
+    filler()
     for g in range(4):
-        if g < 3:
-            filler(g)
         for t in range(8 * g, 8 * g + 8):
             tt = t - 8 * g
             rs = lax.rsqrt(over_sublanes(col[t, g], tt))
@@ -63,7 +63,7 @@
                 fac[t, sg] = col[t, sg] * rs
             for u in range(t + 1, min(8 * g + 16, 32)):
                 ug = u // 8
-                s = over_sublanes(fac[t, ug], u - 8 * ug)
+                s = over_sublanes(col[t, ug], u - 8 * ug) * rs if u == t + 1 else over_sublanes(fac[t, ug], u - 8 * ug)
                 for sg in range(ug, 4):
                     col[u, sg] = col[u, sg] - fac[t, sg] * s
             for ti in tiles:
@@ -78,20 +78,18 @@
                     col[u, sg] = over_lanes(u, sg)
     for ti in tiles:
         for sg in range(4):
-            work[r0 + 8 * sg:r0 + 8 * sg + 8, 128 * ti:128 * ti + 128] = rows[ti][sg]
+            work[r0 + 8 * sg:r0 + 8 * sg + 8, LANES * ti:LANES * ti + LANES] = rows[ti][sg]
     if p == 7:
-        filler(3)
         return
     high, mid, low = split3(jnp.concatenate([jnp.concatenate(rows[ti], axis=0) for ti in tiles], axis=1))
-    first = (r0 + 32 - 128 * diag_tile) // 128 * 128
+    first = (r0 + 32 - LANES * diag_tile) // LANES * LANES
     rhs = jnp.concatenate([high, mid, high, mid, low, high], axis=0)
-    lhs = jnp.concatenate([high, high, mid, mid, high, low], axis=0)[:, first:256 - 128 * diag_tile]
+    lhs = jnp.concatenate([high, high, mid, mid, high, low], axis=0)[:, first:256 - LANES * diag_tile]
     upd = lax.dot_general(lhs, rhs, (((0,), (0,)), ((), ())), preferred_element_type=F32)
-    filler(3)
-    skip = r0 + 32 - first - 128 * diag_tile
+    skip = r0 + 32 - first - LANES * diag_tile
     for j, ti in enumerate(tiles):
-        lanes = slice(128 * ti, 128 * ti + 128)
-        work[r0 + 32:256, lanes] = work[r0 + 32:256, lanes] - upd[skip:, 128 * j:128 * j + 128]
+        lanes = slice(LANES * ti, LANES * ti + LANES)
+        work[r0 + 32:256, lanes] = work[r0 + 32:256, lanes] - upd[skip:, LANES * j:LANES * j + LANES]
 
 
 def spread_factor(b, u_ref, x_ref, work):
@@ -114,7 +112,7 @@
             x_ref[lo:lo + NB, :e] = x_ref[lo:lo + NB, :e] - dot_tn(uc, x_ref[a:e, :e])
 
 
-def factor_block(b, u_ref, x_ref, own_l_ref, own_diag_ref, work, filler=lambda p, k: None):
+def factor_block(b, u_ref, x_ref, own_l_ref, own_diag_ref, work, filler=lambda p: None):
     row = lax.broadcasted_iota(jnp.int32, (NB, NB), 0)
     col = lax.broadcasted_iota(jnp.int32, (NB, NB), 1)
     at = pl.ds(pl.multiple_of(b * NB, NB), NB)
@@ -153,6 +151,10 @@
     return pl.pallas_call(kernel, cost_estimate=cost, compiler_params=pltpu.CompilerParams(vmem_limit_bytes=vmem * MIB), **kw)
 
 
+def fixed(*dims):
+    return pl.BlockSpec(dims, lambda *ids: (0,) * len(dims))
+
+
 def in_hbm(x):
     return pltpu.with_memory_space_constraint(x, pltpu.HBM)
 
@@ -175,7 +177,7 @@
 
 
 def flat_panel(panel):
-    return panel.reshape(-1, 4, 2, 128).transpose(0, 2, 1, 3).reshape(-1, 128)
+    return panel.reshape(-1, 4, 2, LANES).transpose(0, 2, 1, 3).reshape(-1, LANES)
 
 
 def dot_parts(a, b):
@@ -192,7 +194,7 @@
     my_row = lax.axis_index("pr")
 
     def landing_copy(k, w):
-        at = pl.ds(128 * k, 128)
+        at = pl.ds(LANES * k, LANES)
         return pltpu.make_async_copy((mine_ref, theirs_ref)[w].at[at], landing.at[w, at], land_sem.at[2 * k + w])
 
     def block_copy(n):
@@ -212,7 +214,7 @@
                 landing_copy(k, w).wait()
 
                 def split_rows(i, carry, k=k, w=w):
-                    at = pl.ds(pl.multiple_of(128 * k + 32 * i, 32), 32)
+                    at = pl.ds(pl.multiple_of(LANES * k + 32 * i, 32), 32)
                     for n, part in enumerate(split3(landing[w, at, :])):
                         u_parts[n, at, pl.ds(pl.multiple_of((half ^ w) * SUP, SUP), SUP)] = part
                     return carry
@@ -224,12 +226,14 @@
     for n, part in enumerate(split3(l_ref[...])):
         l_parts[n] = part
 
-    def piece(q, k):
-        deep, lanes = slice(NB * k, NB * k + NB), slice(NB * q, NB * q + NB)
-        total = dot_parts(lambda i: l_parts[i, :, deep], lambda j: u_parts[j, deep, lanes])
-        out_ref[:, lanes] = (trail_ref if k == 0 else out_ref)[:, lanes] - total
-
-    factor_block(b, u_ref, x_ref, own_l_ref, own_diag_ref, work, piece)
+    def beside(q):
+        lanes = slice(NB * q, NB * q + NB)
+        for k in range(4):
+            deep = slice(NB * k, NB * k + NB)
+            total = dot_parts(lambda i: l_parts[i, :, deep], lambda j: u_parts[j, deep, lanes])
+            out_ref[:, lanes] = (trail_ref if k == 0 else out_ref)[:, lanes] - total
+
+    factor_block(b, u_ref, x_ref, own_l_ref, own_diag_ref, work, beside)
 
 
 def factor_beside(blocks, source, trail, l_rows, mine, theirs):
@@ -257,14 +261,14 @@
 def unpack_kernel(in_ref, rest_ref):
     for n, s in enumerate((3, 2, 1)):
         for half in range(2):
-            rest_ref[:, NB * n + 128 * half:NB * n + 128 * half + 128] = in_ref[pl.ds(4 * half + s, NB, stride=8), :]
+            rest_ref[:, NB * n + LANES * half:NB * n + LANES * half + LANES] = in_ref[pl.ds(4 * half + s, NB, stride=8), :]
 
 
 def unpack(panel):
     rows = panel.shape[0] - NB
     return call(
         unpack_kernel, 1_000_000, 8 * rows * SUP, 12, grid=(rows // NB,), out_shape=shape(rows, 3 * NB),
-        in_specs=[pl.BlockSpec((8 * NB, 128), lambda i: (i + 1, 0))], out_specs=pl.BlockSpec((NB, 3 * NB), lambda i: (i, 0)),
+        in_specs=[pl.BlockSpec((8 * NB, LANES), lambda i: (i + 1, 0))], out_specs=pl.BlockSpec((NB, 3 * NB), lambda i: (i, 0)),
     )(flat_panel(panel))
 
 
@@ -272,7 +276,7 @@
     for s in range(4):
         value = jnp.where(n > s, cols[s][...], jnp.where(n == s, diags[s][...], 0.0))
         for half in range(2):
-            out_ref[pl.ds(4 * half + s, NB, stride=8), :] = value[:, 128 * half:128 * half + 128]
+            out_ref[pl.ds(4 * half + s, NB, stride=8), :] = value[:, LANES * half:LANES * half + LANES]
 
 
 def rows_kernel(*refs):
@@ -308,7 +312,7 @@
     return call(
         rows_kernel, 30 * rows * SUP * SUP // 4, 12 * rows * SUP, 34, grid=(4,),
         out_shape=(shape(rows, SUP), shape(rows, NB)),
-        in_specs=[block] * 3 + far_blocks + [pl.BlockSpec((SUP, SUP), lambda i: (0, 0))],
+        in_specs=[block] * 3 + far_blocks + [fixed(SUP, SUP)],
         out_specs=(pl.BlockSpec((tile, SUP), lambda i: (i, 0)), block),
         scratch_shapes=[pltpu.VMEM((tile, SUP), F32)],
     )(in_hbm(own), y, z, *far, x)
@@ -342,7 +346,7 @@
     specs = [pl.BlockSpec((SUP, NB), lambda i: (0, jnp.minimum(i, min(SUP, cols) // NB - 1))), pl.BlockSpec((SUP, NB), lambda i: (0, jnp.maximum(i - 4, 0)))]
     return call(
         cols_kernel, 30 * cols * SUP * SUP // 4, 12 * cols * SUP, 20, grid=(cols // NB,), out_shape=outs,
-        in_specs=[pl.BlockSpec((NB, NB), lambda i: (0, i))] * 4 + [pl.BlockSpec((SUP, SUP), lambda i: (0, 0))],
+        in_specs=[pl.BlockSpec((NB, NB), lambda i: (0, i))] * 4 + [fixed(SUP, SUP)],
         out_specs=specs[:len(outs)], scratch_shapes=[pltpu.VMEM((SUP, NB), F32), pltpu.VMEM((SUP, NB), F32)],
     )(*pieces, x)
 
@@ -384,14 +388,13 @@
     rows, width = rest.shape
     keep = width - NB
     below = lambda i: (jnp.maximum(i - 1, 0), 0)
-    zero = lambda i: (0, 0)
     outs = [shape(NB, NB), shape(rows - NB, NB)] + ([shape(NB, keep), shape(rows - NB, keep)] if keep else [])
-    specs = [pl.BlockSpec((NB, NB), zero), pl.BlockSpec((NB, NB), below)]
+    specs = [fixed(NB, NB), pl.BlockSpec((NB, NB), below)]
     if keep:
-        specs += [pl.BlockSpec((NB, keep), zero), pl.BlockSpec((NB, keep), below)]
+        specs += [fixed(NB, keep), pl.BlockSpec((NB, keep), below)]
     return call(
         panel_kernel, 12 * rows * width * SUP, 8 * rows * width + 4 * rows * SUP, 26, grid=(rows // NB,), out_shape=outs,
-        in_specs=[pl.BlockSpec((NB, width), lambda i: (i, 0)), pl.BlockSpec((NB, SUP), lambda i: (i, 0)), pl.BlockSpec((SUP, width), zero)],
+        in_specs=[pl.BlockSpec((NB, width), lambda i: (i, 0)), pl.BlockSpec((NB, SUP), lambda i: (i, 0)), fixed(SUP, width)],
         out_specs=specs, scratch_shapes=[pltpu.VMEM((3, NB, SUP), BF16), pltpu.VMEM((3, SUP, width), BF16)],
     )(in_hbm(rest), in_hbm(l_rows), u_panel)
 
@@ -417,14 +420,14 @@
 def update_row(core, trail, l_rows, mine, theirs, panel_row, step):
     extra = [] if panel_row is None else [panel_row]
     width = SUP + (0 if panel_row is None else panel_row.shape[1])
-    out = pl.BlockSpec((NB, width), lambda j, h: (0, 0))
+    out = fixed(NB, width)
     return call(
         row_kernel, 24 * NB * SUP * SUP, 12 * SUP * SUP, 30,
         grid_spec=pltpu.PrefetchScalarGridSpec(
             num_scalar_prefetch=1, grid=(4,),
-            in_specs=[pl.BlockSpec((NB, SUP // 2), lambda j, h: (step + 1, 2 * (h[0] ^ (j // 2)) + j % 2)), pl.BlockSpec((NB, SUP), lambda j, h: (0, 0)),
+            in_specs=[pl.BlockSpec((NB, SUP // 2), lambda j, h: (step + 1, 2 * (h[0] ^ (j // 2)) + j % 2)), fixed(NB, SUP),
                       pl.BlockSpec((SUP, SUP // 2), lambda j, h: (0, jnp.minimum(j, 1))), pl.BlockSpec((SUP, SUP // 2), lambda j, h: (0, jnp.maximum(j - 2, 0)))]
-            + [pl.BlockSpec(a.shape, lambda j, h: (0, 0)) for a in extra],
+            + [fixed(*a.shape) for a in extra],
             out_specs=(out, out)),
         out_shape=(shape(NB, width), shape(NB, width)),
     )(core, trail, in_hbm(l_rows), in_hbm(mine), in_hbm(theirs), *extra)
@@ -474,14 +477,14 @@
     at = pl.BlockSpec((NB, SUP), lambda j, i, h: (jnp.where(i == 0, step, step + off + i), h[0] ^ j))
     anywhere = pl.BlockSpec(memory_space=pl.ANY)
     ins = [at, pl.BlockSpec((NB, SUP), lambda j, i, h: (jnp.maximum(i, 1) - 1 + off, 0)), anywhere, anywhere,
-           pl.BlockSpec((NB, NB), lambda j, i, h: (0, 0))]
+           fixed(NB, NB)]
     outs, shapes = [at], [shape(rows, cols)]
     if out_cols:
         block = lambda j, i: jnp.clip(j * (count - 1) + i - 1, 0, rows // NB - 1)
         ins += [pl.BlockSpec((NB, NB), lambda j, i, h, s=s: (jnp.maximum(block(j, i) - s - 1, 0), 0)) for s in range(4)]
-        ins += [pl.BlockSpec((NB, NB), lambda j, i, h: (0, 0))] * 4
-        outs.append(pl.BlockSpec((8 * NB, 128), lambda j, i, h: (block(j, i), 0)))
-        shapes.append(shape(rows * 8, 128))
+        ins += [fixed(NB, NB)] * 4
+        outs.append(pl.BlockSpec((8 * NB, LANES), lambda j, i, h: (block(j, i), 0)))
+        shapes.append(shape(rows * 8, LANES))
     return call(
         trail_kernel, 12 * count * NB * cols * SUP, 8 * count * NB * cols, 32,
         grid_spec=pltpu.PrefetchScalarGridSpec(num_scalar_prefetch=1, grid=(2, count), in_specs=ins, out_specs=outs, scratch_shapes=[
@@ -564,7 +567,7 @@
                 keep, send = update_row(core, trail, l_rows, mine, theirs, panel_row, step)
         trail, flat = update_trail(core, trail, l_rows, mine, theirs, own_diag, 3, out_cols, out_diags)
         rows = trail.shape[0]
-        return flat.reshape(rows, 2, 4, 128).transpose(0, 2, 1, 3).reshape(rows, 4, NB), trail
+        return flat.reshape(rows, 2, 4, LANES).transpose(0, 2, 1, 3).reshape(rows, 4, NB), trail
 
     spec_panel = P("pr", "pc", None)
     spec_trail = P("pr", "pc")

time: 950 us -> 946 us (level)
  no operation moved by 1% of the time
where the time goes in v5:
time: 946 us; the launch traced here: 943 us
  Pallas kernels  654 us (69%)
  waiting for transfers between devices  206 us (22%)
  starting transfers between devices  37.6 us (4%)
  local copies, waits for them, and re-layouts  30.8 us (3%)
  between operations  14.3 us (2%)
    pallas_call x4, Pallas kernels, update_trail(): call(trail_kernel, 12 * count * NB * cols * SUP, 8 * count * NB * cols, 3...  199 us
    pallas_call x3, Pallas kernels, factor_beside(): call(fused_kernel, 100000000000, 1 << 25, 48, grid=(4,), out_shape=(near(...  149 us
    pallas_call x4, Pallas kernels, solve_rows(): call(rows_kernel, 30 * rows * SUP * SUP // 4, 12 * rows * SUP, 34, grid=(...  97.8 us
    pallas_call x3, Pallas kernels, update_panel(): call(panel_kernel, 12 * rows * width * SUP, 8 * rows * width + 4 * rows *...  68.3 us
    ppermute x3, waiting for transfers between devices, gather_diag(): at_y, at_z, at_x = (y(block), z(block), x(block))  64.2 us
    pallas_call x5, Pallas kernels, solve_cols(): call(cols_kernel, 30 * cols * SUP * SUP // 4, 12 * cols * SUP, 20, grid=(...  61.3 us
    ppermute x4, waiting for transfers between devices, local_part(): z = lax.ppermute(col_panel, 'pc', FLIP2)  51.2 us
    ppermute x4, waiting for transfers between devices, local_part(): y = lax.ppermute(col_panel, 'pc', FLIP1)  45 us
  transfers between devices with their start and end apart: 43, of which 10 were waited for; matrix products, arithmetic and copies ran while one was open for 2% of the time, Pallas kernels for 58%

profile of v5, /device:TPU:0, one launch (start us, length us, event | category | flops | bytes accessed | tf_op | source)
XLA Modules:
  0.0 942.7 jit_solution(5409110432509654320)
XLA Ops:
  9.9 3.2 collective-permute-start.4
  13.1 6.5 slice.24
  19.6 1.7 copy.20
  21.3 2.1 collective-permute-start.1
  23.4 1.9 collective-permute-start.7
  26.1 1.6 collective-permute-start.6
  28.4 64.2 %collective-permute-done.5 = f32[256,256]{1,0:T(8,128)S(1)} collective-permute-done((f32[256,256]{1,0:T(8,128)S(1)}, f32[256,256]{1,0:T(8,128)S(1)}, u32[]{:S(2)}, u32[]{:S(2)}) %collective-permute-start.5) | collective-permute-done | bytes 262176 | tf_op jit(solution)/shard_map/ppermute | solution.py:505
  92.6 1.9 collective-permute-start.8
  96.8 1.6 collective-permute-start.9
  101.0 5.0 collective-permute-done.9
  106.7 3.5 collective-permute-done.10
  110.9 1.9 constant_dynamic-slice_fusion
  113.4 1.9 collective-permute-start.19
  115.6 4.6 copy-done
  120.1 6.2 shard_map.41.refs_0_
  127.9 27.6 %collective-permute-done.13.refs_2_ = f32[256,768]{1,0:T(8,128)S(1)} collective-permute-done((f32[256,768]{1,0:T(8,128)S(1)}, f32[256,768]{1,0:T(8,128)S(1)}, u32[]{:S(2)}, u32[]{:S(2)}) %collective-permute-start.13) | collective-permute-done | bytes 786464 | tf_op jit(solution)/shard_map/ppermute | solution.py:517
  158.9 1.6 collective-permute-start.3
  160.5 34.7 %shard_map.42 = (f32[1024,1024]{1,0:T(8,128)S(1)}, f32[256,256]{1,0:T(8,128)}, f32[256,256]{1,0:T(8,128)}) custom-call(f32[8,256,256]{2,1,0:T(8,128)} %bitcast_dynamic-update-slice_fusion.refs_0_, f32[8,256,256]{2,1,0:T(8,128)} %collective-permute-done.11.refs_1_), custom_call_target="tpu_custom_call" | custom-call | flops 30000001024 | bytes 16777216 | tf_op jit(solution)/shard_map/pallas_call | solution.py:172
  195.1 10.8 %shard_map.46.mine_ref.refs_3_ = f32[1024,1024]{1,0:T(8,128)} custom-call(f32[256,1024]{1,0:T(8,128)S(1)} %get-tuple-element.109.refs_0_, f32[256,1024]{1,0:T(8,128)S(1)} %collective-permute-done.18.refs_1_, f32[256,1024]{1,0:T(8,128)S(1)} %collective-permute-done.19.refs_2_, f32[256,1024]{1,0:T(8,128)S(1)} %collective-permute-done.20.refs_3_, ...), custom_call_target="tpu_custom_call" | custom-call | flops 8053063680 | bytes 12582912 | tf_op jit(solution)/shard_map/pallas_call | solution.py:347
  206.0 8.3 shard_map.44.refs_2_
  214.3 28.0 %shard_map.43 = (f32[2816,1024]{1,0:T(8,128)}, f32[2816,256]{1,0:T(8,128)}) custom-call(f32[2816,256]{1,0:T(8,128)} %bitcast.40.refs_0_, f32[2816,256]{1,0:T(8,128)S(1)} %collective-permute-done.refs_1_, f32[2816,256]{1,0:T(8,128)} %collective-permute-done.1.refs_2_, f32[1408,256]{1,0:T(8,128)S(1)} %collective-permute-done.2.refs_3_, ...), custom_call_target="tpu_custom_call" | custom-call | flops 22145925120 | bytes 34603008 | tf_op jit(solution)/shard_map/pallas_call | solution.py:312
  242.3 33.7 %shard_map.45 = (f32[256,256]{1,0:T(8,128)}, f32[2560,256]{1,0:T(8,128)}, f32[256,512]{1,0:T(8,128)}, f32[2560,512]{1,0:T(8,128)}) custom-call(f32[2816,768]{1,0:T(8,128)} %shard_map.41.refs_0_, f32[2816,1024]{1,0:T(8,128)} %get-tuple-element.57.refs_1_.l_ref.refs_2_, f32[1024,768]{1,0:T(8,128)S(1)} %copy-done.6), custom_call_target="tpu_custom_call" | custom-call | flops 26575110144 | bytes 28835840 | tf_op jit(solution)/shard_map/pallas_call | solution.py:395
  277.1 2.5 collective-permute-start.17
  280.7 12.8 %shard_map.50 = (f32[256,1536]{1,0:T(8,128)}, f32[256,1536]{1,0:T(8,128)}) custom-call(s32[1]{0:T(128)} %bitcast.core_ref.refs_0_, f32[3072,2048]{1,0:T(8,128)} %refs_1_.1, f32[2816,1024]{1,0:T(8,128)} %get-tuple-element.57.refs_1_.l_ref.refs_2_, f32[1024,1024]{1,0:T(8,128)} %shard_map.46.mine_ref.refs_3_, ...), custom_call_target="tpu_custom_call" | custom-call | flops 6442450944 | bytes 12582912 | tf_op jit(solution)/shard_map/pallas_call | solution.py:424
  294.3 50.2 %shard_map.47.rest_0_ = f32[3072,2048]{1,0:T(8,128)} custom-call(s32[1]{0:T(128)} %bitcast.core_ref.refs_0_, f32[3072,2048]{1,0:T(8,128)} %refs_1_.1, f32[2816,1024]{1,0:T(8,128)} %get-tuple-element.57.refs_1_.l_ref.refs_2_, f32[1024,1024]{1,0:T(8,128)} %shard_map.46.mine_ref.refs_3_, f32[1024,1024]{1,0:T(8,128)} %collective-permute-done.21.theirs_ref.refs_4_, ...), custom_call_target="tpu_custom_call" | custom-call | flops 45097156608 | bytes 29360128 | tf_op jit(solution)/shard_map/pallas_call | solution.py:488
  345.9 49.7 %shard_map.48 = (f32[1024,1024]{1,0:T(8,128)S(1)}, f32[256,256]{1,0:T(8,128)}, f32[256,256]{1,0:T(8,128)}, f32[3072,2048]{1,0:T(8,128)}) custom-call(f32[16,256,256]{2,1,0:T(8,128)} %bitcast.47, f32[3072,2048]{1,0:T(8,128)} %refs_1_.1, f32[2816,1024]{1,0:T(8,128)} %get-tuple-element.57.refs_1_.l_ref.refs_2_, ...), custom_call_target="tpu_custom_call", output_to_operand_aliasing={{3}: (5, {})} | custom-call | flops 99999997952 | bytes 33554432 | tf_op jit(solution)/shard_map/pallas_call | solution.py:253
  395.6 17.0 %shard_map.51 = (f32[1024,1024]{1,0:T(8,128)}, f32[1024,512]{1,0:T(8,128)S(1)}) custom-call(f32[256,1536]{1,0:T(8,128)S(1)} %copy-done.3, f32[256,1536]{1,0:T(8,128)S(1)} %collective-permute-done.22.refs_1_, f32[256,1536]{1,0:T(8,128)S(1)} %collective-permute-done.23.refs_2_, f32[256,1536]{1,0:T(8,128)} %collective-permute-done.24.refs_3_, ...), custom_call_target="tpu_custom_call" | custom-call | flops 12079595520 | bytes 18874368 | tf_op jit(solution)/shard_map/pallas_call | solution.py:347
  412.7 25.8 %shard_map.49 = (f32[2560,1024]{1,0:T(8,128)}, f32[2560,256]{1,0:T(8,128)}) custom-call(f32[2560,256]{1,0:T(8,128)} %get-tuple-element.60.refs_0_, f32[2560,256]{1,0:T(8,128)} %collective-permute-done.15.refs_1_, f32[2560,256]{1,0:T(8,128)} %collective-permute-done.16.refs_2_, f32[2560,256]{1,0:T(8,128)} %collective-permute-done.17.refs_3_, ...), custom_call_target="tpu_custom_call" | custom-call | flops 20132659200 | bytes 31457280 | tf_op jit(solution)/shard_map/pallas_call | solution.py:312
  438.4 21.5 %shard_map.52 = (f32[256,256]{1,0:T(8,128)}, f32[2304,256]{1,0:T(8,128)}, f32[256,256]{1,0:T(8,128)}, f32[2304,256]{1,0:T(8,128)}) custom-call(f32[2560,512]{1,0:T(8,128)} %get-tuple-element.59.refs_0_, f32[2560,1024]{1,0:T(8,128)} %get-tuple-element.66.refs_1_.l_ref.refs_2_, f32[1024,512]{1,0:T(8,128)S(1)} %get-tuple-element.70.refs_2_), custom_call_target="tpu_custom_call" | custom-call | flops 16106127360 | bytes 20971520 | tf_op jit(solution)/shard_map/pallas_call | solution.py:395
  461.2 2.3 collective-permute-start.27
  464.5 12.6 %shard_map.56 = (f32[256,1280]{1,0:T(8,128)}, f32[256,1280]{1,0:T(8,128)}) custom-call(s32[1]{0:T(128)} %bitcast.core_ref.refs_0_, f32[3072,2048]{1,0:T(8,128)} %get-tuple-element.74.trail_ref.refs_1_, f32[2560,1024]{1,0:T(8,128)} %get-tuple-element.66.refs_1_.l_ref.refs_2_, f32[1024,1024]{1,0:T(8,128)} %get-tuple-element.75.mine_ref.refs_3_, ...), custom_call_target="tpu_custom_call" | custom-call | flops 6442450944 | bytes 12582912 | tf_op jit(solution)/shard_map/pallas_call | solution.py:424
  478.0 43.1 %shard_map.53.trail_ref = f32[3072,2048]{1,0:T(8,128)} custom-call(s32[1]{0:T(128)} %bitcast.core_ref.refs_0_, f32[3072,2048]{1,0:T(8,128)} %get-tuple-element.74.trail_ref.refs_1_, f32[2560,1024]{1,0:T(8,128)} %get-tuple-element.66.refs_1_.l_ref.refs_2_, f32[1024,1024]{1,0:T(8,128)} %get-tuple-element.75.mine_ref.refs_3_, ...), custom_call_target="tpu_custom_call", output_to_operand_aliasing={{}: (1, {})} | custom-call | flops 38654705664 | bytes 25165824 | tf_op jit(solution)/shard_map/pallas_call | solution.py:488
  521.1 49.8 %shard_map.54 = (f32[1024,1024]{1,0:T(8,128)S(1)}, f32[256,256]{1,0:T(8,128)}, f32[256,256]{1,0:T(8,128)}, f32[3072,2048]{1,0:T(8,128)}) custom-call(f32[16,256,256]{2,1,0:T(8,128)} %bitcast.48, f32[3072,2048]{1,0:T(8,128)} %shard_map.53.trail_ref, f32[2560,1024]{1,0:T(8,128)} %get-tuple-element.66.refs_1_.l_ref.refs_2_, ...), custom_call_target="tpu_custom_call", output_to_operand_aliasing={{3}: (1, {})} | custom-call | flops 99999997952 | bytes 33554432 | tf_op jit(solution)/shard_map/pallas_call | solution.py:253
  572.2 5.8 collective-permute-done.26.refs_2_
  578.1 23.4 %shard_map.55 = (f32[2304,1024]{1,0:T(8,128)}, f32[2304,256]{1,0:T(8,128)}) custom-call(f32[2304,256]{1,0:T(8,128)} %get-tuple-element.72.refs_0_, f32[2304,256]{1,0:T(8,128)} %collective-permute-done.25.refs_1_, f32[2304,256]{1,0:T(8,128)} %collective-permute-done.26.refs_2_, f32[2304,256]{1,0:T(8,128)} %collective-permute-done.27.refs_3_, ...), custom_call_target="tpu_custom_call" | custom-call | flops 18119393280 | bytes 28311552 | tf_op jit(solution)/shard_map/pallas_call | solution.py:312
  601.7 14.4 %shard_map.57 = (f32[1024,1024]{1,0:T(8,128)}, f32[1024,256]{1,0:T(8,128)S(1)}) custom-call(f32[256,1280]{1,0:T(8,128)S(1)} %copy-done.4, f32[256,1280]{1,0:T(8,128)} %collective-permute-done.29.refs_1_, f32[256,1280]{1,0:T(8,128)S(1)} %collective-permute-done.30.refs_2_, f32[256,1280]{1,0:T(8,128)} %collective-permute-done.31.refs_3_, ...), custom_call_target="tpu_custom_call" | custom-call | flops 10066329600 | bytes 15728640 | tf_op jit(solution)/shard_map/pallas_call | solution.py:347
  616.1 13.1 %shard_map.58 = (f32[256,256]{1,0:T(8,128)}, f32[2048,256]{1,0:T(8,128)}) custom-call(f32[2304,256]{1,0:T(8,128)} %get-tuple-element.71.refs_0_, f32[2304,1024]{1,0:T(8,128)} %get-tuple-element.80.refs_1_.l_ref.refs_2_, f32[1024,256]{1,0:T(8,128)S(1)} %get-tuple-element.84.refs_2_), custom_call_target="tpu_custom_call" | custom-call | flops 7247757312 | bytes 14155776 | tf_op jit(solution)/shard_map/pallas_call | solution.py:395
  629.3 7.4 collective-permute-done.32.theirs_ref.refs_4_
  636.6 2.1 copy-done.7
  638.7 12.3 %shard_map.62 = (f32[256,1024]{1,0:T(8,128)}, f32[256,1024]{1,0:T(8,128)}) custom-call(s32[1]{0:T(128)} %bitcast.core_ref.refs_0_, f32[3072,2048]{1,0:T(8,128)} %get-tuple-element.86.trail_ref.refs_1_, f32[2304,1024]{1,0:T(8,128)} %get-tuple-element.80.refs_1_.l_ref.refs_2_, f32[1024,1024]{1,0:T(8,128)} %get-tuple-element.87.mine_ref.refs_3_, ...), custom_call_target="tpu_custom_call" | custom-call | flops 6442450944 | bytes 12582912 | tf_op jit(solution)/shard_map/pallas_call | solution.py:424
  653.2 36.1 %shard_map.59.trail_ref = f32[3072,2048]{1,0:T(8,128)} custom-call(s32[1]{0:T(128)} %bitcast.core_ref.refs_0_, f32[3072,2048]{1,0:T(8,128)} %get-tuple-element.86.trail_ref.refs_1_, f32[2304,1024]{1,0:T(8,128)} %get-tuple-element.80.refs_1_.l_ref.refs_2_, f32[1024,1024]{1,0:T(8,128)} %get-tuple-element.87.mine_ref.refs_3_, ...), custom_call_target="tpu_custom_call", output_to_operand_aliasing={{}: (1, {})} | custom-call | flops 32212254720 | bytes 20971520 | tf_op jit(solution)/shard_map/pallas_call | solution.py:488
  689.4 49.6 %shard_map.60 = (f32[1024,1024]{1,0:T(8,128)S(1)}, f32[256,256]{1,0:T(8,128)}, f32[256,256]{1,0:T(8,128)}, f32[3072,2048]{1,0:T(8,128)}) custom-call(f32[16,256,256]{2,1,0:T(8,128)} %bitcast.49, f32[3072,2048]{1,0:T(8,128)} %shard_map.59.trail_ref, f32[2304,1024]{1,0:T(8,128)} %get-tuple-element.80.refs_1_.l_ref.refs_2_, ...), custom_call_target="tpu_custom_call", output_to_operand_aliasing={{3}: (1, {})} | custom-call | flops 99999997952 | bytes 33554432 | tf_op jit(solution)/shard_map/pallas_call | solution.py:253
  739.0 10.8 %shard_map.63.mine_ref = f32[1024,1024]{1,0:T(8,128)} custom-call(f32[256,1024]{1,0:T(8,128)S(1)} %copy-done.5, f32[256,1024]{1,0:T(8,128)S(1)} %collective-permute-done.36.refs_1_, f32[256,1024]{1,0:T(8,128)S(1)} %collective-permute-done.37.refs_2_, f32[256,1024]{1,0:T(8,128)S(1)} %collective-permute-done.38.refs_3_, f32[1024,1024]{1,0:T(8,128)S(1)} %get-tuple-element.93.refs_4_), custom_call_target="tpu_custom_call" | custom-call | flops 8053063680 | bytes 12582912 | tf_op jit(solution)/shard_map/pallas_call | solution.py:347
  753.3 45.0 %collective-permute-done.33.refs_1_ = f32[2048,256]{1,0:T(8,128)S(1)} collective-permute-done((f32[2048,256]{1,0:T(8,128)S(1)}, f32[2048,256]{1,0:T(8,128)S(1)}, u32[]{:S(2)}, u32[]{:S(2)}) %collective-permute-start.33) | collective-permute-done | bytes 2097184 | tf_op jit(solution)/shard_map/ppermute | solution.py:539
  798.3 45.4 %collective-permute-done.34.refs_2_ = f32[2048,256]{1,0:T(8,128)S(1)} collective-permute-done((f32[2048,256]{1,0:T(8,128)S(1)}, f32[2048,256]{1,0:T(8,128)S(1)}, u32[]{:S(2)}, u32[]{:S(2)}) %collective-permute-start.34) | collective-permute-done | bytes 2097184 | tf_op jit(solution)/shard_map/ppermute | solution.py:540
  843.7 20.6 %shard_map.61 = (f32[2048,1024]{1,0:T(8,128)}, f32[2048,256]{1,0:T(8,128)}) custom-call(f32[2048,256]{1,0:T(8,128)} %get-tuple-element.92.refs_0_, f32[2048,256]{1,0:T(8,128)S(1)} %collective-permute-done.33.refs_1_, f32[2048,256]{1,0:T(8,128)S(1)} %collective-permute-done.34.refs_2_, f32[2048,256]{1,0:T(8,128)S(1)} %collective-permute-done.35.refs_3_, ...), custom_call_target="tpu_custom_call" | custom-call | flops 16106127360 | bytes 25165824 | tf_op jit(solution)/shard_map/pallas_call | solution.py:312
  864.3 2.0 copy-done.9
  866.3 69.7 %shard_map.64 = (f32[3072,2048]{1,0:T(8,128)}, f32[24576,128]{1,0:T(8,128)}) custom-call(s32[1]{0:T(128)} %bitcast.core_ref.refs_0_, f32[3072,2048]{1,0:T(8,128)} %get-tuple-element.91.trail_ref, f32[2048,1024]{1,0:T(8,128)} %get-tuple-element.94.l_ref, f32[1024,1024]{1,0:T(8,128)} %shard_map.63.mine_ref, ...), custom_call_target="tpu_custom_call", output_to_operand_aliasing={{0}: (1, {})} | custom-call | flops 57982058496 | bytes 37748736 | tf_op jit(solution)/shard_map/pallas_call | solution.py:488
  (107 shorter events, 31.1 us)
Async XLA Ops:
  7.2 337.3 %all-gather.7.cloned.1.call-start = ((), (), s32[]{:S(2)}) async-start(), calls=%async_computation | async-start | bytes 4456448 | tf_op jit(solution)/shard_map/all_gather | solution.py:538
  9.9 16.2 %collective-permute-start.4 = (f32[256,256]{1,0:T(8,128)S(1)}, f32[256,256]{1,0:T(8,128)S(1)}, u32[]{:S(2)}, u32[]{:S(2)}) collective-permute-start(f32[256,256]{1,0:T(8,128)S(1)} %bitcast.43), channel_id=1, source_target_pairs={{0,4},{4,0},{8,12},{12,8},{1,5},{5,1},{9,13},{13,9},{2,6},{6,2},{1... | collective-permute-start | bytes 786440 | tf_op jit(solution)/shard_map/ppermute | solution.py:505
  21.3 106.4 %collective-permute-start = (f32[2816,256]{1,0:T(8,128)}, f32[2816,256]{1,0:T(8,128)S(1)}, u32[]{:S(2)}, u32[]{:S(2)}) collective-permute-start(f32[2816,256]{1,0:T(8,128)} %bitcast.40.refs_0_), channel_id=1, source_target_pairs={{0,4},{4,0},{8,12},{12,8},{1,5},{5,1},{9,13},{13,9},{2,6},{6,2},{1... | collective-permute-start | bytes 8650760 | tf_op jit(solution)/shard_map/ppermute | solution.py:539
  21.3 94.1 %collective-permute-start.1 = (f32[2816,256]{1,0:T(8,128)}, f32[2816,256]{1,0:T(8,128)}, u32[]{:S(2)}, u32[]{:S(2)}) collective-permute-start(f32[2816,256]{1,0:T(8,128)} %bitcast.40.refs_0_), channel_id=1, source_target_pairs={{0,8},{8,0},{4,12},{12,4},{1,9},{9,1},{5,13},{13,5},{2,10},{10,2},... | collective-permute-start | bytes 8650760 | tf_op jit(solution)/shard_map/ppermute | solution.py:540
  23.4 69.2 %collective-permute-start.5 = (f32[256,256]{1,0:T(8,128)S(1)}, f32[256,256]{1,0:T(8,128)S(1)}, u32[]{:S(2)}, u32[]{:S(2)}) collective-permute-start(f32[256,256]{1,0:T(8,128)S(1)} %bitcast.44), channel_id=1, source_target_pairs={{0,8},{8,0},{4,12},{12,4},{1,9},{9,1},{5,13},{13,5},{2,10},{10,2},... | collective-permute-start | bytes 786440 | tf_op jit(solution)/shard_map/ppermute | solution.py:505
  23.4 75.7 %collective-permute-start.7 = (f32[256,256]{1,0:T(8,128)S(1)}, f32[256,256]{1,0:T(8,128)S(1)}, u32[]{:S(2)}, u32[]{:S(2)}) collective-permute-start(f32[256,256]{1,0:T(8,128)S(1)} %bitcast.45), channel_id=1, source_target_pairs={{0,2},{2,0},{1,3},{3,1},{4,6},{6,4},{5,7},{7,5},{8,10},{10,8},{9,1... | collective-permute-start | bytes 786440 | tf_op jit(solution)/shard_map/ppermute | solution.py:505
  26.1 70.7 %collective-permute-start.6 = (f32[256,256]{1,0:T(8,128)S(1)}, f32[256,256]{1,0:T(8,128)S(1)}, u32[]{:S(2)}, u32[]{:S(2)}) collective-permute-start(f32[256,256]{1,0:T(8,128)S(1)} %collective-permute-done.4), channel_id=1, source_target_pairs={{0,8},{8,0},{4,12},{12,4},{1,9},{9,1},{5,13},{13,5},{2,10},{10,2},... | collective-permute-start | bytes 786440 | tf_op jit(solution)/shard_map/ppermute | solution.py:506
  92.6 7.7 collective-permute-start.8
  96.8 9.2 collective-permute-start.9
  99.2 11.1 %collective-permute-start.10 = (f32[256,256]{1,0:T(8,128)S(1)}, f32[256,256]{1,0:T(8,128)S(1)}, u32[]{:S(2)}, u32[]{:S(2)}) collective-permute-start(f32[256,256]{1,0:T(8,128)S(1)} %collective-permute-done.6), channel_id=1, source_target_pairs={{0,2},{2,0},{1,3},{3,1},{4,6},{6,4},{5,7},{7,5},{8,10},{10,8},{9,1... | collective-permute-start | bytes 786440 | tf_op jit(solution)/shard_map/ppermute | solution.py:507
  110.9 47.9 %collective-permute-start.11 = (f32[8,256,256]{2,1,0:T(8,128)}, f32[8,256,256]{2,1,0:T(8,128)}, u32[]{:S(2)}, u32[]{:S(2)}) collective-permute-start(f32[8,256,256]{2,1,0:T(8,128)} %bitcast_dynamic-update-slice_fusion.refs_0_), channel_id=1, source_target_pairs={{0,1},{1,0},{2,3},{3,2},{4,5},{5,4},{6,7},{7,6},{8,9},{9,8},{10,11... | collective-permute-start | bytes 6291464 | tf_op jit(solution)/shard_map/ppermute | solution.py:509
  112.8 43.2 %collective-permute-start.18 = (f32[256,1024]{1,0:T(8,128)S(1)}, f32[256,1024]{1,0:T(8,128)S(1)}, u32[]{:S(2)}, u32[]{:S(2)}) collective-permute-start(f32[256,1024]{1,0:T(8,128)S(1)} %get-tuple-element.108), channel_id=1, source_target_pairs={{0,1},{1,0},{2,3},{3,2},{4,5},{5,4},{6,7},{7,6},{8,9},{9,8},{10,11... | collective-permute-start | bytes 3145736 | tf_op jit(solution)/shard_map/ppermute | solution.py:513
  113.4 44.0 %collective-permute-start.19 = (f32[256,1024]{1,0:T(8,128)S(1)}, f32[256,1024]{1,0:T(8,128)S(1)}, u32[]{:S(2)}, u32[]{:S(2)}) collective-permute-start(f32[256,1024]{1,0:T(8,128)S(1)} %get-tuple-element.109.refs_0_), channel_id=1, source_target_pairs={{0,2},{2,0},{1,3},{3,1},{4,6},{6,4},{5,7},{7,5},{8,10},{10,8},{9,1... | collective-permute-start | bytes 3145736 | tf_op jit(solution)/shard_map/ppermute | solution.py:513
  115.4 40.1 %collective-permute-start.13 = (f32[256,768]{1,0:T(8,128)S(1)}, f32[256,768]{1,0:T(8,128)S(1)}, u32[]{:S(2)}, u32[]{:S(2)}) collective-permute-start(f32[256,768]{1,0:T(8,128)S(1)} %pad_maximum_fusion.refs_0_), channel_id=1, source_target_pairs={{0,2},{2,0},{1,3},{3,1},{4,6},{6,4},{5,7},{7,5},{8,10},{10,8},{9,1... | collective-permute-start | bytes 2359304 | tf_op jit(solution)/shard_map/ppermute | solution.py:517
  127.8 78.2 %collective-permute-start.12 = (f32[256,768]{1,0:T(8,128)S(1)}, f32[256,768]{1,0:T(8,128)S(1)}, u32[]{:S(2)}, u32[]{:S(2)}) collective-permute-start(f32[256,768]{1,0:T(8,128)S(1)} %pad_maximum_fusion.refs_0_), channel_id=1, source_target_pairs={{0,1},{1,0},{2,3},{3,2},{4,5},{5,4},{6,7},{7,6},{8,9},{9,8},{10,11... | collective-permute-start | bytes 2359304 | tf_op jit(solution)/shard_map/ppermute | solution.py:518
  155.5 39.6 %collective-permute-start.20 = (f32[256,1024]{1,0:T(8,128)S(1)}, f32[256,1024]{1,0:T(8,128)S(1)}, u32[]{:S(2)}, u32[]{:S(2)}) collective-permute-start(f32[256,1024]{1,0:T(8,128)S(1)} %get-tuple-element.108), channel_id=1, source_target_pairs={{0,3},{3,0},{1,2},{2,1},{4,7},{7,4},{5,6},{6,5},{8,11},{11,8},{9,1... | collective-permute-start | bytes 3145736 | tf_op jit(solution)/shard_map/ppermute | solution.py:513
  156.0 49.9 %collective-permute-start.14 = (f32[256,768]{1,0:T(8,128)S(1)}, f32[256,768]{1,0:T(8,128)S(1)}, u32[]{:S(2)}, u32[]{:S(2)}) collective-permute-start(f32[256,768]{1,0:T(8,128)S(1)} %collective-permute-done.13.refs_2_), channel_id=1, source_target_pairs={{0,1},{1,0},{2,3},{3,2},{4,5},{5,4},{6,7},{7,6},{8,9},{9,8},{10,11... | collective-permute-start | bytes 2359304 | tf_op jit(solution)/shard_map/ppermute | solution.py:519
  157.4 56.9 %collective-permute-start.2 = (f32[1408,256]{1,0:T(8,128)S(1)}, f32[1408,256]{1,0:T(8,128)S(1)}, u32[]{:S(2)}, u32[]{:S(2)}) collective-permute-start(f32[1408,256]{1,0:T(8,128)S(1)} %slice.32), channel_id=1, source_target_pairs={{0,4},{4,0},{8,12},{12,8},{1,5},{5,1},{9,13},{13,9},{2,6},{6,2},{1... | collective-permute-start | bytes 4325384 | tf_op jit(solution)/shard_map/ppermute | solution.py:552
  158.9 55.4 %collective-permute-start.3 = (f32[1408,256]{1,0:T(8,128)S(1)}, f32[1408,256]{1,0:T(8,128)S(1)}, u32[]{:S(2)}, u32[]{:S(2)}) collective-permute-start(f32[1408,256]{1,0:T(8,128)S(1)} %slice.33), channel_id=1, source_target_pairs={{0,8},{8,0},{4,12},{12,4},{1,9},{9,1},{5,13},{13,5},{2,10},{10,2},... | collective-permute-start | bytes 4325384 | tf_op jit(solution)/shard_map/ppermute | solution.py:552
  205.9 73.7 %collective-permute-start.21 = (f32[1024,1024]{1,0:T(8,128)}, f32[1024,1024]{1,0:T(8,128)}, u32[]{:S(2)}, u32[]{:S(2)}) collective-permute-start(f32[1024,1024]{1,0:T(8,128)} %shard_map.46.mine_ref.refs_3_), channel_id=1, source_target_pairs={{0,1},{1,0},{2,3},{3,2},{4,5},{5,4},{6,7},{7,6},{8,9},{9,8},{10,11... | collective-permute-start | bytes 12582920 | tf_op jit(solution)/shard_map/ppermute | solution.py:560
  214.3 28.0 %copy-start.6 = (f32[1024,768]{1,0:T(8,128)S(1)}, f32[1024,768]{1,0:T(8,128)}, u32[]{:S(2)}) copy-start(f32[1024,768]{1,0:T(8,128)} %shard_map.44.refs_2_) | copy-start | bytes 9437188
  276.0 245.1 %all-gather.9.cloned.1.call-start = ((), (), s32[]{:S(2)}) async-start(), calls=%async_computation.1 | async-start | bytes 4456448 | tf_op jit(solution)/shard_map/all_gather | solution.py:538
  276.1 136.6 %collective-permute-start.15 = (f32[2560,256]{1,0:T(8,128)}, f32[2560,256]{1,0:T(8,128)}, u32[]{:S(2)}, u32[]{:S(2)}) collective-permute-start(f32[2560,256]{1,0:T(8,128)} %get-tuple-element.60.refs_0_), channel_id=1, source_target_pairs={{0,4},{4,0},{8,12},{12,8},{1,5},{5,1},{9,13},{13,9},{2,6},{6,2},{1... | collective-permute-start | bytes 7864328 | tf_op jit(solution)/shard_map/ppermute | solution.py:539
  276.6 136.0 %collective-permute-start.16 = (f32[2560,256]{1,0:T(8,128)}, f32[2560,256]{1,0:T(8,128)}, u32[]{:S(2)}, u32[]{:S(2)}) collective-permute-start(f32[2560,256]{1,0:T(8,128)} %get-tuple-element.60.refs_0_), channel_id=1, source_target_pairs={{0,8},{8,0},{4,12},{12,4},{1,9},{9,1},{5,13},{13,5},{2,10},{10,2},... | collective-permute-start | bytes 7864328 | tf_op jit(solution)/shard_map/ppermute | solution.py:540
  277.1 135.5 %collective-permute-start.17 = (f32[2560,256]{1,0:T(8,128)}, f32[2560,256]{1,0:T(8,128)}, u32[]{:S(2)}, u32[]{:S(2)}) collective-permute-start(f32[2560,256]{1,0:T(8,128)} %get-tuple-element.60.refs_0_), channel_id=1, source_target_pairs={{0,12},{12,0},{4,8},{8,4},{1,13},{13,1},{5,9},{9,5},{2,14},{14,2},... | collective-permute-start | bytes 7864328 | tf_op jit(solution)/shard_map/ppermute | solution.py:549
  293.5 51.0 %collective-permute-start.22 = (f32[256,1536]{1,0:T(8,128)}, f32[256,1536]{1,0:T(8,128)S(1)}, u32[]{:S(2)}, u32[]{:S(2)}) collective-permute-start(f32[256,1536]{1,0:T(8,128)} %get-tuple-element.69), channel_id=1, source_target_pairs={{0,1},{1,0},{2,3},{3,2},{4,5},{5,4},{6,7},{7,6},{8,9},{9,8},{10,11... | collective-permute-start | bytes 4718600 | tf_op jit(solution)/shard_map/ppermute | solution.py:513
  293.5 102.1 %collective-permute-start.24 = (f32[256,1536]{1,0:T(8,128)}, f32[256,1536]{1,0:T(8,128)}, u32[]{:S(2)}, u32[]{:S(2)}) collective-permute-start(f32[256,1536]{1,0:T(8,128)} %get-tuple-element.69), channel_id=1, source_target_pairs={{0,3},{3,0},{1,2},{2,1},{4,7},{7,4},{5,6},{6,5},{8,11},{11,8},{9,1... | collective-permute-start | bytes 4718600 | tf_op jit(solution)/shard_map/ppermute | solution.py:513
  294.3 50.2 %copy-start.3 = (f32[256,1536]{1,0:T(8,128)S(1)}, f32[256,1536]{1,0:T(8,128)}, u32[]{:S(2)}) copy-start(f32[256,1536]{1,0:T(8,128)} %get-tuple-element.68.refs_0_) | copy-start | bytes 4718596
  344.5 51.1 %collective-permute-start.23 = (f32[256,1536]{1,0:T(8,128)S(1)}, f32[256,1536]{1,0:T(8,128)S(1)}, u32[]{:S(2)}, u32[]{:S(2)}) collective-permute-start(f32[256,1536]{1,0:T(8,128)S(1)} %copy-done.3), channel_id=1, source_target_pairs={{0,2},{2,0},{1,3},{3,1},{4,6},{6,4},{5,7},{7,5},{8,10},{10,8},{9,1... | collective-permute-start | bytes 4718600 | tf_op jit(solution)/shard_map/ppermute | solution.py:513
  412.6 50.9 %collective-permute-start.28 = (f32[1024,1024]{1,0:T(8,128)}, f32[1024,1024]{1,0:T(8,128)}, u32[]{:S(2)}, u32[]{:S(2)}) collective-permute-start(f32[1024,1024]{1,0:T(8,128)} %get-tuple-element.75.mine_ref.refs_3_), channel_id=1, source_target_pairs={{0,1},{1,0},{2,3},{3,2},{4,5},{5,4},{6,7},{7,6},{8,9},{9,8},{10,11... | collective-permute-start | bytes 12582920 | tf_op jit(solution)/shard_map/ppermute | solution.py:560
  459.9 229.4 %all-gather.11.cloned.1.call-start = ((), (), s32[]{:S(2)}) async-start(), calls=%async_computation.2 | async-start | bytes 4456448 | tf_op jit(solution)/shard_map/all_gather | solution.py:538
  460.0 111.0 %collective-permute-start.25 = (f32[2304,256]{1,0:T(8,128)}, f32[2304,256]{1,0:T(8,128)}, u32[]{:S(2)}, u32[]{:S(2)}) collective-permute-start(f32[2304,256]{1,0:T(8,128)} %get-tuple-element.72.refs_0_), channel_id=1, source_target_pairs={{0,4},{4,0},{8,12},{12,8},{1,5},{5,1},{9,13},{13,9},{2,6},{6,2},{1... | collective-permute-start | bytes 7077896 | tf_op jit(solution)/shard_map/ppermute | solution.py:539
  460.7 117.4 %collective-permute-start.26 = (f32[2304,256]{1,0:T(8,128)}, f32[2304,256]{1,0:T(8,128)}, u32[]{:S(2)}, u32[]{:S(2)}) collective-permute-start(f32[2304,256]{1,0:T(8,128)} %get-tuple-element.72.refs_0_), channel_id=1, source_target_pairs={{0,8},{8,0},{4,12},{12,4},{1,9},{9,1},{5,13},{13,5},{2,10},{10,2},... | collective-permute-start | bytes 7077896 | tf_op jit(solution)/shard_map/ppermute | solution.py:540
  461.2 116.9 %collective-permute-start.27 = (f32[2304,256]{1,0:T(8,128)}, f32[2304,256]{1,0:T(8,128)}, u32[]{:S(2)}, u32[]{:S(2)}) collective-permute-start(f32[2304,256]{1,0:T(8,128)} %get-tuple-element.72.refs_0_), channel_id=1, source_target_pairs={{0,12},{12,0},{4,8},{8,4},{1,13},{13,1},{5,9},{9,5},{2,14},{14,2},... | collective-permute-start | bytes 7077896 | tf_op jit(solution)/shard_map/ppermute | solution.py:549
  477.1 124.3 %collective-permute-start.29 = (f32[256,1280]{1,0:T(8,128)}, f32[256,1280]{1,0:T(8,128)}, u32[]{:S(2)}, u32[]{:S(2)}) collective-permute-start(f32[256,1280]{1,0:T(8,128)} %get-tuple-element.83), channel_id=1, source_target_pairs={{0,1},{1,0},{2,3},{3,2},{4,5},{5,4},{6,7},{7,6},{8,9},{9,8},{10,11... | collective-permute-start | bytes 3932168 | tf_op jit(solution)/shard_map/ppermute | solution.py:513
  477.1 124.6 %collective-permute-start.31 = (f32[256,1280]{1,0:T(8,128)}, f32[256,1280]{1,0:T(8,128)}, u32[]{:S(2)}, u32[]{:S(2)}) collective-permute-start(f32[256,1280]{1,0:T(8,128)} %get-tuple-element.83), channel_id=1, source_target_pairs={{0,3},{3,0},{1,2},{2,1},{4,7},{7,4},{5,6},{6,5},{8,11},{11,8},{9,1... | collective-permute-start | bytes 3932168 | tf_op jit(solution)/shard_map/ppermute | solution.py:513
  521.1 49.8 %copy-start.4 = (f32[256,1280]{1,0:T(8,128)S(1)}, f32[256,1280]{1,0:T(8,128)}, u32[]{:S(2)}) copy-start(f32[256,1280]{1,0:T(8,128)} %get-tuple-element.82.refs_0_) | copy-start | bytes 3932164
  571.0 30.7 %collective-permute-start.30 = (f32[256,1280]{1,0:T(8,128)S(1)}, f32[256,1280]{1,0:T(8,128)S(1)}, u32[]{:S(2)}, u32[]{:S(2)}) collective-permute-start(f32[256,1280]{1,0:T(8,128)S(1)} %copy-done.4), channel_id=1, source_target_pairs={{0,2},{2,0},{1,3},{3,1},{4,6},{6,4},{5,7},{7,5},{8,10},{10,8},{9,1... | collective-permute-start | bytes 3932168 | tf_op jit(solution)/shard_map/ppermute | solution.py:513
  629.2 7.4 collective-permute-start.32
  651.0 87.9 %collective-permute-start.36 = (f32[256,1024]{1,0:T(8,128)}, f32[256,1024]{1,0:T(8,128)S(1)}, u32[]{:S(2)}, u32[]{:S(2)}) collective-permute-start(f32[256,1024]{1,0:T(8,128)} %get-tuple-element.96), channel_id=1, source_target_pairs={{0,1},{1,0},{2,3},{3,2},{4,5},{5,4},{6,7},{7,6},{8,9},{9,8},{10,11... | collective-permute-start | bytes 3145736 | tf_op jit(solution)/shard_map/ppermute | solution.py:513
  651.2 87.8 %collective-permute-start.38 = (f32[256,1024]{1,0:T(8,128)}, f32[256,1024]{1,0:T(8,128)S(1)}, u32[]{:S(2)}, u32[]{:S(2)}) collective-permute-start(f32[256,1024]{1,0:T(8,128)} %get-tuple-element.96), channel_id=1, source_target_pairs={{0,3},{3,0},{1,2},{2,1},{4,7},{7,4},{5,6},{6,5},{8,11},{11,8},{9,1... | collective-permute-start | bytes 3145736 | tf_op jit(solution)/shard_map/ppermute | solution.py:513
  652.4 86.6 %collective-permute-start.37 = (f32[256,1024]{1,0:T(8,128)}, f32[256,1024]{1,0:T(8,128)S(1)}, u32[]{:S(2)}, u32[]{:S(2)}) collective-permute-start(f32[256,1024]{1,0:T(8,128)} %get-tuple-element.95.refs_0_), channel_id=1, source_target_pairs={{0,2},{2,0},{1,3},{3,1},{4,6},{6,4},{5,7},{7,5},{8,10},{10,8},{9,1... | collective-permute-start | bytes 3145736 | tf_op jit(solution)/shard_map/ppermute | solution.py:513
  689.4 49.7 %copy-start.5 = (f32[256,1024]{1,0:T(8,128)S(1)}, f32[256,1024]{1,0:T(8,128)}, u32[]{:S(2)}) copy-start(f32[256,1024]{1,0:T(8,128)} %get-tuple-element.95.refs_0_) | copy-start | bytes 3145732
  739.0 10.8 %copy-start.10 = (f32[2048,256]{1,0:T(8,128)S(1)}, f32[2048,256]{1,0:T(8,128)}, u32[]{:S(2)}) copy-start(f32[2048,256]{1,0:T(8,128)} %get-tuple-element.92.refs_0_) | copy-start | bytes 6291460
  749.8 114.5 %collective-permute-start.39 = (f32[1024,1024]{1,0:T(8,128)}, f32[1024,1024]{1,0:T(8,128)S(1)}, u32[]{:S(2)}, u32[]{:S(2)}) collective-permute-start(f32[1024,1024]{1,0:T(8,128)} %shard_map.63.mine_ref), channel_id=1, source_target_pairs={{0,1},{1,0},{2,3},{3,2},{4,5},{5,4},{6,7},{7,6},{8,9},{9,8},{10,11... | collective-permute-start | bytes 12582920 | tf_op jit(solution)/shard_map/ppermute | solution.py:560
  749.8 48.5 %collective-permute-start.33 = (f32[2048,256]{1,0:T(8,128)S(1)}, f32[2048,256]{1,0:T(8,128)S(1)}, u32[]{:S(2)}, u32[]{:S(2)}) collective-permute-start(f32[2048,256]{1,0:T(8,128)S(1)} %copy-done.10), channel_id=1, source_target_pairs={{0,4},{4,0},{8,12},{12,8},{1,5},{5,1},{9,13},{13,9},{2,6},{6,2},{1... | collective-permute-start | bytes 6291464 | tf_op jit(solution)/shard_map/ppermute | solution.py:539
  751.0 92.6 %collective-permute-start.34 = (f32[2048,256]{1,0:T(8,128)S(1)}, f32[2048,256]{1,0:T(8,128)S(1)}, u32[]{:S(2)}, u32[]{:S(2)}) collective-permute-start(f32[2048,256]{1,0:T(8,128)S(1)} %copy-done.10), channel_id=1, source_target_pairs={{0,8},{8,0},{4,12},{12,4},{1,9},{9,1},{5,13},{13,5},{2,10},{10,2},... | collective-permute-start | bytes 6291464 | tf_op jit(solution)/shard_map/ppermute | solution.py:540
  752.3 91.4 %collective-permute-start.35 = (f32[2048,256]{1,0:T(8,128)S(1)}, f32[2048,256]{1,0:T(8,128)S(1)}, u32[]{:S(2)}, u32[]{:S(2)}) collective-permute-start(f32[2048,256]{1,0:T(8,128)S(1)} %copy-done.10), channel_id=1, source_target_pairs={{0,12},{12,0},{4,8},{8,4},{1,13},{13,1},{5,9},{9,5},{2,14},{14,2},... | collective-permute-start | bytes 6291464 | tf_op jit(solution)/shard_map/ppermute | solution.py:549
  (7 other events, 16.6 us)
Sparse Core Ops, SparseCore 0:
  276.2 47.1 all-gather.6
  460.1 47.3 all-gather.8
  629.3 41.8 all-gather.10

commit v6 on v5

--- a/solution.py
+++ b/solution.py
@@ -280,7 +280,7 @@
 
 
 def rows_kernel(*refs):
-    (own, y, z, *far), (x_ref, out_ref, own_ref, wide) = refs[:-4], refs[-4:]
+    (own, y, z, *far), (x_ref, *_, out_ref, own_ref, wide) = refs[:ROW_PIECES[len(refs)]], refs[ROW_PIECES[len(refs)]:]
     my_col = lax.axis_index("pc")
     i = pl.program_id(0)
 
@@ -293,8 +293,8 @@
     if len(far) == 1:
         place(3, far[0])
     else:
-        pl.when(i < 2)(lambda: place(3, far[0]))
-        pl.when(i >= 2)(lambda: place(3, far[1]))
+        pl.when(i == 0)(lambda: place(3, far[0]))
+        pl.when(i > 0)(lambda: place(3, far[1]))
     for k in range(4):
         lanes = slice(NB * k, NB * k + NB)
         part = dot_nt(wide[:, lanes], x_ref[NB * k:, lanes])
@@ -302,20 +302,24 @@
     own_ref[...] = out_ref[:, pl.ds(pl.multiple_of(my_col * NB, NB), NB)]
 
 
-def solve_rows(pieces, x):
+ROW_PIECES = {8: 4, 9: 5, 11: 5}
+
+
+def solve_rows(pieces, x, part=0, before=()):
     own, y, z, *far = pieces
     rows = own.shape[0]
     tile = rows // 4
-    block = pl.BlockSpec((tile, NB), lambda i: (i, 0))
-    far_blocks = [block] if len(far) == 1 else [
-        pl.BlockSpec((tile, NB), lambda i: (jnp.minimum(i, 1), 0)), pl.BlockSpec((tile, NB), lambda i: (jnp.maximum(i - 2, 0), 0))]
-    return call(
-        rows_kernel, 30 * rows * SUP * SUP // 4, 12 * rows * SUP, 34, grid=(4,),
+    whole = len(far) == 1
+    at = (lambda i: (i, 0)) if whole else (lambda i: (2 * i + part, 0))
+    block, wide_block = pl.BlockSpec((tile, NB), at), pl.BlockSpec((tile, SUP), at)
+    count = 4 if whole else 2
+    return call(
+        rows_kernel, 30 * count * tile * SUP * SUP // 4, 12 * count * tile * SUP, 34, grid=(count,),
         out_shape=(shape(rows, SUP), shape(rows, NB)),
-        in_specs=[block] * 3 + far_blocks + [fixed(SUP, SUP)],
-        out_specs=(pl.BlockSpec((tile, SUP), lambda i: (i, 0)), block),
-        scratch_shapes=[pltpu.VMEM((tile, SUP), F32)],
-    )(in_hbm(own), y, z, *far, x)
+        in_specs=[block] * 3 + ([block] if whole else [fixed(tile, NB)] * 2) + [fixed(SUP, SUP)] + [pl.BlockSpec(memory_space=pl.ANY)] * len(before),
+        out_specs=(wide_block, block), scratch_shapes=[pltpu.VMEM((tile, SUP), F32)],
+        input_output_aliases={6: 0, 7: 1} if before else {},
+    )(in_hbm(own), y, z, *far, x, *(in_hbm(a) for a in before))
 
 
 def cols_kernel(*refs):
@@ -548,8 +552,9 @@
             if step:
                 far = [lax.ppermute(col_panel, "pc", FLIP3)]
             else:
-                split = col_panel.shape[0] // 2
-                far = [lax.ppermute(z[:split], "pc", FLIP1), lax.ppermute(y[split:], "pc", FLIP2)]
+                tile = col_panel.shape[0] // 4
+                far = [lax.ppermute(z[:tile], "pc", FLIP1), lax.ppermute(y[2 * tile:3 * tile], "pc", FLIP2)]
+                later_far = [lax.ppermute(z[tile:2 * tile], "pc", FLIP1), lax.ppermute(y[3 * tile:], "pc", FLIP2)]
             if step == 0:
                 x_sup, own_l, own_diag = factor(blocks)
             else:
@@ -559,6 +564,8 @@
                 more = solve_cols(row_pieces, x_sup)
             theirs = lax.ppermute(mine, "pr", FLIP1)
             l_rows, own_col = solve_rows([col_panel, y, z, *far], x_sup)
+            if step == 0:
+                l_rows, own_col = solve_rows([col_panel, y, z, *later_far], x_sup, 1, (l_rows, own_col))
             out_cols.append(own_col)
             out_diags.append(own_l)
             if step < 3:

time: 946 us -> 936 us (0.989)
  waiting for transfers between devices: 206 us -> 195 us
    ppermute x3, waiting for transfers between devices: 64.2 us -> 0.01 us  [gather_diag(): at_y, at_z, at_x = (y(block), z(block), x(block))]
    ppermute x3, waiting for transfers between devices: 6.57 us -> 63 us  [gather_diag(): at_yz, at_xy, at_xz = (z(at_y), x(at_y), x(at_z))]
    ppermute x1, waiting for transfers between devices: 27.6 us -> 0.01 us  [gather_all(): x = lax.ppermute(panel, 'pr', FLIP2)]
    ppermute x4, waiting for transfers between devices: 45 us -> 59.4 us  [local_part(): y = lax.ppermute(col_panel, 'pc', FLIP1)]
    ppermute x2 -> x4, waiting for transfers between devices: 0.01 us -> 10.6 us  [the longest x1 10.6 us: local_part(): lax.ppermute(z[:tile], 'pc', FLIP1)]
    pallas_call x4 -> x5, Pallas kernels: 97.8 us -> 101 us  [solve_rows(): call(rows_kernel, 30 * count * tile * SUP * SUP // 4, 12 * count * tile *...]
  transfers between devices with their start and end apart: 43 -> 45, of which waited for: 10 -> 10; matrix products, arithmetic and copies ran while one was open for 2% -> 2% of each run, Pallas kernels for 58% -> 59%
where the time goes in v6:
time: 936 us; the launch traced here: 933 us
  Pallas kernels  657 us (70%)
  waiting for transfers between devices  195 us (21%)
  starting transfers between devices  35.5 us (4%)
  local copies, waits for them, and re-layouts  30.8 us (3%)
  between operations  14.4 us (2%)
    pallas_call x4, Pallas kernels, update_trail(): call(trail_kernel, 12 * count * NB * cols * SUP, 8 * count * NB * cols, 3...  199 us
    pallas_call x3, Pallas kernels, factor_beside(): call(fused_kernel, 100000000000, 1 << 25, 48, grid=(4,), out_shape=(near(...  149 us
    pallas_call x5, Pallas kernels, solve_rows(): call(rows_kernel, 30 * count * tile * SUP * SUP // 4, 12 * count * tile *...  101 us
    pallas_call x3, Pallas kernels, update_panel(): call(panel_kernel, 12 * rows * width * SUP, 8 * rows * width + 4 * rows *...  68 us
    ppermute x3, waiting for transfers between devices, gather_diag(): at_yz, at_xy, at_xz = (z(at_y), x(at_y), x(at_z))  63 us
    pallas_call x5, Pallas kernels, solve_cols(): call(cols_kernel, 30 * cols * SUP * SUP // 4, 12 * cols * SUP, 20, grid=(...  61.3 us
    ppermute x4, waiting for transfers between devices, local_part(): y = lax.ppermute(col_panel, 'pc', FLIP1)  59.4 us
    ppermute x4, waiting for transfers between devices, local_part(): z = lax.ppermute(col_panel, 'pc', FLIP2)  51.2 us
  transfers between devices with their start and end apart: 45, of which 10 were waited for; matrix products, arithmetic and copies ran while one was open for 2% of the time, Pallas kernels for 59%

profile of v6, /device:TPU:0, one launch (start us, length us, event | category | flops | bytes accessed | tf_op | source)
XLA Modules:
  0.0 932.9 jit_solution(2353250950424486997)
XLA Ops:
  9.9 3.2 collective-permute-start.4
  13.1 1.6 collective-permute-start.5
  16.2 6.5 slice.30
  22.7 1.8 copy.22
  25.6 1.6 collective-permute-start.6
  28.5 1.5 collective-permute-start.9
  30.7 63.0 %collective-permute-done.6 = f32[256,256]{1,0:T(8,128)S(1)} collective-permute-done((f32[256,256]{1,0:T(8,128)S(1)}, f32[256,256]{1,0:T(8,128)S(1)}, u32[]{:S(2)}, u32[]{:S(2)}) %collective-permute-start.6) | collective-permute-done | bytes 262176 | tf_op jit(solution)/shard_map/ppermute | solution.py:510
  97.1 2.9 collective-permute-done.10
  101.3 1.8 constant_dynamic-slice_fusion
  103.8 4.6 copy-done
  108.3 6.2 shard_map.41.refs_0_
  114.6 1.5 collective-permute-start.15
  116.7 34.7 %shard_map.42 = (f32[1024,1024]{1,0:T(8,128)S(1)}, f32[256,256]{1,0:T(8,128)}, f32[256,256]{1,0:T(8,128)}) custom-call(f32[8,256,256]{2,1,0:T(8,128)} %bitcast_dynamic-update-slice_fusion.refs_0_, f32[8,256,256]{2,1,0:T(8,128)} %collective-permute-done.11.refs_1_), custom_call_target="tpu_custom_call" | custom-call | flops 30000001024 | bytes 16777216 | tf_op jit(solution)/shard_map/pallas_call | solution.py:172
  151.6 14.4 %collective-permute-done.refs_1_ = f32[2816,256]{1,0:T(8,128)} collective-permute-done((f32[2816,256]{1,0:T(8,128)}, f32[2816,256]{1,0:T(8,128)}, u32[]{:S(2)}, u32[]{:S(2)}) %collective-permute-start) | collective-permute-done | bytes 2883616 | tf_op jit(solution)/shard_map/ppermute | solution.py:543
  168.1 1.5 collective-permute-start.12
  170.1 10.8 %shard_map.47.mine_ref.refs_3_ = f32[1024,1024]{1,0:T(8,128)} custom-call(f32[256,1024]{1,0:T(8,128)S(1)} %get-tuple-element.113.refs_0_, f32[256,1024]{1,0:T(8,128)S(1)} %collective-permute-done.20.refs_1_, f32[256,1024]{1,0:T(8,128)S(1)} %collective-permute-done.21.refs_2_, f32[256,1024]{1,0:T(8,128)S(1)} %collective-permute-done.22.refs_3_, ...), custom_call_target="tpu_custom_call" | custom-call | flops 8053063680 | bytes 12582912 | tf_op jit(solution)/shard_map/pallas_call | solution.py:351
  180.9 1.6 collective-permute-start.3
  182.5 8.3 shard_map.45.refs_2_
  190.8 10.6 %collective-permute-done.12.refs_3_ = f32[704,256]{1,0:T(8,128)S(1)} collective-permute-done((f32[704,256]{1,0:T(8,128)S(1)}, f32[704,256]{1,0:T(8,128)S(1)}, u32[]{:S(2)}, u32[]{:S(2)}) %collective-permute-start.12) | collective-permute-done | bytes 720928 | tf_op jit(solution)/shard_map/ppermute | solution.py:556
  201.5 15.8 %shard_map.43 = (f32[2816,1024]{1,0:T(8,128)}, f32[2816,256]{1,0:T(8,128)}) custom-call(f32[2816,256]{1,0:T(8,128)} %bitcast.40.refs_0_, f32[2816,256]{1,0:T(8,128)} %collective-permute-done.refs_1_, f32[2816,256]{1,0:T(8,128)S(1)} %collective-permute-done.1.refs_2_, f32[704,256]{1,0:T(8,128)S(1)} %collective-permute-done.12.refs_3_, ...), custom_call_target="tpu_custom_call" | custom-call | flops 11072962560 | bytes 17301504 | tf_op jit(solution)/shard_map/pallas_call | solution.py:316
  217.3 15.6 %shard_map.44 = (f32[2816,1024]{1,0:T(8,128)}, f32[2816,256]{1,0:T(8,128)}) custom-call(f32[2816,256]{1,0:T(8,128)} %bitcast.40.refs_0_, f32[2816,256]{1,0:T(8,128)} %collective-permute-done.refs_1_, f32[2816,256]{1,0:T(8,128)S(1)} %collective-permute-done.1.refs_2_, ...), custom_call_target="tpu_custom_call", output_to_operand_aliasing={{0}: (6, {}), {1}: (7, {})} | custom-call | flops 11072962560 | bytes 17301504 | tf_op jit(solution)/shard_map/pallas_call | solution.py:316
  233.0 33.3 %shard_map.46 = (f32[256,256]{1,0:T(8,128)}, f32[2560,256]{1,0:T(8,128)}, f32[256,512]{1,0:T(8,128)}, f32[2560,512]{1,0:T(8,128)}) custom-call(f32[2816,768]{1,0:T(8,128)} %shard_map.41.refs_0_, f32[2816,1024]{1,0:T(8,128)} %get-tuple-element.61.refs_1_.l_ref.refs_2_, f32[1024,768]{1,0:T(8,128)S(1)} %copy-done.6), custom_call_target="tpu_custom_call" | custom-call | flops 26575110144 | bytes 28835840 | tf_op jit(solution)/shard_map/pallas_call | solution.py:399
  267.3 2.5 collective-permute-start.19
  270.9 12.7 %shard_map.51 = (f32[256,1536]{1,0:T(8,128)}, f32[256,1536]{1,0:T(8,128)}) custom-call(s32[1]{0:T(128)} %bitcast.core_ref.refs_0_, f32[3072,2048]{1,0:T(8,128)} %refs_1_.1, f32[2816,1024]{1,0:T(8,128)} %get-tuple-element.61.refs_1_.l_ref.refs_2_, f32[1024,1024]{1,0:T(8,128)} %shard_map.47.mine_ref.refs_3_, ...), custom_call_target="tpu_custom_call" | custom-call | flops 6442450944 | bytes 12582912 | tf_op jit(solution)/shard_map/pallas_call | solution.py:428
  284.4 50.2 %shard_map.48.rest_0_ = f32[3072,2048]{1,0:T(8,128)} custom-call(s32[1]{0:T(128)} %bitcast.core_ref.refs_0_, f32[3072,2048]{1,0:T(8,128)} %refs_1_.1, f32[2816,1024]{1,0:T(8,128)} %get-tuple-element.61.refs_1_.l_ref.refs_2_, f32[1024,1024]{1,0:T(8,128)} %shard_map.47.mine_ref.refs_3_, f32[1024,1024]{1,0:T(8,128)} %collective-permute-done.23.theirs_ref.refs_4_, ...), custom_call_target="tpu_custom_call" | custom-call | flops 45097156608 | bytes 29360128 | tf_op jit(solution)/shard_map/pallas_call | solution.py:492
  336.1 49.7 %shard_map.49 = (f32[1024,1024]{1,0:T(8,128)S(1)}, f32[256,256]{1,0:T(8,128)}, f32[256,256]{1,0:T(8,128)}, f32[3072,2048]{1,0:T(8,128)}) custom-call(f32[16,256,256]{2,1,0:T(8,128)} %bitcast.47, f32[3072,2048]{1,0:T(8,128)} %refs_1_.1, f32[2816,1024]{1,0:T(8,128)} %get-tuple-element.61.refs_1_.l_ref.refs_2_, ...), custom_call_target="tpu_custom_call", output_to_operand_aliasing={{3}: (5, {})} | custom-call | flops 99999997952 | bytes 33554432 | tf_op jit(solution)/shard_map/pallas_call | solution.py:253
  385.8 17.0 %shard_map.52 = (f32[1024,1024]{1,0:T(8,128)}, f32[1024,512]{1,0:T(8,128)S(1)}) custom-call(f32[256,1536]{1,0:T(8,128)S(1)} %copy-done.3, f32[256,1536]{1,0:T(8,128)S(1)} %collective-permute-done.24.refs_1_, f32[256,1536]{1,0:T(8,128)S(1)} %collective-permute-done.25.refs_2_, f32[256,1536]{1,0:T(8,128)} %collective-permute-done.26.refs_3_, ...), custom_call_target="tpu_custom_call" | custom-call | flops 12079595520 | bytes 18874368 | tf_op jit(solution)/shard_map/pallas_call | solution.py:351
  402.8 25.8 %shard_map.50 = (f32[2560,1024]{1,0:T(8,128)}, f32[2560,256]{1,0:T(8,128)}) custom-call(f32[2560,256]{1,0:T(8,128)} %get-tuple-element.64.refs_0_, f32[2560,256]{1,0:T(8,128)} %collective-permute-done.17.refs_1_, f32[2560,256]{1,0:T(8,128)} %collective-permute-done.18.refs_2_, f32[2560,256]{1,0:T(8,128)} %collective-permute-done.19.refs_3_, ...), custom_call_target="tpu_custom_call" | custom-call | flops 20132659200 | bytes 31457280 | tf_op jit(solution)/shard_map/pallas_call | solution.py:316
  428.6 21.5 %shard_map.53 = (f32[256,256]{1,0:T(8,128)}, f32[2304,256]{1,0:T(8,128)}, f32[256,256]{1,0:T(8,128)}, f32[2304,256]{1,0:T(8,128)}) custom-call(f32[2560,512]{1,0:T(8,128)} %get-tuple-element.63.refs_0_, f32[2560,1024]{1,0:T(8,128)} %get-tuple-element.70.refs_1_.l_ref.refs_2_, f32[1024,512]{1,0:T(8,128)S(1)} %get-tuple-element.74.refs_2_), custom_call_target="tpu_custom_call" | custom-call | flops 16106127360 | bytes 20971520 | tf_op jit(solution)/shard_map/pallas_call | solution.py:399
  451.4 2.3 collective-permute-start.29
  454.6 12.6 %shard_map.57 = (f32[256,1280]{1,0:T(8,128)}, f32[256,1280]{1,0:T(8,128)}) custom-call(s32[1]{0:T(128)} %bitcast.core_ref.refs_0_, f32[3072,2048]{1,0:T(8,128)} %get-tuple-element.78.trail_ref.refs_1_, f32[2560,1024]{1,0:T(8,128)} %get-tuple-element.70.refs_1_.l_ref.refs_2_, f32[1024,1024]{1,0:T(8,128)} %get-tuple-element.79.mine_ref.refs_3_, ...), custom_call_target="tpu_custom_call" | custom-call | flops 6442450944 | bytes 12582912 | tf_op jit(solution)/shard_map/pallas_call | solution.py:428
  468.2 43.1 %shard_map.54.trail_ref = f32[3072,2048]{1,0:T(8,128)} custom-call(s32[1]{0:T(128)} %bitcast.core_ref.refs_0_, f32[3072,2048]{1,0:T(8,128)} %get-tuple-element.78.trail_ref.refs_1_, f32[2560,1024]{1,0:T(8,128)} %get-tuple-element.70.refs_1_.l_ref.refs_2_, f32[1024,1024]{1,0:T(8,128)} %get-tuple-element.79.mine_ref.refs_3_, ...), custom_call_target="tpu_custom_call", output_to_operand_aliasing={{}: (1, {})} | custom-call | flops 38654705664 | bytes 25165824 | tf_op jit(solution)/shard_map/pallas_call | solution.py:492
  511.3 49.8 %shard_map.55 = (f32[1024,1024]{1,0:T(8,128)S(1)}, f32[256,256]{1,0:T(8,128)}, f32[256,256]{1,0:T(8,128)}, f32[3072,2048]{1,0:T(8,128)}) custom-call(f32[16,256,256]{2,1,0:T(8,128)} %bitcast.48, f32[3072,2048]{1,0:T(8,128)} %shard_map.54.trail_ref, f32[2560,1024]{1,0:T(8,128)} %get-tuple-element.70.refs_1_.l_ref.refs_2_, ...), custom_call_target="tpu_custom_call", output_to_operand_aliasing={{3}: (1, {})} | custom-call | flops 99999997952 | bytes 33554432 | tf_op jit(solution)/shard_map/pallas_call | solution.py:253
  562.4 5.8 collective-permute-done.28.refs_2_
  568.2 23.4 %shard_map.56 = (f32[2304,1024]{1,0:T(8,128)}, f32[2304,256]{1,0:T(8,128)}) custom-call(f32[2304,256]{1,0:T(8,128)} %get-tuple-element.76.refs_0_, f32[2304,256]{1,0:T(8,128)} %collective-permute-done.27.refs_1_, f32[2304,256]{1,0:T(8,128)} %collective-permute-done.28.refs_2_, f32[2304,256]{1,0:T(8,128)} %collective-permute-done.29.refs_3_, ...), custom_call_target="tpu_custom_call" | custom-call | flops 18119393280 | bytes 28311552 | tf_op jit(solution)/shard_map/pallas_call | solution.py:316
  591.8 14.4 %shard_map.58 = (f32[1024,1024]{1,0:T(8,128)}, f32[1024,256]{1,0:T(8,128)S(1)}) custom-call(f32[256,1280]{1,0:T(8,128)S(1)} %copy-done.4, f32[256,1280]{1,0:T(8,128)} %collective-permute-done.31.refs_1_, f32[256,1280]{1,0:T(8,128)S(1)} %collective-permute-done.32.refs_2_, f32[256,1280]{1,0:T(8,128)} %collective-permute-done.33.refs_3_, ...), custom_call_target="tpu_custom_call" | custom-call | flops 10066329600 | bytes 15728640 | tf_op jit(solution)/shard_map/pallas_call | solution.py:351
  606.2 13.1 %shard_map.59 = (f32[256,256]{1,0:T(8,128)}, f32[2048,256]{1,0:T(8,128)}) custom-call(f32[2304,256]{1,0:T(8,128)} %get-tuple-element.75.refs_0_, f32[2304,1024]{1,0:T(8,128)} %get-tuple-element.84.refs_1_.l_ref.refs_2_, f32[1024,256]{1,0:T(8,128)S(1)} %get-tuple-element.88.refs_2_), custom_call_target="tpu_custom_call" | custom-call | flops 7247757312 | bytes 14155776 | tf_op jit(solution)/shard_map/pallas_call | solution.py:399
  619.4 7.4 collective-permute-done.34.theirs_ref.refs_4_
  626.8 2.1 copy-done.7
  628.9 12.4 %shard_map.63 = (f32[256,1024]{1,0:T(8,128)}, f32[256,1024]{1,0:T(8,128)}) custom-call(s32[1]{0:T(128)} %bitcast.core_ref.refs_0_, f32[3072,2048]{1,0:T(8,128)} %get-tuple-element.90.trail_ref.refs_1_, f32[2304,1024]{1,0:T(8,128)} %get-tuple-element.84.refs_1_.l_ref.refs_2_, f32[1024,1024]{1,0:T(8,128)} %get-tuple-element.91.mine_ref.refs_3_, ...), custom_call_target="tpu_custom_call" | custom-call | flops 6442450944 | bytes 12582912 | tf_op jit(solution)/shard_map/pallas_call | solution.py:428
  643.4 36.1 %shard_map.60.trail_ref = f32[3072,2048]{1,0:T(8,128)} custom-call(s32[1]{0:T(128)} %bitcast.core_ref.refs_0_, f32[3072,2048]{1,0:T(8,128)} %get-tuple-element.90.trail_ref.refs_1_, f32[2304,1024]{1,0:T(8,128)} %get-tuple-element.84.refs_1_.l_ref.refs_2_, f32[1024,1024]{1,0:T(8,128)} %get-tuple-element.91.mine_ref.refs_3_, ...), custom_call_target="tpu_custom_call", output_to_operand_aliasing={{}: (1, {})} | custom-call | flops 32212254720 | bytes 20971520 | tf_op jit(solution)/shard_map/pallas_call | solution.py:492
  679.6 49.6 %shard_map.61 = (f32[1024,1024]{1,0:T(8,128)S(1)}, f32[256,256]{1,0:T(8,128)}, f32[256,256]{1,0:T(8,128)}, f32[3072,2048]{1,0:T(8,128)}) custom-call(f32[16,256,256]{2,1,0:T(8,128)} %bitcast.49, f32[3072,2048]{1,0:T(8,128)} %shard_map.60.trail_ref, f32[2304,1024]{1,0:T(8,128)} %get-tuple-element.84.refs_1_.l_ref.refs_2_, ...), custom_call_target="tpu_custom_call", output_to_operand_aliasing={{3}: (1, {})} | custom-call | flops 99999997952 | bytes 33554432 | tf_op jit(solution)/shard_map/pallas_call | solution.py:253
  729.2 10.8 %shard_map.64.mine_ref = f32[1024,1024]{1,0:T(8,128)} custom-call(f32[256,1024]{1,0:T(8,128)S(1)} %copy-done.5, f32[256,1024]{1,0:T(8,128)S(1)} %collective-permute-done.38.refs_1_, f32[256,1024]{1,0:T(8,128)S(1)} %collective-permute-done.39.refs_2_, f32[256,1024]{1,0:T(8,128)S(1)} %collective-permute-done.40.refs_3_, f32[1024,1024]{1,0:T(8,128)S(1)} %get-tuple-element.97.refs_4_), custom_call_target="tpu_custom_call" | custom-call | flops 8053063680 | bytes 12582912 | tf_op jit(solution)/shard_map/pallas_call | solution.py:351
  743.5 45.0 %collective-permute-done.35.refs_1_ = f32[2048,256]{1,0:T(8,128)S(1)} collective-permute-done((f32[2048,256]{1,0:T(8,128)S(1)}, f32[2048,256]{1,0:T(8,128)S(1)}, u32[]{:S(2)}, u32[]{:S(2)}) %collective-permute-start.35) | collective-permute-done | bytes 2097184 | tf_op jit(solution)/shard_map/ppermute | solution.py:543
  788.5 45.4 %collective-permute-done.36.refs_2_ = f32[2048,256]{1,0:T(8,128)S(1)} collective-permute-done((f32[2048,256]{1,0:T(8,128)S(1)}, f32[2048,256]{1,0:T(8,128)S(1)}, u32[]{:S(2)}, u32[]{:S(2)}) %collective-permute-start.36) | collective-permute-done | bytes 2097184 | tf_op jit(solution)/shard_map/ppermute | solution.py:544
  833.9 20.6 %shard_map.62 = (f32[2048,1024]{1,0:T(8,128)}, f32[2048,256]{1,0:T(8,128)}) custom-call(f32[2048,256]{1,0:T(8,128)} %get-tuple-element.96.refs_0_, f32[2048,256]{1,0:T(8,128)S(1)} %collective-permute-done.35.refs_1_, f32[2048,256]{1,0:T(8,128)S(1)} %collective-permute-done.36.refs_2_, f32[2048,256]{1,0:T(8,128)S(1)} %collective-permute-done.37.refs_3_, ...), custom_call_target="tpu_custom_call" | custom-call | flops 16106127360 | bytes 25165824 | tf_op jit(solution)/shard_map/pallas_call | solution.py:316
  854.5 2.1 copy-done.9
  856.5 69.6 %shard_map.65 = (f32[3072,2048]{1,0:T(8,128)}, f32[24576,128]{1,0:T(8,128)}) custom-call(s32[1]{0:T(128)} %bitcast.core_ref.refs_0_, f32[3072,2048]{1,0:T(8,128)} %get-tuple-element.95.trail_ref, f32[2048,1024]{1,0:T(8,128)} %get-tuple-element.98.l_ref, f32[1024,1024]{1,0:T(8,128)} %shard_map.64.mine_ref, ...), custom_call_target="tpu_custom_call", output_to_operand_aliasing={{0}: (1, {})} | custom-call | flops 57982058496 | bytes 37748736 | tf_op jit(solution)/shard_map/pallas_call | solution.py:492
  (112 shorter events, 30.9 us)
Async XLA Ops:
  7.2 327.5 %all-gather.7.cloned.1.call-start = ((), (), s32[]{:S(2)}) async-start(), calls=%async_computation | async-start | bytes 4456448 | tf_op jit(solution)/shard_map/all_gather | solution.py:542
  9.9 15.7 %collective-permute-start.4 = (f32[256,256]{1,0:T(8,128)S(1)}, f32[256,256]{1,0:T(8,128)S(1)}, u32[]{:S(2)}, u32[]{:S(2)}) collective-permute-start(f32[256,256]{1,0:T(8,128)S(1)} %bitcast.43), channel_id=1, source_target_pairs={{0,4},{4,0},{8,12},{12,8},{1,5},{5,1},{9,13},{13,9},{2,6},{6,2},{1... | collective-permute-start | bytes 786440 | tf_op jit(solution)/shard_map/ppermute | solution.py:509
  13.1 15.3 %collective-permute-start.5 = (f32[256,256]{1,0:T(8,128)S(1)}, f32[256,256]{1,0:T(8,128)S(1)}, u32[]{:S(2)}, u32[]{:S(2)}) collective-permute-start(f32[256,256]{1,0:T(8,128)S(1)} %bitcast.44), channel_id=1, source_target_pairs={{0,8},{8,0},{4,12},{12,4},{1,9},{9,1},{5,13},{13,5},{2,10},{10,2},... | collective-permute-start | bytes 786440 | tf_op jit(solution)/shard_map/ppermute | solution.py:509
  14.7 80.2 %collective-permute-start.7 = (f32[256,256]{1,0:T(8,128)S(1)}, f32[256,256]{1,0:T(8,128)S(1)}, u32[]{:S(2)}, u32[]{:S(2)}) collective-permute-start(f32[256,256]{1,0:T(8,128)S(1)} %bitcast.45), channel_id=1, source_target_pairs={{0,2},{2,0},{1,3},{3,1},{4,6},{6,4},{5,7},{7,5},{8,10},{10,8},{9,1... | collective-permute-start | bytes 786440 | tf_op jit(solution)/shard_map/ppermute | solution.py:509
  24.5 90.2 %collective-permute-start.1 = (f32[2816,256]{1,0:T(8,128)}, f32[2816,256]{1,0:T(8,128)S(1)}, u32[]{:S(2)}, u32[]{:S(2)}) collective-permute-start(f32[2816,256]{1,0:T(8,128)} %bitcast.40.refs_0_), channel_id=1, source_target_pairs={{0,8},{8,0},{4,12},{12,4},{1,9},{9,1},{5,13},{13,5},{2,10},{10,2},... | collective-permute-start | bytes 8650760 | tf_op jit(solution)/shard_map/ppermute | solution.py:544
  25.6 68.0 %collective-permute-start.6 = (f32[256,256]{1,0:T(8,128)S(1)}, f32[256,256]{1,0:T(8,128)S(1)}, u32[]{:S(2)}, u32[]{:S(2)}) collective-permute-start(f32[256,256]{1,0:T(8,128)S(1)} %collective-permute-done.4), channel_id=1, source_target_pairs={{0,8},{8,0},{4,12},{12,4},{1,9},{9,1},{5,13},{13,5},{2,10},{10,2},... | collective-permute-start | bytes 786440 | tf_op jit(solution)/shard_map/ppermute | solution.py:510
  27.2 68.4 %collective-permute-start.8 = (f32[256,256]{1,0:T(8,128)S(1)}, f32[256,256]{1,0:T(8,128)S(1)}, u32[]{:S(2)}, u32[]{:S(2)}) collective-permute-start(f32[256,256]{1,0:T(8,128)S(1)} %collective-permute-done.4), channel_id=1, source_target_pairs={{0,2},{2,0},{1,3},{3,1},{4,6},{6,4},{5,7},{7,5},{8,10},{10,8},{9,1... | collective-permute-start | bytes 786440 | tf_op jit(solution)/shard_map/ppermute | solution.py:510
  28.5 67.9 %collective-permute-start.9 = (f32[256,256]{1,0:T(8,128)S(1)}, f32[256,256]{1,0:T(8,128)S(1)}, u32[]{:S(2)}, u32[]{:S(2)}) collective-permute-start(f32[256,256]{1,0:T(8,128)S(1)} %collective-permute-done.5), channel_id=1, source_target_pairs={{0,2},{2,0},{1,3},{3,1},{4,6},{6,4},{5,7},{7,5},{8,10},{10,8},{9,1... | collective-permute-start | bytes 786440 | tf_op jit(solution)/shard_map/ppermute | solution.py:510
  93.7 6.4 collective-permute-start.10
  100.8 15.4 %collective-permute-start.11 = (f32[8,256,256]{2,1,0:T(8,128)}, f32[8,256,256]{2,1,0:T(8,128)}, u32[]{:S(2)}, u32[]{:S(2)}) collective-permute-start(f32[8,256,256]{2,1,0:T(8,128)} %bitcast_dynamic-update-slice_fusion.refs_0_), channel_id=1, source_target_pairs={{0,1},{1,0},{2,3},{3,2},{4,5},{5,4},{6,7},{7,6},{8,9},{9,8},{10,11... | collective-permute-start | bytes 6291464 | tf_op jit(solution)/shard_map/ppermute | solution.py:513
  100.8 65.2 %collective-permute-start = (f32[2816,256]{1,0:T(8,128)}, f32[2816,256]{1,0:T(8,128)}, u32[]{:S(2)}, u32[]{:S(2)}) collective-permute-start(f32[2816,256]{1,0:T(8,128)} %bitcast.40.refs_0_), channel_id=1, source_target_pairs={{0,4},{4,0},{8,12},{12,8},{1,5},{5,1},{9,13},{13,9},{2,6},{6,2},{1... | collective-permute-start | bytes 8650760 | tf_op jit(solution)/shard_map/ppermute | solution.py:543
  103.1 64.4 %collective-permute-start.20 = (f32[256,1024]{1,0:T(8,128)S(1)}, f32[256,1024]{1,0:T(8,128)S(1)}, u32[]{:S(2)}, u32[]{:S(2)}) collective-permute-start(f32[256,1024]{1,0:T(8,128)S(1)} %get-tuple-element.112), channel_id=1, source_target_pairs={{0,1},{1,0},{2,3},{3,2},{4,5},{5,4},{6,7},{7,6},{8,9},{9,8},{10,11... | collective-permute-start | bytes 3145736 | tf_op jit(solution)/shard_map/ppermute | solution.py:517
  103.3 66.3 %collective-permute-start.22 = (f32[256,1024]{1,0:T(8,128)S(1)}, f32[256,1024]{1,0:T(8,128)S(1)}, u32[]{:S(2)}, u32[]{:S(2)}) collective-permute-start(f32[256,1024]{1,0:T(8,128)S(1)} %get-tuple-element.112), channel_id=1, source_target_pairs={{0,3},{3,0},{1,2},{2,1},{4,7},{7,4},{5,6},{6,5},{8,11},{11,8},{9,1... | collective-permute-start | bytes 3145736 | tf_op jit(solution)/shard_map/ppermute | solution.py:517
  114.6 36.9 %collective-permute-start.15 = (f32[256,768]{1,0:T(8,128)S(1)}, f32[256,768]{1,0:T(8,128)S(1)}, u32[]{:S(2)}, u32[]{:S(2)}) collective-permute-start(f32[256,768]{1,0:T(8,128)S(1)} %pad_maximum_fusion.refs_0_), channel_id=1, source_target_pairs={{0,2},{2,0},{1,3},{3,1},{4,6},{6,4},{5,7},{7,5},{8,10},{10,8},{9,1... | collective-permute-start | bytes 2359304 | tf_op jit(solution)/shard_map/ppermute | solution.py:521
  116.2 51.9 %collective-permute-start.21 = (f32[256,1024]{1,0:T(8,128)S(1)}, f32[256,1024]{1,0:T(8,128)S(1)}, u32[]{:S(2)}, u32[]{:S(2)}) collective-permute-start(f32[256,1024]{1,0:T(8,128)S(1)} %get-tuple-element.113.refs_0_), channel_id=1, source_target_pairs={{0,2},{2,0},{1,3},{3,1},{4,6},{6,4},{5,7},{7,5},{8,10},{10,8},{9,1... | collective-permute-start | bytes 3145736 | tf_op jit(solution)/shard_map/ppermute | solution.py:517
  151.5 29.4 %collective-permute-start.14 = (f32[256,768]{1,0:T(8,128)S(1)}, f32[256,768]{1,0:T(8,128)S(1)}, u32[]{:S(2)}, u32[]{:S(2)}) collective-permute-start(f32[256,768]{1,0:T(8,128)S(1)} %pad_maximum_fusion.refs_0_), channel_id=1, source_target_pairs={{0,1},{1,0},{2,3},{3,2},{4,5},{5,4},{6,7},{7,6},{8,9},{9,8},{10,11... | collective-permute-start | bytes 2359304 | tf_op jit(solution)/shard_map/ppermute | solution.py:522
  166.0 16.5 %collective-permute-start.16 = (f32[256,768]{1,0:T(8,128)S(1)}, f32[256,768]{1,0:T(8,128)S(1)}, u32[]{:S(2)}, u32[]{:S(2)}) collective-permute-start(f32[256,768]{1,0:T(8,128)S(1)} %collective-permute-done.15.refs_2_), channel_id=1, source_target_pairs={{0,1},{1,0},{2,3},{3,2},{4,5},{5,4},{6,7},{7,6},{8,9},{9,8},{10,11... | collective-permute-start | bytes 2359304 | tf_op jit(solution)/shard_map/ppermute | solution.py:523
  167.4 49.9 %collective-permute-start.2 = (f32[704,256]{1,0:T(8,128)S(1)}, f32[704,256]{1,0:T(8,128)S(1)}, u32[]{:S(2)}, u32[]{:S(2)}) collective-permute-start(f32[704,256]{1,0:T(8,128)S(1)} %get-tuple-element.117), channel_id=1, source_target_pairs={{0,4},{4,0},{8,12},{12,8},{1,5},{5,1},{9,13},{13,9},{2,6},{6,2},{1... | collective-permute-start | bytes 2162696 | tf_op jit(solution)/shard_map/ppermute | solution.py:557
  168.1 33.3 %collective-permute-start.12 = (f32[704,256]{1,0:T(8,128)S(1)}, f32[704,256]{1,0:T(8,128)S(1)}, u32[]{:S(2)}, u32[]{:S(2)}) collective-permute-start(f32[704,256]{1,0:T(8,128)S(1)} %get-tuple-element.116), channel_id=1, source_target_pairs={{0,4},{4,0},{8,12},{12,8},{1,5},{5,1},{9,13},{13,9},{2,6},{6,2},{1... | collective-permute-start | bytes 2162696 | tf_op jit(solution)/shard_map/ppermute | solution.py:556
  169.6 31.8 %collective-permute-start.13 = (f32[704,256]{1,0:T(8,128)S(1)}, f32[704,256]{1,0:T(8,128)S(1)}, u32[]{:S(2)}, u32[]{:S(2)}) collective-permute-start(f32[704,256]{1,0:T(8,128)S(1)} %get-tuple-element.114), channel_id=1, source_target_pairs={{0,8},{8,0},{4,12},{12,4},{1,9},{9,1},{5,13},{13,5},{2,10},{10,2},... | collective-permute-start | bytes 2162696 | tf_op jit(solution)/shard_map/ppermute | solution.py:556
  180.9 36.4 %collective-permute-start.3 = (f32[704,256]{1,0:T(8,128)S(1)}, f32[704,256]{1,0:T(8,128)S(1)}, u32[]{:S(2)}, u32[]{:S(2)}) collective-permute-start(f32[704,256]{1,0:T(8,128)S(1)} %get-tuple-element.115), channel_id=1, source_target_pairs={{0,8},{8,0},{4,12},{12,4},{1,9},{9,1},{5,13},{13,5},{2,10},{10,2},... | collective-permute-start | bytes 2162696 | tf_op jit(solution)/shard_map/ppermute | solution.py:557
  182.5 87.4 %collective-permute-start.23 = (f32[1024,1024]{1,0:T(8,128)}, f32[1024,1024]{1,0:T(8,128)}, u32[]{:S(2)}, u32[]{:S(2)}) collective-permute-start(f32[1024,1024]{1,0:T(8,128)} %shard_map.47.mine_ref.refs_3_), channel_id=1, source_target_pairs={{0,1},{1,0},{2,3},{3,2},{4,5},{5,4},{6,7},{7,6},{8,9},{9,8},{10,11... | collective-permute-start | bytes 12582920 | tf_op jit(solution)/shard_map/ppermute | solution.py:565
  266.3 245.0 %all-gather.9.cloned.1.call-start = ((), (), s32[]{:S(2)}) async-start(), calls=%async_computation.1 | async-start | bytes 4456448 | tf_op jit(solution)/shard_map/all_gather | solution.py:542
  266.3 136.5 %collective-permute-start.17 = (f32[2560,256]{1,0:T(8,128)}, f32[2560,256]{1,0:T(8,128)}, u32[]{:S(2)}, u32[]{:S(2)}) collective-permute-start(f32[2560,256]{1,0:T(8,128)} %get-tuple-element.64.refs_0_), channel_id=1, source_target_pairs={{0,4},{4,0},{8,12},{12,8},{1,5},{5,1},{9,13},{13,9},{2,6},{6,2},{1... | collective-permute-start | bytes 7864328 | tf_op jit(solution)/shard_map/ppermute | solution.py:543
  266.9 135.9 %collective-permute-start.18 = (f32[2560,256]{1,0:T(8,128)}, f32[2560,256]{1,0:T(8,128)}, u32[]{:S(2)}, u32[]{:S(2)}) collective-permute-start(f32[2560,256]{1,0:T(8,128)} %get-tuple-element.64.refs_0_), channel_id=1, source_target_pairs={{0,8},{8,0},{4,12},{12,4},{1,9},{9,1},{5,13},{13,5},{2,10},{10,2},... | collective-permute-start | bytes 7864328 | tf_op jit(solution)/shard_map/ppermute | solution.py:544
  267.3 135.5 %collective-permute-start.19 = (f32[2560,256]{1,0:T(8,128)}, f32[2560,256]{1,0:T(8,128)}, u32[]{:S(2)}, u32[]{:S(2)}) collective-permute-start(f32[2560,256]{1,0:T(8,128)} %get-tuple-element.64.refs_0_), channel_id=1, source_target_pairs={{0,12},{12,0},{4,8},{8,4},{1,13},{13,1},{5,9},{9,5},{2,14},{14,2},... | collective-permute-start | bytes 7864328 | tf_op jit(solution)/shard_map/ppermute | solution.py:553
  283.6 51.0 %collective-permute-start.24 = (f32[256,1536]{1,0:T(8,128)}, f32[256,1536]{1,0:T(8,128)S(1)}, u32[]{:S(2)}, u32[]{:S(2)}) collective-permute-start(f32[256,1536]{1,0:T(8,128)} %get-tuple-element.73), channel_id=1, source_target_pairs={{0,1},{1,0},{2,3},{3,2},{4,5},{5,4},{6,7},{7,6},{8,9},{9,8},{10,11... | collective-permute-start | bytes 4718600 | tf_op jit(solution)/shard_map/ppermute | solution.py:517
  283.6 102.1 %collective-permute-start.26 = (f32[256,1536]{1,0:T(8,128)}, f32[256,1536]{1,0:T(8,128)}, u32[]{:S(2)}, u32[]{:S(2)}) collective-permute-start(f32[256,1536]{1,0:T(8,128)} %get-tuple-element.73), channel_id=1, source_target_pairs={{0,3},{3,0},{1,2},{2,1},{4,7},{7,4},{5,6},{6,5},{8,11},{11,8},{9,1... | collective-permute-start | bytes 4718600 | tf_op jit(solution)/shard_map/ppermute | solution.py:517
  284.4 50.2 %copy-start.3 = (f32[256,1536]{1,0:T(8,128)S(1)}, f32[256,1536]{1,0:T(8,128)}, u32[]{:S(2)}) copy-start(f32[256,1536]{1,0:T(8,128)} %get-tuple-element.72.refs_0_) | copy-start | bytes 4718596
  334.7 51.1 %collective-permute-start.25 = (f32[256,1536]{1,0:T(8,128)S(1)}, f32[256,1536]{1,0:T(8,128)S(1)}, u32[]{:S(2)}, u32[]{:S(2)}) collective-permute-start(f32[256,1536]{1,0:T(8,128)S(1)} %copy-done.3), channel_id=1, source_target_pairs={{0,2},{2,0},{1,3},{3,1},{4,6},{6,4},{5,7},{7,5},{8,10},{10,8},{9,1... | collective-permute-start | bytes 4718600 | tf_op jit(solution)/shard_map/ppermute | solution.py:517
  402.8 50.9 %collective-permute-start.30 = (f32[1024,1024]{1,0:T(8,128)}, f32[1024,1024]{1,0:T(8,128)}, u32[]{:S(2)}, u32[]{:S(2)}) collective-permute-start(f32[1024,1024]{1,0:T(8,128)} %get-tuple-element.79.mine_ref.refs_3_), channel_id=1, source_target_pairs={{0,1},{1,0},{2,3},{3,2},{4,5},{5,4},{6,7},{7,6},{8,9},{9,8},{10,11... | collective-permute-start | bytes 12582920 | tf_op jit(solution)/shard_map/ppermute | solution.py:565
  450.1 229.4 %all-gather.11.cloned.1.call-start = ((), (), s32[]{:S(2)}) async-start(), calls=%async_computation.2 | async-start | bytes 4456448 | tf_op jit(solution)/shard_map/all_gather | solution.py:542
  450.1 111.0 %collective-permute-start.27 = (f32[2304,256]{1,0:T(8,128)}, f32[2304,256]{1,0:T(8,128)}, u32[]{:S(2)}, u32[]{:S(2)}) collective-permute-start(f32[2304,256]{1,0:T(8,128)} %get-tuple-element.76.refs_0_), channel_id=1, source_target_pairs={{0,4},{4,0},{8,12},{12,8},{1,5},{5,1},{9,13},{13,9},{2,6},{6,2},{1... | collective-permute-start | bytes 7077896 | tf_op jit(solution)/shard_map/ppermute | solution.py:543
  450.8 117.4 %collective-permute-start.28 = (f32[2304,256]{1,0:T(8,128)}, f32[2304,256]{1,0:T(8,128)}, u32[]{:S(2)}, u32[]{:S(2)}) collective-permute-start(f32[2304,256]{1,0:T(8,128)} %get-tuple-element.76.refs_0_), channel_id=1, source_target_pairs={{0,8},{8,0},{4,12},{12,4},{1,9},{9,1},{5,13},{13,5},{2,10},{10,2},... | collective-permute-start | bytes 7077896 | tf_op jit(solution)/shard_map/ppermute | solution.py:544
  451.4 116.8 %collective-permute-start.29 = (f32[2304,256]{1,0:T(8,128)}, f32[2304,256]{1,0:T(8,128)}, u32[]{:S(2)}, u32[]{:S(2)}) collective-permute-start(f32[2304,256]{1,0:T(8,128)} %get-tuple-element.76.refs_0_), channel_id=1, source_target_pairs={{0,12},{12,0},{4,8},{8,4},{1,13},{13,1},{5,9},{9,5},{2,14},{14,2},... | collective-permute-start | bytes 7077896 | tf_op jit(solution)/shard_map/ppermute | solution.py:553
  467.3 124.3 %collective-permute-start.31 = (f32[256,1280]{1,0:T(8,128)}, f32[256,1280]{1,0:T(8,128)}, u32[]{:S(2)}, u32[]{:S(2)}) collective-permute-start(f32[256,1280]{1,0:T(8,128)} %get-tuple-element.87), channel_id=1, source_target_pairs={{0,1},{1,0},{2,3},{3,2},{4,5},{5,4},{6,7},{7,6},{8,9},{9,8},{10,11... | collective-permute-start | bytes 3932168 | tf_op jit(solution)/shard_map/ppermute | solution.py:517
  467.3 124.6 %collective-permute-start.33 = (f32[256,1280]{1,0:T(8,128)}, f32[256,1280]{1,0:T(8,128)}, u32[]{:S(2)}, u32[]{:S(2)}) collective-permute-start(f32[256,1280]{1,0:T(8,128)} %get-tuple-element.87), channel_id=1, source_target_pairs={{0,3},{3,0},{1,2},{2,1},{4,7},{7,4},{5,6},{6,5},{8,11},{11,8},{9,1... | collective-permute-start | bytes 3932168 | tf_op jit(solution)/shard_map/ppermute | solution.py:517
  511.3 49.8 %copy-start.4 = (f32[256,1280]{1,0:T(8,128)S(1)}, f32[256,1280]{1,0:T(8,128)}, u32[]{:S(2)}) copy-start(f32[256,1280]{1,0:T(8,128)} %get-tuple-element.86.refs_0_) | copy-start | bytes 3932164
  561.1 30.7 %collective-permute-start.32 = (f32[256,1280]{1,0:T(8,128)S(1)}, f32[256,1280]{1,0:T(8,128)S(1)}, u32[]{:S(2)}, u32[]{:S(2)}) collective-permute-start(f32[256,1280]{1,0:T(8,128)S(1)} %copy-done.4), channel_id=1, source_target_pairs={{0,2},{2,0},{1,3},{3,1},{4,6},{6,4},{5,7},{7,5},{8,10},{10,8},{9,1... | collective-permute-start | bytes 3932168 | tf_op jit(solution)/shard_map/ppermute | solution.py:517
  619.4 7.4 collective-permute-start.34
  641.2 87.9 %collective-permute-start.38 = (f32[256,1024]{1,0:T(8,128)}, f32[256,1024]{1,0:T(8,128)S(1)}, u32[]{:S(2)}, u32[]{:S(2)}) collective-permute-start(f32[256,1024]{1,0:T(8,128)} %get-tuple-element.100), channel_id=1, source_target_pairs={{0,1},{1,0},{2,3},{3,2},{4,5},{5,4},{6,7},{7,6},{8,9},{9,8},{10,11... | collective-permute-start | bytes 3145736 | tf_op jit(solution)/shard_map/ppermute | solution.py:517
  641.4 87.8 %collective-permute-start.40 = (f32[256,1024]{1,0:T(8,128)}, f32[256,1024]{1,0:T(8,128)S(1)}, u32[]{:S(2)}, u32[]{:S(2)}) collective-permute-start(f32[256,1024]{1,0:T(8,128)} %get-tuple-element.100), channel_id=1, source_target_pairs={{0,3},{3,0},{1,2},{2,1},{4,7},{7,4},{5,6},{6,5},{8,11},{11,8},{9,1... | collective-permute-start | bytes 3145736 | tf_op jit(solution)/shard_map/ppermute | solution.py:517
  642.6 86.6 %collective-permute-start.39 = (f32[256,1024]{1,0:T(8,128)}, f32[256,1024]{1,0:T(8,128)S(1)}, u32[]{:S(2)}, u32[]{:S(2)}) collective-permute-start(f32[256,1024]{1,0:T(8,128)} %get-tuple-element.99.refs_0_), channel_id=1, source_target_pairs={{0,2},{2,0},{1,3},{3,1},{4,6},{6,4},{5,7},{7,5},{8,10},{10,8},{9,1... | collective-permute-start | bytes 3145736 | tf_op jit(solution)/shard_map/ppermute | solution.py:517
  679.5 49.7 %copy-start.5 = (f32[256,1024]{1,0:T(8,128)S(1)}, f32[256,1024]{1,0:T(8,128)}, u32[]{:S(2)}) copy-start(f32[256,1024]{1,0:T(8,128)} %get-tuple-element.99.refs_0_) | copy-start | bytes 3145732
  740.0 114.4 %collective-permute-start.41 = (f32[1024,1024]{1,0:T(8,128)}, f32[1024,1024]{1,0:T(8,128)S(1)}, u32[]{:S(2)}, u32[]{:S(2)}) collective-permute-start(f32[1024,1024]{1,0:T(8,128)} %shard_map.64.mine_ref), channel_id=1, source_target_pairs={{0,1},{1,0},{2,3},{3,2},{4,5},{5,4},{6,7},{7,6},{8,9},{9,8},{10,11... | collective-permute-start | bytes 12582920 | tf_op jit(solution)/shard_map/ppermute | solution.py:565
  740.0 48.5 %collective-permute-start.35 = (f32[2048,256]{1,0:T(8,128)S(1)}, f32[2048,256]{1,0:T(8,128)S(1)}, u32[]{:S(2)}, u32[]{:S(2)}) collective-permute-start(f32[2048,256]{1,0:T(8,128)S(1)} %copy-done.10), channel_id=1, source_target_pairs={{0,4},{4,0},{8,12},{12,8},{1,5},{5,1},{9,13},{13,9},{2,6},{6,2},{1... | collective-permute-start | bytes 6291464 | tf_op jit(solution)/shard_map/ppermute | solution.py:543
  741.2 92.6 %collective-permute-start.36 = (f32[2048,256]{1,0:T(8,128)S(1)}, f32[2048,256]{1,0:T(8,128)S(1)}, u32[]{:S(2)}, u32[]{:S(2)}) collective-permute-start(f32[2048,256]{1,0:T(8,128)S(1)} %copy-done.10), channel_id=1, source_target_pairs={{0,8},{8,0},{4,12},{12,4},{1,9},{9,1},{5,13},{13,5},{2,10},{10,2},... | collective-permute-start | bytes 6291464 | tf_op jit(solution)/shard_map/ppermute | solution.py:544
  742.4 91.5 %collective-permute-start.37 = (f32[2048,256]{1,0:T(8,128)S(1)}, f32[2048,256]{1,0:T(8,128)S(1)}, u32[]{:S(2)}, u32[]{:S(2)}) collective-permute-start(f32[2048,256]{1,0:T(8,128)S(1)} %copy-done.10), channel_id=1, source_target_pairs={{0,12},{12,0},{4,8},{8,4},{1,13},{13,1},{5,9},{9,5},{2,14},{14,2},... | collective-permute-start | bytes 6291464 | tf_op jit(solution)/shard_map/ppermute | solution.py:553
  (9 other events, 44.9 us)
Sparse Core Ops, SparseCore 0:
  266.4 46.9 all-gather.6
  450.2 47.3 all-gather.8
  619.5 41.8 all-gather.10
